TPU v7x, 256 devices: a whole 4x4x8 slice. The times are simulated.
256 devices in a mesh: freq: 32 (over z, x), rcv: 8 (over y, core).
Axes of the slice: x: 4, y: 4, z: 8, core: 2. Of those that a mesh axis runs over, the one named last changes fastest.
Arguments:
- primaries_start: float32 [512, 1024, 128], P(('rcv', 'freq')), may hold values from -6 to 6
- surface_operator: bfloat16 [512, 2, 384, 512], P('freq', None, 'rcv'), may hold values from -0.25 to 0.25
- data_spectra: bfloat16 [384, 512, 2, 128], P('rcv', 'freq'), may hold values from -6 to 6
- shrinkage: float32 [128], replicated, may hold values from 0.2 to 2
Outputs:
- primaries: float32 [512, 1024, 128], P(('rcv', 'freq'))
- residual_spectra: bfloat16 [384, 512, 2, 128], P('rcv', 'freq')
All inputs are finite; a program needn't handle non-finite values.
Results may differ from a plain program's by a relative error of at most 0.0085.
Values may be sent and summed in bfloat16 or wider, within the bound.
No kernel may reach another device: no remote copies, remote signals or barrier semaphores. Data moves between devices by JAX's collectives and lax.ppermute only.
A program may use at most 64 MiB of HBM per device.

v0:
```python
import math

import jax
import jax.numpy as jnp
from jax import lax
from jax.sharding import PartitionSpec as P

S = 128
NS = 512
T_SIZE = 1024
ITERS = 2
NF = 512


def transform_table(frequencies, samples):
    freq_index = jnp.arange(frequencies, dtype=jnp.int32)[:, None]
    sample_index = jnp.arange(samples, dtype=jnp.int32)[None, :]
    phase = freq_index * sample_index % samples
    angle = phase.astype(jnp.float32) * (2.0 * math.pi / samples)
    factor = math.sqrt(2.0 / samples)
    return jnp.stack([factor * jnp.cos(angle), -factor * jnp.sin(angle)], axis=1).astype(
        jnp.bfloat16
    )


def forward_product(block, piece):
    real_op = block[:, 0]
    imag_op = block[:, 1]
    real_in = piece[:, :, 0]
    imag_in = piece[:, :, 1]

    def product(left, right):
        return jnp.einsum("krn,nks->rks", left, right, preferred_element_type=jnp.float32)

    real_out = product(real_op, real_in) - product(imag_op, imag_in)
    imag_out = product(real_op, imag_in) + product(imag_op, real_in)
    return jnp.stack([real_out, imag_out], axis=2)


def adjoint_product(block, resid):
    real_op = block[:, 0]
    imag_op = block[:, 1]
    real_res = resid[:, :, 0]
    imag_res = resid[:, :, 1]

    def product(left, right):
        return jnp.einsum("krn,rks->nks", left, right, preferred_element_type=jnp.float32)

    real_dir = product(real_op, real_res) + product(imag_op, imag_res)
    imag_dir = product(real_op, imag_res) - product(imag_op, real_res)
    return jnp.stack([real_dir, imag_dir], axis=2)


def local(primaries_start, surface_operator, data_spectra, shrinkage):
    table = transform_table(NF, T_SIZE)
    primaries = primaries_start
    count_total = 2.0 * NF * NS * S
    residual = data_spectra
    for iteration in range(ITERS):
        local_spectra = jnp.einsum(
            "kct,nts->nkcs",
            table,
            primaries.astype(jnp.bfloat16),
            preferred_element_type=jnp.float32,
        ).astype(jnp.bfloat16)
        spectra = lax.all_to_all(local_spectra, "freq", split_axis=1, concat_axis=0, tiled=True)
        predicted = forward_product(
            surface_operator, lax.all_gather(spectra, "rcv", axis=0, tiled=True)
        )
        residual = (data_spectra.astype(jnp.float32) - predicted).astype(jnp.bfloat16)
        residual_sq = jnp.sum(jnp.square(residual.astype(jnp.float32)))
        direction = lax.psum_scatter(
            adjoint_product(surface_operator, residual), "rcv", scatter_dimension=0, tiled=True
        )
        direction_sq = jnp.sum(jnp.square(direction))
        residual_norm, direction_norm = lax.psum((residual_sq, direction_sq), ("freq", "rcv"))
        step_size = 0.5 * residual_norm / (direction_norm + 1e-06)
        threshold = shrinkage[None, None, :] * (step_size * jnp.sqrt(direction_norm / count_total))
        direction_low = direction.astype(jnp.bfloat16)
        update = jnp.einsum(
            "kct,nkcs->nts",
            table,
            lax.all_to_all(direction_low, "freq", split_axis=0, concat_axis=1, tiled=True),
            preferred_element_type=jnp.float32,
        )
        moved = primaries + step_size * update
        primaries = moved - jnp.clip(moved, -threshold, threshold)
    return (primaries, residual)


def solution(mesh):
    return jax.shard_map(
        local,
        mesh=mesh,
        in_specs=(
            P(("rcv", "freq"), None, None),
            P("freq", None, "rcv", None),
            P("rcv", "freq", None, None),
            P(),
        ),
        out_specs=(P(("rcv", "freq"), None, None), P("rcv", "freq", None, None)),
        check_vma=False,
    )
```

profile of v0, /device:TPU:1, one launch (start us, length us, event | category | flops | bytes accessed | tf_op | source)
XLA Modules:
  0.0 497.7 jit_solution(7442395549814731971)
XLA Ops:
  7.2 8.6 %multiply_convert_fusion = (bf16[512,1,1024]{2,0,1:T(8,128)(2,1)S(1)}, bf16[512,1,1024]{2,0,1:T(8,128)(2,1)S(1)}) fusion(), kind=kLoop, calls=%fused_computation.25 | loop fusion | flops 9437184 | bytes 2097152 | tf_op jit(solution)/shard_map/convert.1
  15.8 1.0 copy-done.5
  16.8 0.7 fusion.52
  17.5 0.5 copy.32
  18.1 27.9 %all_to_all.72 = bf16[2,512,2,128]{3,0,2,1:T(2,128)(2,1)S(1)} all-to-all(bf16[2,512,2,128]{3,0,2,1:T(2,128)(2,1)S(1)} %copy.32), channel_id=1, replica_groups=mesh['freq'=32,'rcv'=8] {'freq'}, dimensions={1} | all-to-all | bytes 1048576 | tf_op jit(solution)/shard_map/all_to_all | solution.py:66
  46.0 1.4 copy.33
  47.5 33.2 %all-gather.3.cloned.1.call-done = bf16[512,16,2,128]{3,0,1,2:T(8,128)(2,1)} async-done(((bf16[64,16,2,128]{3,0,1,2:T(8,128)(2,1)}), bf16[512,16,2,128]{3,0,1,2:T(8,128)(2,1)}) %all-gather.3.cloned.1.call-update) | async-done | bytes 4194320 | tf_op jit(solution)/shard_map/all_gather | solution.py:68
  80.6 2.2 fusion.14
  82.8 2.0 fusion.15
  84.9 0.5 fusion.65
  85.4 0.5 fusion.63
  85.9 0.5 copy-done.3
  86.4 0.8 multiply_reduce_fusion.3
  87.2 0.7 fusion.88
  88.0 0.8 fusion.86
  88.8 0.8 add_bitcast_fusion.1
  89.5 0.8 subtract_bitcast_fusion.1
  90.3 4.2 pad_maximum_fusion
  94.5 10.3 %copy.36 = f32[512,16,2,128]{3,1,2,0:T(8,128)} copy(f32[512,16,2,128]{0,3,1,2:T(8,128)} %pad_maximum_fusion) | data formatting | bytes 16777216 | tf_op jit(solution)/shard_map/stack | solution.py:51
  104.9 54.2 %reduce-scatter.3.cloned.1.call-done = f32[64,16,2,128]{3,1,2,0:T(8,128)} async-done(((f32[512,16,2,128]{3,1,2,0:T(8,128)}), f32[64,16,2,128]{3,1,2,0:T(8,128)}) %reduce-scatter.3.cloned.1.call-update) | async-done | bytes 1048592 | tf_op jit(solution)/shard_map/reduce_scatter | solution.py:72
  159.1 3.4 multiply_reduce_fusion.1
  162.4 9.5 %all-to-all-start.1 = ((bf16[64,16,2,128]{3,1,2,0:T(8,128)(2,1)}), bf16[64,16,2,128]{3,1,2,0:T(8,128)(2,1)S(1)}, u32[]{:S(2)}, u32[]{:S(2)}) async-start(bf16[64,16,2,128]{3,1,2,0:T(8,128)(2,1)} %get-tuple-element.23), calls=%async_computation.2 | async-start | bytes 1048576 | tf_op jit(solution)/shard_map/all_to_all | solution.py:83
  172.0 1.3 copy.39
  173.3 77.2 %all-reduce.1 = (f32[]{:T(128)}, f32[]{:T(128)}) all-reduce(f32[]{:T(128)} %get-tuple-element.18, f32[]{:T(128)} %get-tuple-element.22), channel_id=1, replica_groups=mesh['freq'=32,'rcv'=8] {'freq','rcv'}, use_global_device_ids=true, to_apply=%region_1.2 | all-reduce | flops 2 | bytes 16 | tf_op jit(solution)/shard_map/psum | solution.py:76
  252.7 2.8 minimum_subtract_fusion.1
  255.5 1.0 copy-done.11
  256.5 1.6 fusion.55
  258.0 1.3 copy.40
  259.4 22.7 %all_to_all.73 = bf16[2,512,2,128]{3,2,0,1:T(2,128)(2,1)S(1)} all-to-all(bf16[2,512,2,128]{3,2,0,1:T(2,128)(2,1)S(1)} %copy.40), channel_id=1, replica_groups=mesh['freq'=32,'rcv'=8] {'freq'}, dimensions={1} | all-to-all | bytes 1048576 | tf_op jit(solution)/shard_map/all_to_all | solution.py:66
  282.1 1.3 copy.42
  283.5 30.9 %all-gather.5.cloned.1.call-done = bf16[512,16,2,128]{3,0,1,2:T(8,128)(2,1)} async-done(((bf16[64,16,2,128]{3,0,1,2:T(8,128)(2,1)}), bf16[512,16,2,128]{3,0,1,2:T(8,128)(2,1)}) %all-gather.5.cloned.1.call-update) | async-done | bytes 4194320 | tf_op jit(solution)/shard_map/all_gather | solution.py:68
  314.5 2.2 fusion.18
  316.7 2.0 fusion.19
  319.2 0.5 fusion.59
  319.7 0.9 multiply_reduce_fusion.2
  320.7 0.8 fusion.82
  321.4 0.8 fusion.80
  322.2 0.8 add_bitcast_fusion
  322.9 0.8 subtract_bitcast_fusion
  323.7 4.2 pad_maximum_fusion.1
  327.9 10.3 %copy.43 = f32[512,16,2,128]{3,1,2,0:T(8,128)} copy(f32[512,16,2,128]{0,3,1,2:T(8,128)} %pad_maximum_fusion.1) | data formatting | bytes 16777216 | tf_op jit(solution)/shard_map/stack | solution.py:51
  338.3 54.2 %reduce-scatter.5.cloned.1.call-done = f32[64,16,2,128]{3,1,2,0:T(8,128)} async-done(((f32[512,16,2,128]{3,1,2,0:T(8,128)}), f32[64,16,2,128]{3,1,2,0:T(8,128)}) %reduce-scatter.5.cloned.1.call-update) | async-done | bytes 1048592 | tf_op jit(solution)/shard_map/reduce_scatter | solution.py:72
  392.5 3.4 multiply_reduce_fusion
  395.8 9.5 %all-to-all-start.3 = ((bf16[64,16,2,128]{3,1,2,0:T(8,128)(2,1)}), bf16[64,16,2,128]{3,1,2,0:T(8,128)(2,1)S(1)}, u32[]{:S(2)}, u32[]{:S(2)}) async-start(bf16[64,16,2,128]{3,1,2,0:T(8,128)(2,1)} %get-tuple-element.21), calls=%async_computation.5 | async-start | bytes 1048576 | tf_op jit(solution)/shard_map/all_to_all | solution.py:83
  405.4 1.2 copy.47
  406.5 77.0 %all-reduce = (f32[]{:T(128)}, f32[]{:T(128)}) all-reduce(f32[]{:T(128)} %get-tuple-element.14, f32[]{:T(128)} %get-tuple-element.20), channel_id=1, replica_groups=mesh['freq'=32,'rcv'=8] {'freq','rcv'}, use_global_device_ids=true, to_apply=%region_6.7 | all-reduce | flops 2 | bytes 16 | tf_op jit(solution)/shard_map/psum | solution.py:76
  485.7 3.0 minimum_subtract_fusion
  488.6 2.5 copy.46
  (37 shorter events, 0.9 us)
Async XLA Ops:
  7.2 9.6 %copy-start.4 = (f32[2,1024,128]{2,1,0:T(8,128)S(1)}, f32[2,1024,128]{2,1,0:T(8,128)}, u32[]{:S(2)}) copy-start(f32[2,1024,128]{2,1,0:T(8,128)} %param.4) | copy-start | bytes 3145732
  7.2 73.5 %all-gather.3.cloned.1.call-start = ((), (), s32[]{:S(2)}) async-start(), calls=%async_computation.6 | async-start | bytes 4718592 | tf_op jit(solution)/shard_map/all_gather | solution.py:68
  15.8 1.0 copy-start.5
  15.8 1.7 copy-start.7
  17.5 63.1 %copy-start = (bf16[16,2,48,512]{3,2,1,0:T(8,128)(2,1)S(1)}, bf16[16,2,48,512]{3,2,1,0:T(8,128)(2,1)}, u32[]{:S(2)}) copy-start(bf16[16,2,48,512]{3,2,1,0:T(8,128)(2,1)} %param.5) | copy-start | bytes 4718596
  47.4 111.6 %reduce-scatter.3.cloned.1.call-start = ((), (), s32[]{:S(2)}) async-start(), calls=%async_computation.7 | async-start | bytes 9437184 | tf_op jit(solution)/shard_map/reduce_scatter | solution.py:72
  80.6 4.3 copy-start.1
  85.4 1.0 copy-start.3
  104.8 147.8 %copy-start.10 = (f32[128]{0:T(128)S(1)}, f32[128]{0:T(128)}, u32[]{:S(2)}) copy-start(f32[128]{0:T(128)} %param.7) | copy-start | bytes 1540
  162.4 90.2 %all-to-all-start.1 = ((bf16[64,16,2,128]{3,1,2,0:T(8,128)(2,1)}), bf16[64,16,2,128]{3,1,2,0:T(8,128)(2,1)S(1)}, u32[]{:S(2)}, u32[]{:S(2)}) async-start(bf16[64,16,2,128]{3,1,2,0:T(8,128)(2,1)} %get-tuple-element.23), calls=%async_computation.2 | async-start | bytes 1048576 | tf_op jit(solution)/shard_map/all_to_all | solution.py:83
  172.0 142.5 %all-gather.5.cloned.1.call-start = ((), (), s32[]{:S(2)}) async-start(), calls=%async_computation.8 | async-start | bytes 4718592 | tf_op jit(solution)/shard_map/all_gather | solution.py:68
  252.7 3.8 copy-start.6
  252.7 3.8 copy-start.8
  255.5 1.0 copy-start.11
  283.5 109.0 %reduce-scatter.5.cloned.1.call-start = ((), (), s32[]{:S(2)}) async-start(), calls=%async_computation.9 | async-start | bytes 9437184 | tf_op jit(solution)/shard_map/reduce_scatter | solution.py:72
  314.5 4.3 copy-start.2
  338.2 147.4 %copy-start.9 = (bf16[512,1,1024]{2,0,1:T(8,128)(2,1)S(1)}, bf16[512,1,1024]{2,0,1:T(8,128)(2,1)}, u32[]{:S(2)}) copy-start(bf16[512,1,1024]{2,0,1:T(8,128)(2,1)} %copy-done.7) | copy-start | bytes 3145732
  395.8 89.8 %all-to-all-start.3 = ((bf16[64,16,2,128]{3,1,2,0:T(8,128)(2,1)}), bf16[64,16,2,128]{3,1,2,0:T(8,128)(2,1)S(1)}, u32[]{:S(2)}, u32[]{:S(2)}) async-start(bf16[64,16,2,128]{3,1,2,0:T(8,128)(2,1)} %get-tuple-element.21), calls=%async_computation.5 | async-start | bytes 1048576 | tf_op jit(solution)/shard_map/all_to_all | solution.py:83
Sparse Core Ops, SparseCore 0:
  47.5 33.0 all-gather.2
  105.0 54.0 reduce-scatter.2
  283.6 30.8 all-gather.4
  338.4 54.0 reduce-scatter.4
where the time goes:
time: 499 us; the launch traced here: 498 us
  blocking collectives  205 us (41%)
  waiting for transfers between devices  173 us (35%)
  local copies, waits for them, and re-layouts  32.7 us (7%)
  other arithmetic  25.5 us (5%)
  matrix products  24.5 us (5%)
  starting transfers between devices  19.2 us (4%)
  between operations  18.3 us (4%)
    psum x2, blocking collectives, local(): lax.psum((residual_sq, direction_sq), ('freq', 'rcv'))  154 us
    reduce_scatter x2, waiting for transfers between devices, local(): lax.psum_scatter(adjoint_product(surface_operator, residual), 'rcv', scat...  108 us
    all_gather x2, waiting for transfers between devices, local(): lax.all_gather(spectra, 'rcv', axis=0, tiled=True)  64.1 us
    all_to_all x2, blocking collectives, local(): lax.all_to_all(local_spectra, 'freq', split_axis=1, concat_axis=0, tiled=...  50.6 us
    another operation x2, local copies, waits for them, and re-layouts, adjoint_product(): return jnp.stack([real_dir, imag_dir], axis=2)  20.6 us
    all_to_all x2, starting transfers between devices, local(): lax.all_to_all(direction_low, 'freq', split_axis=0, concat_axis=1, tiled=...  19.1 us
    dot_general x8, matrix products, product(): jnp.einsum('krn,nks->rks', left, right, preferred_element_type=jnp.float32)  10.5 us
  transfers between devices with their start and end apart: 6, of which 4 were waited for; matrix products, arithmetic and copies ran while one was open for 0% of the time, Pallas kernels for 0%

commit v1 on v0

v1 whole, which is shorter than its diff:
```python
import math

import jax
import jax.numpy as jnp
import numpy as np
from jax import lax
from jax.sharding import PartitionSpec as P

S = 128
NS = 512
R = 384
T_SIZE = 1024
ITERS = 2
NF = 512
ALL = ("rcv", "freq")


def transform_table(freq_parts, rcv_parts):
    freq_index = np.arange(NF).reshape(freq_parts, rcv_parts, -1).transpose(1, 0, 2).reshape(-1, 1)
    phase = freq_index * np.arange(T_SIZE)[None, :] % T_SIZE
    angle = phase * (2.0 * math.pi / T_SIZE)
    factor = math.sqrt(2.0 / T_SIZE)
    table = np.stack([factor * np.cos(angle), -factor * np.sin(angle)], axis=1)
    return jnp.asarray(table.reshape(2 * NF, T_SIZE).astype(np.float32)).astype(jnp.bfloat16)


def split_three(value):
    high = lax.reduce_precision(value, 8, 7)
    rest = value - high
    middle = lax.reduce_precision(rest, 8, 7)
    return jnp.stack([high, middle, rest - middle])


def forward(op, points):
    def product(left, right):
        return jnp.einsum("akrn,nks->arks", left, right, preferred_element_type=jnp.float32)

    real_op, imag_op = op[:, :, 0], op[:, :, 1]
    real_in, imag_in = points[:, :, 0], points[:, :, 1]
    real_out = product(real_op, real_in) - product(imag_op, imag_in)
    imag_out = product(real_op, imag_in) + product(imag_op, real_in)
    return jnp.stack([real_out, imag_out], axis=3)


def adjoint(op, resid):
    def product(left, right):
        return jnp.einsum("akrn,arks->nks", left, right, preferred_element_type=jnp.float32)

    real_op, imag_op = op[:, :, 0], op[:, :, 1]
    real_res, imag_res = resid[:, :, :, 0], resid[:, :, :, 1]
    real_dir = product(real_op, real_res) + product(imag_op, imag_res)
    imag_dir = product(real_op, imag_res) - product(imag_op, real_res)
    return jnp.stack([real_dir, imag_dir], axis=2)


def local(freq_parts, rcv_parts, primaries_start, surface_operator, data_spectra, shrinkage):
    devices = freq_parts * rcv_parts
    own_n = NS // devices
    own_k = NF // devices
    rows = R // rcv_parts
    table = transform_table(freq_parts, rcv_parts)
    op = lax.all_to_all(surface_operator, "rcv", split_axis=0, concat_axis=0, tiled=True)
    op = op.reshape(rcv_parts, own_k, 2, rows, NS)
    data = lax.all_to_all(data_spectra, "rcv", split_axis=1, concat_axis=0, tiled=True)
    data = data.reshape(rcv_parts, rows, own_k, 2, S).astype(jnp.float32)
    primaries = primaries_start
    count_total = 2.0 * NF * NS * S
    residual = None
    for iteration in range(ITERS):
        spectra = jnp.einsum(
            "kt,nts->kns", table, primaries.astype(jnp.bfloat16), preferred_element_type=jnp.float32
        ).astype(jnp.bfloat16)
        spectra = spectra.reshape(devices, own_k, 2, own_n, S).transpose(0, 3, 1, 2, 4)
        points = lax.all_to_all(spectra, ALL, split_axis=0, concat_axis=0, tiled=True)
        points = points.reshape(NS, own_k, 2, S)
        residual = (data - forward(op, points)).astype(jnp.bfloat16)
        direction = adjoint(op, residual)
        residual_sq = jnp.sum(jnp.square(residual.astype(jnp.float32)))
        direction_sq = jnp.sum(jnp.square(direction))
        sums = jnp.concatenate([split_three(residual_sq), split_three(direction_sq)])
        sums = jnp.pad(sums.astype(jnp.bfloat16), (0, 2 * S - 6)).reshape(1, 1, 2, S)
        low = direction.astype(jnp.bfloat16).reshape(devices, own_n * own_k, 2, S)
        packed = jnp.concatenate([low, jnp.broadcast_to(sums, (devices, 1, 2, S))], axis=1)
        packed = lax.all_to_all(packed, ALL, split_axis=0, concat_axis=0, tiled=True)
        totals = jnp.sum(packed[:, -1, 0, :6].astype(jnp.float32), axis=0)
        residual_norm = jnp.sum(totals[:3])
        direction_norm = jnp.sum(totals[3:])
        step_size = 0.5 * residual_norm / (direction_norm + 1e-06)
        threshold = shrinkage[None, None, :] * (step_size * jnp.sqrt(direction_norm / count_total))
        own = packed[:, :-1].reshape(devices, own_n, own_k, 2, S).transpose(1, 0, 2, 3, 4)
        update = jnp.einsum(
            "kt,nks->nts",
            table,
            own.reshape(own_n, 2 * NF, S),
            preferred_element_type=jnp.float32,
        )
        moved = primaries + step_size * update
        primaries = moved - jnp.clip(moved, -threshold, threshold)
    residual = residual.reshape(R, own_k, 2, S)
    residual = lax.all_to_all(residual, "rcv", split_axis=0, concat_axis=1, tiled=True)
    return (primaries, residual)


def solution(mesh):
    freq_parts, rcv_parts = mesh.shape["freq"], mesh.shape["rcv"]

    def body(*args):
        return local(freq_parts, rcv_parts, *args)

    return jax.shard_map(
        body,
        mesh=mesh,
        in_specs=(
            P(("rcv", "freq"), None, None),
            P("freq", None, "rcv", None),
            P("rcv", "freq", None, None),
            P(),
        ),
        out_specs=(P(("rcv", "freq"), None, None), P("rcv", "freq", None, None)),
        check_vma=False,
    )
```

time: 499 us -> 242 us (0.48)
  blocking collectives: 205 us -> 32.7 us
  waiting for transfers between devices: 173 us -> 81.8 us
  starting transfers between devices: 19.2 us -> 37.3 us
  other arithmetic: 25.5 us -> 9.77 us
  between operations: 18.3 us -> 24.2 us
    psum x2 -> x0, blocking collectives: 154 us -> none  [local(): lax.psum((residual_sq, direction_sq), ('freq', 'rcv'))]
    reduce_scatter x2 -> x0, waiting for transfers between devices: 108 us -> none  [local(): lax.psum_scatter(adjoint_product(surface_operator, residual), 'rcv', scat...]
    all_to_all x2 -> x6, waiting for transfers between devices: 0.01 us -> 81.8 us  [the longest x2 41.4 us: local(): lax.all_to_all(packed, ALL, split_axis=0, concat_axis=0, tiled=True)]
    all_gather x2 -> x0, waiting for transfers between devices: 64.1 us -> none  [local(): lax.all_gather(spectra, 'rcv', axis=0, tiled=True)]
    all_to_all x2 -> x6, starting transfers between devices: 19.1 us -> 37.3 us  [the longest x2 13.3 us: local(): lax.all_to_all(packed, ALL, split_axis=0, concat_axis=0, tiled=True)]
    all_to_all x2 -> x1, blocking collectives: 50.6 us -> 32.7 us  [local(): lax.all_to_all(spectra, ALL, split_axis=0, concat_axis=0, tiled=True)]
    another operation x3 -> x0, other arithmetic: 17 us -> none
    another operation x2 -> x4, local copies, waits for them, and re-layouts: 20.6 us -> 5.87 us  [adjoint_product(): return jnp.stack([real_dir, imag_dir], axis=2)]
  transfers between devices with their start and end apart: 6 -> 6, of which waited for: 4 -> 5; matrix products, arithmetic and copies ran while one was open for 0% -> 9% of each run, Pallas kernels for 0% -> 0%
where the time goes in v1:
time: 242 us; the launch traced here: 240 us
  waiting for transfers between devices  81.8 us (34%)
  starting transfers between devices  37.3 us (15%)
  local copies, waits for them, and re-layouts  33.7 us (14%)
  blocking collectives  32.7 us (14%)
  between operations  24.2 us (10%)
  matrix products  20.9 us (9%)
  other arithmetic  9.77 us (4%)
    all_to_all x2, waiting for transfers between devices, local(): lax.all_to_all(packed, ALL, split_axis=0, concat_axis=0, tiled=True)  41.4 us
    all_to_all x1, blocking collectives, local(): lax.all_to_all(spectra, ALL, split_axis=0, concat_axis=0, tiled=True)  32.7 us
    all_to_all x1, waiting for transfers between devices, local(): lax.all_to_all(surface_operator, 'rcv', split_axis=0, concat_axis=0, tile...  18.3 us
    all_to_all x1, waiting for transfers between devices, local(): lax.all_to_all(spectra, ALL, split_axis=0, concat_axis=0, tiled=True)  17.3 us
    all_to_all x2, starting transfers between devices, local(): lax.all_to_all(packed, ALL, split_axis=0, concat_axis=0, tiled=True)  13.3 us
    dot_general x8, matrix products, product(): jnp.einsum('akrn,arks->nks', left, right, preferred_element_type=jnp.floa...  8.53 us
    all_to_all x1, starting transfers between devices, local(): lax.all_to_all(spectra, ALL, split_axis=0, concat_axis=0, tiled=True)  7.2 us
    unnamed x27, local copies, waits for them, and re-layouts  7.09 us
  transfers between devices with their start and end apart: 6, of which 5 were waited for; matrix products, arithmetic and copies ran while one was open for 9% of the time, Pallas kernels for 0%

profile of v1, /device:TPU:1, one launch (start us, length us, event | category | flops | bytes accessed | tf_op | source)
XLA Modules:
  0.0 240.3 jit_solution(11943342839610291102)
XLA Ops:
  0.6 1.9 copy.59
  2.5 6.6 %all-to-all-start = ((bf16[48,16,2,128]{3,0,2,1:T(8,128)(2,1)}), bf16[48,16,2,128]{3,0,2,1:T(8,128)(2,1)S(1)}, u32[]{:S(2)}, u32[]{:S(2)}) async-start(bf16[48,16,2,128]{3,0,2,1:T(8,128)(2,1)} %copy.59), calls=%async_computation | async-start | bytes 786432 | tf_op jit(solution)/shard_map/all_to_all | solution.py:64
  9.1 2.6 %convolution_convert_fusion.1 = bf16[1024,2,128]{2,0,1:T(8,128)(2,1)S(1)} fusion(bf16[1024,1024,1]{1,0,2:T(8,128)(2,1)} %constant.24, f32[2,1024,128]{2,1,0:T(8,128)} %param.5), kind=kOutput, calls=%fused_computation.7 | convolution fusion | flops 537395200 | bytes 3670016 | tf_op jit(solution)/shard_map/kt,nts->kns/dot_general | solution.py:70
  12.0 4.8 %all-to-all-done = bf16[48,16,2,128]{3,0,2,1:T(8,128)(2,1)S(1)} async-done(((bf16[48,16,2,128]{3,0,2,1:T(8,128)(2,1)}), bf16[48,16,2,128]{3,0,2,1:T(8,128)(2,1)S(1)}, u32[]{:S(2)}, u32[]{:S(2)}) %all-to-all-start) | async-done | bytes 393248 | tf_op jit(solution)/shard_map/all_to_all | solution.py:64
  16.8 32.7 %all_to_all.52 = bf16[256,2,2,2,128]{4,3,2,1,0:T(2,128)(2,1)} all-to-all(bf16[256,2,2,2,128]{4,3,2,1,0:T(2,128)(2,1)S(1)} %bitcast.237), channel_id=1, replica_groups=mesh['freq'=32,'rcv'=8] {'rcv','freq'}, dimensions={0} | all-to-all | bytes 1048576 | tf_op jit(solution)/shard_map/all_to_all | solution.py:74
  49.5 4.8 %all-to-all-start.2 = ((bf16[16,2,48,512]{3,2,1,0:T(8,128)(2,1)}), bf16[16,2,48,512]{3,2,1,0:T(8,128)(2,1)S(1)}, u32[]{:S(2)}, u32[]{:S(2)}) async-start(bf16[16,2,48,512]{3,2,1,0:T(8,128)(2,1)} %param.6), calls=%async_computation.2 | async-start | bytes 3145728 | tf_op jit(solution)/shard_map/all_to_all | solution.py:62
  54.4 2.2 copy.62
  56.6 18.3 %all-to-all-done.2 = bf16[16,2,48,512]{3,2,1,0:T(8,128)(2,1)S(1)} async-done(((bf16[16,2,48,512]{3,2,1,0:T(8,128)(2,1)}), bf16[16,2,48,512]{3,2,1,0:T(8,128)(2,1)S(1)}, u32[]{:S(2)}, u32[]{:S(2)}) %all-to-all-start.2) | async-done | bytes 1572896 | tf_op jit(solution)/shard_map/all_to_all | solution.py:62
  74.9 1.2 copy-done.1
  76.1 1.6 fusion.28
  79.2 0.8 multiply_reduce_fusion.1
  85.6 1.1 bitcast_convert_fusion.2
  86.6 1.0 bitcast_convert_fusion.3
  87.7 0.9 fusion.11
  93.2 1.8 copy.66
  95.1 1.8 copy.65
  97.1 1.6 pad_maximum_fusion
  98.7 1.9 copy.67
  100.6 6.0 %all-to-all-start.3 = ((bf16[256,5,2,128]{3,2,1,0:T(2,128)(2,1)}), bf16[256,5,2,128]{3,2,1,0:T(2,128)(2,1)S(1)}, u32[]{:S(2)}, u32[]{:S(2)}) async-start(bf16[256,5,2,128]{3,2,1,0:T(2,128)(2,1)} %copy.67), calls=%async_computation.3 | async-start | bytes 1310720 | tf_op jit(solution)/shard_map/all_to_all | solution.py:84
  106.6 2.5 %copy.71 = f32[2,1024,128]{1,2,0:T(8,128)} copy(f32[2,1024,128]{2,1,0:T(8,128)} %param.5) | data formatting | bytes 2097152 | tf_op args[0]
  109.1 20.5 %all-to-all-done.3 = bf16[256,5,2,128]{3,2,1,0:T(2,128)(2,1)S(1)} async-done(((bf16[256,5,2,128]{3,2,1,0:T(2,128)(2,1)}), bf16[256,5,2,128]{3,2,1,0:T(2,128)(2,1)S(1)}, u32[]{:S(2)}, u32[]{:S(2)}) %all-to-all-start.3) | async-done | bytes 655392 | tf_op jit(solution)/shard_map/all_to_all | solution.py:84
  130.1 1.3 copy.69
  131.7 0.7 slice_reduce_fusion.2
  134.6 2.9 %minimum_subtract_fusion.1 = f32[2,1024,128]{1,2,0:T(8,128)S(1)} fusion(f32[2,1024,128]{1,2,0:T(8,128)} %copy.71, bf16[2,1024,128]{2,1,0:T(8,128)(2,1)} %bitcast.235, bf16[1024,1024,1]{1,0,2:T(8,128)(2,1)} %constant.24, f32[128]{0:T(128)S(1)} %get-tuple-element.18, f32[128]{0:T(128)S(1)} %get-tuple-element.19, f32[]{:T(128)S(6)} %div.12), kind=kOutput, calls=%fused_computation.34 | convolution fusion | flops 538181632 | bytes 4719620 | tf_op jit(solution)/shard_map/kt,nks->nts/dot_general | solution.py:91
  137.5 1.6 fusion.4
  139.1 2.0 copy.72
  141.2 2.2 copy.73
  143.4 7.2 %all-to-all-start.4 = ((bf16[256,2,2,2,128]{4,3,2,1,0:T(2,128)(2,1)}), bf16[256,2,2,2,128]{4,3,2,1,0:T(2,128)(2,1)}, u32[]{:S(2)}, u32[]{:S(2)}) async-start(bf16[256,2,2,2,128]{4,3,2,1,0:T(2,128)(2,1)} %copy.73), calls=%async_computation.4 | async-start | bytes 1048576 | tf_op jit(solution)/shard_map/all_to_all | solution.py:74
  150.6 1.1 convert_bitcast_fusion
  151.6 0.9 copy.81
  152.6 17.3 %all-to-all-done.4 = bf16[256,2,2,2,128]{4,3,2,1,0:T(2,128)(2,1)} async-done(((bf16[256,2,2,2,128]{4,3,2,1,0:T(2,128)(2,1)}), bf16[256,2,2,2,128]{4,3,2,1,0:T(2,128)(2,1)}, u32[]{:S(2)}, u32[]{:S(2)}) %all-to-all-start.4) | async-done | bytes 524320 | tf_op jit(solution)/shard_map/all_to_all | solution.py:74
  169.8 1.4 copy.74
  172.8 0.8 multiply_reduce_fusion
  173.6 1.1 convolution_bitcast_fusion
  174.8 1.2 convolution_bitcast_fusion.2
  176.0 1.1 copy.82
  177.2 5.4 %all-to-all-start.6 = ((bf16[384,2,2,128]{3,1,2,0:T(2,128)(2,1)}), bf16[384,2,2,128]{3,1,2,0:T(2,128)(2,1)}, u32[]{:S(2)}, u32[]{:S(2)}) async-start(bf16[384,2,2,128]{3,1,2,0:T(2,128)(2,1)} %copy.82), calls=%async_computation.6 | async-start | bytes 786432 | tf_op jit(solution)/shard_map/all_to_all | solution.py:100
  182.6 2.2 bitcast_convert_fusion.1
  184.8 1.2 bitcast_convert_fusion
  190.7 1.9 fusion.12
  197.5 1.1 copy.76
  198.7 1.1 copy.75
  200.6 1.8 copy.77
  202.4 7.3 %all-to-all-start.5 = ((bf16[256,5,2,128]{3,2,1,0:T(2,128)(2,1)}), bf16[256,5,2,128]{3,2,1,0:T(2,128)(2,1)S(1)}, u32[]{:S(2)}, u32[]{:S(2)}) async-start(bf16[256,5,2,128]{3,2,1,0:T(2,128)(2,1)} %copy.77), calls=%async_computation.5 | async-start | bytes 1310720 | tf_op jit(solution)/shard_map/all_to_all | solution.py:84
  209.7 2.0 copy.83
  211.7 20.9 %all-to-all-done.5 = bf16[256,5,2,128]{3,2,1,0:T(2,128)(2,1)S(1)} async-done(((bf16[256,5,2,128]{3,2,1,0:T(2,128)(2,1)}), bf16[256,5,2,128]{3,2,1,0:T(2,128)(2,1)S(1)}, u32[]{:S(2)}, u32[]{:S(2)}) %all-to-all-start.5) | async-done | bytes 655392 | tf_op jit(solution)/shard_map/all_to_all | solution.py:84
  236.6 2.4 minimum_subtract_fusion
  239.0 1.3 copy.84
  (52 shorter events, 7.9 us)
Async XLA Ops:
  2.5 14.3 %all-to-all-start = ((bf16[48,16,2,128]{3,0,2,1:T(8,128)(2,1)}), bf16[48,16,2,128]{3,0,2,1:T(8,128)(2,1)S(1)}, u32[]{:S(2)}, u32[]{:S(2)}) async-start(bf16[48,16,2,128]{3,0,2,1:T(8,128)(2,1)} %copy.59), calls=%async_computation | async-start | bytes 786432 | tf_op jit(solution)/shard_map/all_to_all | solution.py:64
  16.8 58.1 %copy-start.3 = (bf16[48,16,2,128]{3,0,2,1:T(8,128)(2,1)}, bf16[48,16,2,128]{3,0,2,1:T(8,128)(2,1)S(1)}, u32[]{:S(2)}) copy-start(bf16[48,16,2,128]{3,0,2,1:T(8,128)(2,1)S(1)} %all-to-all-done) | copy-start | bytes 1179652
  49.5 25.4 %all-to-all-start.2 = ((bf16[16,2,48,512]{3,2,1,0:T(8,128)(2,1)}), bf16[16,2,48,512]{3,2,1,0:T(8,128)(2,1)S(1)}, u32[]{:S(2)}, u32[]{:S(2)}) async-start(bf16[16,2,48,512]{3,2,1,0:T(8,128)(2,1)} %param.6), calls=%async_computation.2 | async-start | bytes 3145728 | tf_op jit(solution)/shard_map/all_to_all | solution.py:62
  74.9 1.2 copy-start.1
  76.1 1.6 copy-start.2
  100.6 29.0 %all-to-all-start.3 = ((bf16[256,5,2,128]{3,2,1,0:T(2,128)(2,1)}), bf16[256,5,2,128]{3,2,1,0:T(2,128)(2,1)S(1)}, u32[]{:S(2)}, u32[]{:S(2)}) async-start(bf16[256,5,2,128]{3,2,1,0:T(2,128)(2,1)} %copy.67), calls=%async_computation.3 | async-start | bytes 1310720 | tf_op jit(solution)/shard_map/all_to_all | solution.py:84
  109.1 25.4 %copy-start.10 = (f32[128]{0:T(128)S(1)}, f32[128]{0:T(128)}, u32[]{:S(2)}) copy-start(f32[128]{0:T(128)} %param.8) | copy-start | bytes 1540
  134.6 3.0 %copy-start = (bf16[1024,1024,1]{1,0,2:T(8,128)(2,1)S(1)}, bf16[1024,1024,1]{1,0,2:T(8,128)(2,1)}, u32[]{:S(2)}) copy-start(bf16[1024,1024,1]{1,0,2:T(8,128)(2,1)} %constant.24) | copy-start | bytes 6291460
  143.4 26.5 %all-to-all-start.4 = ((bf16[256,2,2,2,128]{4,3,2,1,0:T(2,128)(2,1)}), bf16[256,2,2,2,128]{4,3,2,1,0:T(2,128)(2,1)}, u32[]{:S(2)}, u32[]{:S(2)}) async-start(bf16[256,2,2,2,128]{4,3,2,1,0:T(2,128)(2,1)} %copy.73), calls=%async_computation.4 | async-start | bytes 1048576 | tf_op jit(solution)/shard_map/all_to_all | solution.py:74
  172.8 3.1 %copy-start.6 = (f32[8,48,2,2,128]{4,1,0,3,2:T(8,128)S(1)}, f32[8,48,2,2,128]{4,1,0,3,2:T(8,128)}, u32[]{:S(2)}) copy-start(f32[8,48,2,2,128]{4,1,0,3,2:T(8,128)} %copy.81) | copy-start | bytes 2359300
  173.6 2.4 copy-start.4
  175.9 6.7 %copy-start.8 = (f32[2,128,512]{2,1,0:T(8,128)S(1)}, f32[2,128,512]{2,1,0:T(8,128)}, u32[]{:S(2)}) copy-start(f32[2,128,512]{2,1,0:T(8,128)} %convolution_bitcast_fusion.2) | copy-start | bytes 1572868
  176.0 8.8 %copy-start.7 = (f32[2,128,512]{2,1,0:T(8,128)S(1)}, f32[2,128,512]{2,1,0:T(8,128)}, u32[]{:S(2)}) copy-start(f32[2,128,512]{2,1,0:T(8,128)} %convolution_bitcast_fusion) | copy-start | bytes 1572868
  177.2 7.6 %copy-start.5 = (bf16[8,48,2,2,128]{4,1,0,2,3:T(8,128)(2,1)S(1)}, bf16[8,48,2,2,128]{4,1,0,2,3:T(8,128)(2,1)}, u32[]{:S(2)}) copy-start(bf16[8,48,2,2,128]{4,1,0,2,3:T(8,128)(2,1)} %copy-done.4) | copy-start | bytes 1179652
  177.2 25.2 %all-to-all-start.6 = ((bf16[384,2,2,128]{3,1,2,0:T(2,128)(2,1)}), bf16[384,2,2,128]{3,1,2,0:T(2,128)(2,1)}, u32[]{:S(2)}, u32[]{:S(2)}) async-start(bf16[384,2,2,128]{3,1,2,0:T(2,128)(2,1)} %copy.82), calls=%async_computation.6 | async-start | bytes 786432 | tf_op jit(solution)/shard_map/all_to_all | solution.py:100
  184.8 5.9 %copy-start.9 = (f32[2,128,512]{2,1,0:T(8,128)S(1)}, f32[2,128,512]{2,1,0:T(8,128)}, u32[]{:S(2)}) copy-start(f32[2,128,512]{2,1,0:T(8,128)} %get-tuple-element.31) | copy-start | bytes 1572868
  202.4 30.2 %all-to-all-start.5 = ((bf16[256,5,2,128]{3,2,1,0:T(2,128)(2,1)}), bf16[256,5,2,128]{3,2,1,0:T(2,128)(2,1)S(1)}, u32[]{:S(2)}, u32[]{:S(2)}) async-start(bf16[256,5,2,128]{3,2,1,0:T(2,128)(2,1)} %copy.77), calls=%async_computation.5 | async-start | bytes 1310720 | tf_op jit(solution)/shard_map/all_to_all | solution.py:84

commit v2 on v1

v2 whole, which is shorter than its diff:
```python
import functools
import math

import jax
import jax.numpy as jnp
import numpy as np
from jax import lax
from jax.experimental import pallas as pl
from jax.experimental.pallas import tpu as pltpu
from jax.sharding import PartitionSpec as P

S = 128
NS = 512
R = 384
T_SIZE = 1024
ITERS = 2
NF = 512
ALL = ("rcv", "freq")
PARTS = 4
WIDE = PARTS + 1


def transform_table(freq_parts, rcv_parts):
    freq_index = np.arange(NF).reshape(freq_parts, rcv_parts, -1).transpose(2, 1, 0).reshape(-1, 1, freq_parts * rcv_parts, 1)
    phase = freq_index * np.arange(T_SIZE) % T_SIZE
    angle = phase * (2.0 * math.pi / T_SIZE)
    factor = math.sqrt(2.0 / T_SIZE)
    table = np.concatenate([factor * np.cos(angle), -factor * np.sin(angle)], axis=1)
    return jnp.asarray(table.reshape(2 * NF, T_SIZE).astype(np.float32)).astype(jnp.bfloat16)


def call(kernel, out_shape, scratch, inputs, flops):
    return pl.pallas_call(
        kernel,
        out_shape=out_shape,
        in_specs=[pl.BlockSpec(memory_space=pltpu.VMEM)] * len(inputs),
        out_specs=jax.tree.map(lambda _: pl.BlockSpec(memory_space=pltpu.VMEM), out_shape),
        scratch_shapes=[pltpu.VMEM(shape, jnp.float32) for shape in scratch],
        compiler_params=pltpu.CompilerParams(vmem_limit_bytes=32 * 2**20),
        cost_estimate=pl.CostEstimate(flops=flops, bytes_accessed=4 * 2**20, transcendentals=0),
    )(*inputs)


def transform(table_ref, low, rows_ref, spectra_ref, owners):
    for part in range(PARTS):
        block = jnp.dot(table_ref[pl.ds(part * owners, owners), :], low, preferred_element_type=jnp.float32)
        for point in range(2):
            rows_ref[pl.ds(point * PARTS + part, owners, stride=2 * PARTS), :] = block[:, point * S:(point + 1) * S]
    spectra_ref[...] = rows_ref[...].astype(jnp.bfloat16)


def start_kernel(owners, primaries_ref, table_ref, spectra_ref, rows_ref):
    low = jnp.concatenate([primaries_ref[0].astype(jnp.bfloat16), primaries_ref[1].astype(jnp.bfloat16)], axis=1)
    transform(table_ref, low, rows_ref, spectra_ref, owners)


def split_three(value):
    high = value.astype(jnp.bfloat16).astype(jnp.float32)
    rest = value - high
    middle = rest.astype(jnp.bfloat16).astype(jnp.float32)
    return [high, middle, rest - middle]


def physics_kernel(blocks, points_ref, op_ref, data_ref, packed_ref, residual_ref, rows_ref, wide_ref):
    rows = op_ref.shape[2]
    rows_ref[...] = points_ref[...].astype(jnp.float32)
    residual_sq = jnp.zeros((1, 1), jnp.float32)
    direction_sq = jnp.zeros((1, 1), jnp.float32)
    for k in range(2):
        spectra = jnp.concatenate(
            [rows_ref[pl.ds(2 * k + c, NS, stride=PARTS), :].astype(jnp.bfloat16) for c in range(2)], axis=1
        )
        op = jnp.concatenate([op_ref[2 * a + k].reshape(2 * rows, NS) for a in range(blocks)], axis=0)
        product = jnp.dot(op, spectra, preferred_element_type=jnp.float32).reshape(blocks, 2, rows, 2 * S)
        stacked = []
        for a in range(blocks):
            real = product[a, 0, :, :S] - product[a, 1, :, S:]
            imag = product[a, 0, :, S:] + product[a, 1, :, :S]
            real = (data_ref[2 * a + k, 0].astype(jnp.float32) - real).astype(jnp.bfloat16)
            imag = (data_ref[2 * a + k, 1].astype(jnp.float32) - imag).astype(jnp.bfloat16)
            residual_ref[2 * a + k, 0] = real
            residual_ref[2 * a + k, 1] = imag
            wide_real = real.astype(jnp.float32)
            wide_imag = imag.astype(jnp.float32)
            residual_sq += jnp.sum(wide_real * wide_real + wide_imag * wide_imag, keepdims=True)
            stacked.append(jnp.concatenate([real, imag], axis=1))
            stacked.append(jnp.concatenate([imag, -real], axis=1))
        direction = lax.dot_general(
            op, jnp.concatenate(stacked, axis=0), (((0,), (0,)), ((), ())), preferred_element_type=jnp.float32
        )
        direction_sq += jnp.sum(direction * direction, keepdims=True)
        for c in range(2):
            wide_ref[pl.ds(2 * k + c, NS, stride=WIDE), :] = direction[:, c * S:(c + 1) * S]
    lane = lax.broadcasted_iota(jnp.int32, (8, S), 1)
    sums = jnp.zeros((8, S), jnp.float32)
    for place, piece in enumerate(split_three(residual_sq) + split_three(direction_sq)):
        sums = jnp.where(lane == place, piece, sums)
    wide_ref[pl.ds(PARTS, NS, stride=WIDE), :] = jnp.broadcast_to(sums[:1], (NS, S))
    packed_ref[...] = wide_ref[...].astype(jnp.bfloat16)


def update(owners, packed_ref, table_ref, primaries_ref, shrinkage_ref, wide_ref, new_ref):
    wide_ref[...] = packed_ref[...].astype(jnp.float32)
    totals = jnp.sum(wide_ref[pl.ds(PARTS, owners, stride=2 * WIDE), :], axis=0, keepdims=True)
    lane = lax.broadcasted_iota(jnp.int32, (1, S), 1)
    residual_norm = jnp.sum(jnp.where(lane < 3, totals, 0.0), axis=1, keepdims=True)
    direction_norm = jnp.sum(jnp.where((lane >= 3) & (lane < 6), totals, 0.0), axis=1, keepdims=True)
    step_size = 0.5 * residual_norm / (direction_norm + 1e-06)
    threshold = shrinkage_ref[...] * (step_size * jnp.sqrt(direction_norm / (2.0 * NF * NS * S)))
    sides = []
    for point in range(2):
        pieces = [
            wide_ref[pl.ds(point * WIDE + part, owners, stride=2 * WIDE), :].astype(jnp.bfloat16)
            for part in range(PARTS)
        ]
        sides.append(jnp.concatenate(pieces, axis=0))
    direction = jnp.concatenate(sides, axis=1)
    lows = []
    block = 256
    for start in range(0, T_SIZE, block):
        change = lax.dot_general(
            table_ref[:, pl.ds(start, block)], direction, (((0,), (0,)), ((), ())), preferred_element_type=jnp.float32
        )
        halves = []
        for point in range(2):
            moved = primaries_ref[point, pl.ds(start, block), :] + step_size * change[:, point * S:(point + 1) * S]
            new = moved - jnp.clip(moved, -threshold, threshold)
            new_ref[point, pl.ds(start, block), :] = new
            halves.append(new.astype(jnp.bfloat16))
        lows.append(jnp.concatenate(halves, axis=1))
    return lows


def middle_kernel(owners, packed_ref, table_ref, primaries_ref, shrinkage_ref, new_ref, spectra_ref, wide_ref, rows_ref):
    lows = update(owners, packed_ref, table_ref, primaries_ref, shrinkage_ref, wide_ref, new_ref)
    transform(table_ref, jnp.concatenate(lows, axis=0), rows_ref, spectra_ref, owners)


def last_kernel(owners, packed_ref, table_ref, primaries_ref, shrinkage_ref, new_ref, wide_ref):
    update(owners, packed_ref, table_ref, primaries_ref, shrinkage_ref, wide_ref, new_ref)


def exchange(array, devices, scope):
    with jax.named_scope(scope):
        pairs = array.reshape(devices, array.shape[0] // (2 * devices), 2, S)
        return lax.all_to_all(pairs, ALL, split_axis=0, concat_axis=0, tiled=True).reshape(array.shape)


def local(freq_parts, rcv_parts, primaries_start, surface_operator, data_spectra, shrinkage):
    devices = freq_parts * rcv_parts
    rows = R // rcv_parts
    half, wide = (devices * 2 * PARTS, S), (devices * 2 * WIDE, S)
    bf16, f32 = jnp.bfloat16, jnp.float32
    table = transform_table(freq_parts, rcv_parts)
    shrinkage = shrinkage.reshape(1, S)
    with jax.named_scope("operator"):
        op = lax.all_to_all(surface_operator, "rcv", split_axis=0, concat_axis=0, tiled=True)
    with jax.named_scope("recorded"):
        data = lax.all_to_all(data_spectra.transpose(1, 2, 0, 3), "rcv", split_axis=0, concat_axis=0, tiled=True)
    primaries = primaries_start
    spectra = call(
        functools.partial(start_kernel, devices),
        jax.ShapeDtypeStruct(half, bf16),
        [half],
        (primaries, table),
        2 * 1024 * 1024 * 256,
    )
    for iteration in range(ITERS):
        points = exchange(spectra, devices, f"spectra{iteration}")
        packed, residual = call(
            functools.partial(physics_kernel, rcv_parts),
            (jax.ShapeDtypeStruct(wide, bf16), jax.ShapeDtypeStruct((2 * rcv_parts, 2, rows, S), bf16)),
            [half, wide],
            (points, op, data),
            4 * 2 * 768 * 512 * 256,
        )
        packed = exchange(packed, devices, f"direction{iteration}")
        shape = jax.ShapeDtypeStruct(primaries.shape, f32)
        inputs = (packed, table, primaries, shrinkage)
        if iteration + 1 < ITERS:
            primaries, spectra = call(
                functools.partial(middle_kernel, devices),
                (shape, jax.ShapeDtypeStruct(half, bf16)),
                [wide, half],
                inputs,
                4 * 1024 * 1024 * 256,
            )
        else:
            primaries = call(functools.partial(last_kernel, devices), shape, [wide], inputs, 2 * 1024 * 1024 * 256)
    with jax.named_scope("returned"):
        residual = lax.all_to_all(residual, "rcv", split_axis=0, concat_axis=0, tiled=True)
    return (primaries, residual.transpose(2, 0, 1, 3))


def solution(mesh):
    freq_parts, rcv_parts = mesh.shape["freq"], mesh.shape["rcv"]

    def body(*args):
        return local(freq_parts, rcv_parts, *args)

    return jax.shard_map(
        body,
        mesh=mesh,
        in_specs=(
            P(("rcv", "freq"), None, None),
            P("freq", None, "rcv", None),
            P("rcv", "freq", None, None),
            P(),
        ),
        out_specs=(P(("rcv", "freq"), None, None), P("rcv", "freq", None, None)),
        check_vma=False,
    )
```

time: 242 us -> 179 us (0.74)
  blocking collectives: 32.7 us -> 124 us
  waiting for transfers between devices: 81.8 us -> 27.3 us
  local copies, waits for them, and re-layouts: 33.7 us -> 5.87 us
  starting transfers between devices: 37.3 us -> 12.4 us
  between operations: 24.2 us -> 0.68 us
  matrix products: 20.9 us -> 0 us
  other arithmetic: 9.77 us -> 0 us
  Pallas kernels: 0 us -> 8.73 us
    all_to_all x1 -> x5, blocking collectives: 32.7 us -> 124 us  [the longest x3 87.2 us: exchange(): lax.all_to_all(pairs, ALL, split_axis=0, concat_axis=0, tiled=True)]
    all_to_all x6 -> x2, waiting for transfers between devices: 81.8 us -> 27.3 us  [the longest x1 22 us: exchange(): lax.all_to_all(pairs, ALL, split_axis=0, concat_axis=0, tiled=True)]
    all_to_all x6 -> x2, starting transfers between devices: 37.3 us -> 12.4 us  [the longest x1 6.56 us: local(): lax.all_to_all(data_spectra.transpose(1, 2, 0, 3), 'rcv', split_axis=0, c...]
    dot_general x20 -> x0, matrix products: 20.9 us -> none  [the longest x8 8.53 us: product(): jnp.einsum('akrn,arks->nks', left, right, preferred_element_type=jnp.floa...]
    pallas_call x0 -> x5, Pallas kernels: none -> 8.73 us  [call(): pl.pallas_call(kernel, out_shape=out_shape, in_specs=[pl.BlockSpec(memory...]
    reduce_sum x8 -> x0, other arithmetic: 6.42 us -> none  [the longest x2 2.81 us: local(): direction_sq = jnp.sum(jnp.square(direction))]
    another operation x4 -> x0, local copies, waits for them, and re-layouts: 5.87 us -> none
    all_to_all x3 -> x0, local copies, waits for them, and re-layouts: 5.7 us -> none  [the longest x2 3.69 us: local(): lax.all_to_all(spectra, ALL, split_axis=0, concat_axis=0, tiled=True)]
  transfers between devices with their start and end apart: 6 -> 2, of which waited for: 5 -> 2; matrix products, arithmetic and copies ran while one was open for 9% -> 1% of each run, Pallas kernels for 0% -> 0%
where the time goes in v2:
time: 179 us
  blocking collectives  124 us (69%)
  waiting for transfers between devices  27.3 us (15%)
  starting transfers between devices  12.4 us (7%)
  Pallas kernels  8.73 us (5%)
  local copies, waits for them, and re-layouts  5.87 us (3%)
    all_to_all x3, blocking collectives, exchange(): lax.all_to_all(pairs, ALL, split_axis=0, concat_axis=0, tiled=True)  87.2 us
    all_to_all x1, blocking collectives, local(): lax.all_to_all(surface_operator, 'rcv', split_axis=0, concat_axis=0, tile...  24.6 us
    all_to_all x1, waiting for transfers between devices, exchange(): lax.all_to_all(pairs, ALL, split_axis=0, concat_axis=0, tiled=True)  22 us
    all_to_all x1, blocking collectives, local(): lax.all_to_all(residual, 'rcv', split_axis=0, concat_axis=0, tiled=True)  12.1 us
    pallas_call x5, Pallas kernels, call(): pl.pallas_call(kernel, out_shape=out_shape, in_specs=[pl.BlockSpec(memory...  8.73 us
    all_to_all x1, starting transfers between devices, local(): lax.all_to_all(data_spectra.transpose(1, 2, 0, 3), 'rcv', split_axis=0, c...  6.56 us
    all_to_all x1, starting transfers between devices, exchange(): lax.all_to_all(pairs, ALL, split_axis=0, concat_axis=0, tiled=True)  5.89 us
    unnamed x16, local copies, waits for them, and re-layouts  5.87 us
  transfers between devices with their start and end apart: 2, of which 2 were waited for; matrix products, arithmetic and copies ran while one was open for 1% of the time, Pallas kernels for 0%

profile of v2, /device:TPU:1, one launch (start us, length us, event | category | flops | bytes accessed | tf_op | source)
XLA Modules:
  0.0 179.0 jit_solution(700951179561227792)
XLA Ops:
  0.6 0.0 copy-start.2
  0.6 2.0 %copy.10 = bf16[48,16,2,128]{3,0,2,1:T(8,128)(2,1)} copy(bf16[48,16,2,128]{3,2,1,0:T(2,128)(2,1)} %param.7) | data formatting | bytes 786432 | tf_op args[2]
  2.6 6.6 %all-to-all-start.2 = ((bf16[16,2,48,128]{3,2,1,0:T(8,128)(2,1)}), bf16[16,2,48,128]{3,2,1,0:T(8,128)(2,1)S(1)}, u32[]{:S(2)}, u32[]{:S(2)}) async-start(bf16[16,2,48,128]{3,2,1,0:T(8,128)(2,1)} %bitcast.12), calls=%async_computation.2 | async-start | bytes 786432 | tf_op jit(solution)/shard_map/recorded/all_to_all | solution.py:159
  9.2 0.0 copy-done.2
  9.2 0.0 copy-start
  9.2 1.6 copy-done
  10.8 0.0 copy-start.6
  10.8 0.8 shard_map.68
  11.6 5.3 %all-to-all-done.2.data_ref = bf16[16,2,48,128]{3,2,1,0:T(8,128)(2,1)S(1)} async-done(((bf16[16,2,48,128]{3,2,1,0:T(8,128)(2,1)}), bf16[16,2,48,128]{3,2,1,0:T(8,128)(2,1)S(1)}, u32[]{:S(2)}, u32[]{:S(2)}) %all-to-all-start.2) | async-done | bytes 393248 | tf_op jit(solution)/shard_map/recorded/all_to_all | solution.py:159
  16.9 32.6 %all_to_all.35 = bf16[256,4,2,128]{3,2,1,0:T(2,128)(2,1)S(1)} all-to-all(bf16[256,4,2,128]{3,2,1,0:T(2,128)(2,1)S(1)} %bitcast.14), channel_id=1, replica_groups=mesh['freq'=32,'rcv'=8] {'rcv','freq'}, dimensions={0} | all-to-all | bytes 1048576 | tf_op jit(solution)/shard_map/spectra0/all_to_all | solution.py:146
  49.5 0.0 copy-done.6
  49.5 24.6 %all_to_all.36.op_ref = bf16[16,2,48,512]{3,2,1,0:T(8,128)(2,1)S(1)} all-to-all(bf16[16,2,48,512]{3,2,1,0:T(8,128)(2,1)S(1)} %copy-done.6), channel_id=1, replica_groups=mesh['freq'=32,'rcv'=8] {'rcv'}, dimensions={0} | all-to-all | bytes 3145728 | tf_op jit(solution)/shard_map/operator/all_to_all | solution.py:157
  74.1 0.0 copy-start.1
  74.1 0.0 copy-start.5
  74.1 1.8 %shard_map.69 = (bf16[2560,128]{1,0:T(8,128)(2,1)S(1)}, bf16[16,2,48,128]{3,2,1,0:T(8,128)(2,1)}) custom-call(bf16[2048,128]{1,0:T(8,128)(2,1)S(1)} %bitcast.18, bf16[16,2,48,512]{3,2,1,0:T(8,128)(2,1)S(1)} %all_to_all.36.op_ref, bf16[16,2,48,128]{3,2,1,0:T(8,128)(2,1)S(1)} %all-to-all-done.2.data_ref), custom_call_target="tpu_custom_call" | custom-call | flops 805306368 | bytes 4194304 | tf_op jit(solution)/shard_map/pallas_call | solution.py:33
  75.9 28.8 %all_to_all.37 = bf16[256,5,2,128]{3,2,1,0:T(2,128)(2,1)S(1)} all-to-all(bf16[256,5,2,128]{3,2,1,0:T(2,128)(2,1)S(1)} %bitcast.15), channel_id=1, replica_groups=mesh['freq'=32,'rcv'=8] {'rcv','freq'}, dimensions={0} | all-to-all | bytes 1310720 | tf_op jit(solution)/shard_map/direction0/all_to_all | solution.py:146
  104.7 0.0 copy-done.1
  104.7 0.0 copy-done.5
  104.7 1.7 shard_map.70
  106.4 0.0 copy-start.3
  106.4 25.9 %all_to_all.38 = bf16[256,4,2,128]{3,2,1,0:T(2,128)(2,1)S(1)} all-to-all(bf16[256,4,2,128]{3,2,1,0:T(2,128)(2,1)S(1)} %bitcast.19), channel_id=1, replica_groups=mesh['freq'=32,'rcv'=8] {'rcv','freq'}, dimensions={0} | all-to-all | bytes 1048576 | tf_op jit(solution)/shard_map/spectra1/all_to_all | solution.py:146
  132.3 2.5 %shard_map.71 = (bf16[2560,128]{1,0:T(8,128)(2,1)}, bf16[16,2,48,128]{3,2,1,0:T(8,128)(2,1)S(1)}) custom-call(bf16[2048,128]{1,0:T(8,128)(2,1)S(1)} %bitcast.17, bf16[16,2,48,512]{3,2,1,0:T(8,128)(2,1)S(1)} %all_to_all.36.op_ref, bf16[16,2,48,128]{3,2,1,0:T(8,128)(2,1)S(1)} %all-to-all-done.2.data_ref), custom_call_target="tpu_custom_call" | custom-call | flops 805306368 | bytes 4194304 | tf_op jit(solution)/shard_map/pallas_call | solution.py:33
  134.8 0.0 copy-done.3
  134.8 12.1 %all_to_all.39 = bf16[16,2,48,128]{3,2,1,0:T(8,128)(2,1)S(1)} all-to-all(bf16[16,2,48,128]{3,2,1,0:T(8,128)(2,1)S(1)} %get-tuple-element.11), channel_id=1, replica_groups=mesh['freq'=32,'rcv'=8] {'rcv'}, dimensions={0} | all-to-all | bytes 786432 | tf_op jit(solution)/shard_map/returned/all_to_all | solution.py:191
  146.9 5.9 %all-to-all-start.5 = ((bf16[256,5,2,128]{3,2,1,0:T(2,128)(2,1)}), bf16[256,5,2,128]{3,2,1,0:T(2,128)(2,1)S(1)}, u32[]{:S(2)}, u32[]{:S(2)}) async-start(bf16[256,5,2,128]{3,2,1,0:T(2,128)(2,1)} %bitcast.8), calls=%async_computation.5 | async-start | bytes 1310720 | tf_op jit(solution)/shard_map/direction1/all_to_all | solution.py:146
  152.8 1.1 copy.8
  153.8 22.0 %all-to-all-done.5 = bf16[256,5,2,128]{3,2,1,0:T(2,128)(2,1)S(1)} async-done(((bf16[256,5,2,128]{3,2,1,0:T(2,128)(2,1)}), bf16[256,5,2,128]{3,2,1,0:T(2,128)(2,1)S(1)}, u32[]{:S(2)}, u32[]{:S(2)}) %all-to-all-start.5) | async-done | bytes 655392 | tf_op jit(solution)/shard_map/direction1/all_to_all | solution.py:146
  175.8 0.0 copy-start.4
  175.8 1.2 copy-done.4
  177.1 1.9 %shard_map.72 = f32[2,1024,128]{2,1,0:T(8,128)} custom-call(bf16[2560,128]{1,0:T(8,128)(2,1)S(1)} %bitcast.13, bf16[1024,1024]{1,0:T(8,128)(2,1)S(1)} %copy-done.1, f32[2,1024,128]{2,1,0:T(8,128)S(1)} %copy-done.4, f32[1,128]{1,0:T(1,128)S(1)} %bitcast.21), custom_call_target="tpu_custom_call" | custom-call | flops 536870912 | bytes 4194304 | tf_op jit(solution)/shard_map/pallas_call | solution.py:33
Async XLA Ops:
  0.6 8.6 %copy-start.2 = (f32[2,1024,128]{2,1,0:T(8,128)S(1)}, f32[2,1024,128]{2,1,0:T(8,128)}, u32[]{:S(2)}) copy-start(f32[2,1024,128]{2,1,0:T(8,128)} %primaries_ref.3) | copy-start | bytes 3145732
  2.6 14.3 %all-to-all-start.2 = ((bf16[16,2,48,128]{3,2,1,0:T(8,128)(2,1)}), bf16[16,2,48,128]{3,2,1,0:T(8,128)(2,1)S(1)}, u32[]{:S(2)}, u32[]{:S(2)}) async-start(bf16[16,2,48,128]{3,2,1,0:T(8,128)(2,1)} %bitcast.12), calls=%async_computation.2 | async-start | bytes 786432 | tf_op jit(solution)/shard_map/recorded/all_to_all | solution.py:159
  9.2 1.6 copy-start
  10.8 38.7 %copy-start.6 = (bf16[16,2,48,512]{3,2,1,0:T(8,128)(2,1)S(1)}, bf16[16,2,48,512]{3,2,1,0:T(8,128)(2,1)}, u32[]{:S(2)}) copy-start(bf16[16,2,48,512]{3,2,1,0:T(8,128)(2,1)} %param.6) | copy-start | bytes 4718596
  74.1 30.6 %copy-start.1 = (bf16[1024,1024]{1,0:T(8,128)(2,1)S(1)}, bf16[1024,1024]{1,0:T(8,128)(2,1)}, u32[]{:S(2)}) copy-start(bf16[1024,1024]{1,0:T(8,128)(2,1)} %constant.6.table_ref) | copy-start | bytes 6291460
  74.1 30.6 %copy-start.5 = (f32[128]{0:T(128)S(1)}, f32[128]{0:T(128)}, u32[]{:S(2)}) copy-start(f32[128]{0:T(128)} %param.8) | copy-start | bytes 1540
  106.4 28.4 %copy-start.3 = (f32[2,1024,128]{2,1,0:T(8,128)}, f32[2,1024,128]{2,1,0:T(8,128)S(1)}, u32[]{:S(2)}) copy-start(f32[2,1024,128]{2,1,0:T(8,128)S(1)} %get-tuple-element.10.primaries_ref) | copy-start | bytes 3145732
  146.9 28.9 %all-to-all-start.5 = ((bf16[256,5,2,128]{3,2,1,0:T(2,128)(2,1)}), bf16[256,5,2,128]{3,2,1,0:T(2,128)(2,1)S(1)}, u32[]{:S(2)}, u32[]{:S(2)}) async-start(bf16[256,5,2,128]{3,2,1,0:T(2,128)(2,1)} %bitcast.8), calls=%async_computation.5 | async-start | bytes 1310720 | tf_op jit(solution)/shard_map/direction1/all_to_all | solution.py:146
  175.8 1.2 copy-start.4

commit v3 on v2

--- a/solution.py
+++ b/solution.py
@@ -9,6 +9,7 @@
 from jax.experimental.pallas import tpu as pltpu
 from jax.sharding import PartitionSpec as P
 
+
 S = 128
 NS = 512
 R = 384
@@ -16,26 +17,41 @@
 ITERS = 2
 NF = 512
 ALL = ("rcv", "freq")
+LANES = 128
 PARTS = 4
 WIDE = PARTS + 1
 
 
-def transform_table(freq_parts, rcv_parts):
-    freq_index = np.arange(NF).reshape(freq_parts, rcv_parts, -1).transpose(2, 1, 0).reshape(-1, 1, freq_parts * rcv_parts, 1)
-    phase = freq_index * np.arange(T_SIZE) % T_SIZE
-    angle = phase * (2.0 * math.pi / T_SIZE)
+def table_base(freq_parts, rcv_parts):
+    freq_index = np.arange(NF).reshape(freq_parts, rcv_parts, -1).transpose(2, 1, 0).reshape(-1, 1)
+    angle = freq_index * np.arange(LANES) % T_SIZE * (2.0 * math.pi / T_SIZE)
     factor = math.sqrt(2.0 / T_SIZE)
-    table = np.concatenate([factor * np.cos(angle), -factor * np.sin(angle)], axis=1)
-    return jnp.asarray(table.reshape(2 * NF, T_SIZE).astype(np.float32)).astype(jnp.bfloat16)
-
-
-def call(kernel, out_shape, scratch, inputs, flops):
+    return jnp.asarray(np.stack([factor * np.cos(angle), factor * np.sin(angle)]).astype(np.float32))
+
+
+def fill_table(base_ref, table_ref, owners, rcv_parts):
+    run = owners // rcv_parts
+    for place in range(2):
+        for owner in range(rcv_parts):
+            rows = pl.ds(place * owners + owner * run, run)
+            cosine, sine = base_ref[0, rows, :], base_ref[1, rows, :]
+            for tile in range(T_SIZE // LANES):
+                turn = math.pi / 4 * ((2 * owner + place) * tile % 8)
+                cos, sin = round(math.cos(turn), 12), round(math.sin(turn), 12)
+                columns = pl.ds(tile * LANES, LANES)
+                real = cosine * cos - sine * sin
+                imag = -(sine * cos + cosine * sin)
+                for part, value in ((0, real), (1, imag)):
+                    table_ref[pl.ds((2 * place + part) * owners + owner * run, run), columns] = value.astype(jnp.bfloat16)
+
+
+def call(kernel, out_shape, scratch, inputs, flops, spaces=None):
     return pl.pallas_call(
         kernel,
         out_shape=out_shape,
-        in_specs=[pl.BlockSpec(memory_space=pltpu.VMEM)] * len(inputs),
+        in_specs=[pl.BlockSpec(memory_space=space) for space in spaces or [pltpu.VMEM] * len(inputs)],
         out_specs=jax.tree.map(lambda _: pl.BlockSpec(memory_space=pltpu.VMEM), out_shape),
-        scratch_shapes=[pltpu.VMEM(shape, jnp.float32) for shape in scratch],
+        scratch_shapes=scratch,
         compiler_params=pltpu.CompilerParams(vmem_limit_bytes=32 * 2**20),
         cost_estimate=pl.CostEstimate(flops=flops, bytes_accessed=4 * 2**20, transcendentals=0),
     )(*inputs)
@@ -49,7 +65,8 @@
     spectra_ref[...] = rows_ref[...].astype(jnp.bfloat16)
 
 
-def start_kernel(owners, primaries_ref, table_ref, spectra_ref, rows_ref):
+def start_kernel(owners, rcv_parts, primaries_ref, base_ref, spectra_ref, rows_ref, table_ref):
+    fill_table(base_ref, table_ref, owners, rcv_parts)
     low = jnp.concatenate([primaries_ref[0].astype(jnp.bfloat16), primaries_ref[1].astype(jnp.bfloat16)], axis=1)
     transform(table_ref, low, rows_ref, spectra_ref, owners)
 
@@ -61,25 +78,35 @@
     return [high, middle, rest - middle]
 
 
-def physics_kernel(blocks, points_ref, op_ref, data_ref, packed_ref, residual_ref, rows_ref, wide_ref):
-    rows = op_ref.shape[2]
+def physics_kernel(blocks, returned, points_ref, *refs):
+    sources, data_refs = refs[:blocks], refs[blocks:2 * blocks]
+    packed_ref = refs[2 * blocks]
+    residual_refs = refs[2 * blocks + 1:2 * blocks + 1 + returned]
+    op_ref, rows_ref, wide_ref, sem = refs[2 * blocks + 1 + returned:]
+    rows = op_ref.shape[3]
+    copies = [pltpu.make_async_copy(source, op_ref.at[a], sem.at[a]) for a, source in enumerate(sources)]
+    for copy in copies:
+        copy.start()
     rows_ref[...] = points_ref[...].astype(jnp.float32)
+    for copy in copies:
+        copy.wait()
     residual_sq = jnp.zeros((1, 1), jnp.float32)
     direction_sq = jnp.zeros((1, 1), jnp.float32)
     for k in range(2):
         spectra = jnp.concatenate(
             [rows_ref[pl.ds(2 * k + c, NS, stride=PARTS), :].astype(jnp.bfloat16) for c in range(2)], axis=1
         )
-        op = jnp.concatenate([op_ref[2 * a + k].reshape(2 * rows, NS) for a in range(blocks)], axis=0)
+        op = jnp.concatenate([op_ref[a, k].reshape(2 * rows, NS) for a in range(blocks)], axis=0)
         product = jnp.dot(op, spectra, preferred_element_type=jnp.float32).reshape(blocks, 2, rows, 2 * S)
         stacked = []
         for a in range(blocks):
             real = product[a, 0, :, :S] - product[a, 1, :, S:]
             imag = product[a, 0, :, S:] + product[a, 1, :, :S]
-            real = (data_ref[2 * a + k, 0].astype(jnp.float32) - real).astype(jnp.bfloat16)
-            imag = (data_ref[2 * a + k, 1].astype(jnp.float32) - imag).astype(jnp.bfloat16)
-            residual_ref[2 * a + k, 0] = real
-            residual_ref[2 * a + k, 1] = imag
+            real = (data_refs[a][k, 0].astype(jnp.float32) - real).astype(jnp.bfloat16)
+            imag = (data_refs[a][k, 1].astype(jnp.float32) - imag).astype(jnp.bfloat16)
+            if returned:
+                residual_refs[a][k, 0] = real
+                residual_refs[a][k, 1] = imag
             wide_real = real.astype(jnp.float32)
             wide_imag = imag.astype(jnp.float32)
             residual_sq += jnp.sum(wide_real * wide_real + wide_imag * wide_imag, keepdims=True)
@@ -131,19 +158,70 @@
     return lows
 
 
-def middle_kernel(owners, packed_ref, table_ref, primaries_ref, shrinkage_ref, new_ref, spectra_ref, wide_ref, rows_ref):
+def middle_kernel(owners, rcv_parts, packed_ref, base_ref, primaries_ref, shrinkage_ref, new_ref, spectra_ref, wide_ref, table_ref, rows_ref):
+    fill_table(base_ref, table_ref, owners, rcv_parts)
     lows = update(owners, packed_ref, table_ref, primaries_ref, shrinkage_ref, wide_ref, new_ref)
     transform(table_ref, jnp.concatenate(lows, axis=0), rows_ref, spectra_ref, owners)
 
 
-def last_kernel(owners, packed_ref, table_ref, primaries_ref, shrinkage_ref, new_ref, wide_ref):
+def last_kernel(owners, rcv_parts, packed_ref, base_ref, primaries_ref, shrinkage_ref, new_ref, wide_ref, table_ref):
+    fill_table(base_ref, table_ref, owners, rcv_parts)
     update(owners, packed_ref, table_ref, primaries_ref, shrinkage_ref, wide_ref, new_ref)
 
 
-def exchange(array, devices, scope):
-    with jax.named_scope(scope):
-        pairs = array.reshape(devices, array.shape[0] // (2 * devices), 2, S)
-        return lax.all_to_all(pairs, ALL, split_axis=0, concat_axis=0, tiled=True).reshape(array.shape)
+def split_kernel(blocks, me_ref, whole_ref, *refs):
+    pieces, sem = refs[:blocks], refs[blocks]
+    copies = [
+        pltpu.make_async_copy(whole_ref.at[pl.ds(2 * (me_ref[0] ^ place), 2)], piece, sem.at[place])
+        for place, piece in enumerate(pieces)
+    ]
+    for copy in copies:
+        copy.start()
+    for copy in copies:
+        copy.wait()
+
+
+def split(whole, me, blocks, space):
+    piece = jax.ShapeDtypeStruct((2,) + whole.shape[1:], whole.dtype)
+    return pl.pallas_call(
+        functools.partial(split_kernel, blocks),
+        out_shape=[piece] * blocks,
+        in_specs=[pl.BlockSpec(memory_space=pltpu.SMEM), pl.BlockSpec(memory_space=pl.ANY)],
+        out_specs=[pl.BlockSpec(memory_space=space)] * blocks,
+        scratch_shapes=[pltpu.SemaphoreType.DMA((blocks,))],
+        compiler_params=pltpu.CompilerParams(vmem_limit_bytes=8 * 2**20),
+    )(me, whole)
+
+
+def join_kernel(blocks, me_ref, *refs):
+    pieces, whole_ref = refs[:blocks], refs[blocks]
+    for place, piece in enumerate(pieces):
+        whole_ref[pl.ds(2 * (me_ref[0] ^ place), 2)] = piece[...]
+
+
+def join(pieces, me):
+    blocks = len(pieces)
+    shape = pieces[0].shape
+    return pl.pallas_call(
+        functools.partial(join_kernel, blocks),
+        out_shape=jax.ShapeDtypeStruct((2 * blocks,) + shape[1:], pieces[0].dtype),
+        in_specs=[pl.BlockSpec(memory_space=pltpu.SMEM)] + [pl.BlockSpec(memory_space=pltpu.VMEM)] * blocks,
+        out_specs=pl.BlockSpec(memory_space=pltpu.VMEM),
+        compiler_params=pltpu.CompilerParams(vmem_limit_bytes=8 * 2**20),
+    )(me, *pieces)
+
+
+def trade(pieces):
+    blocks = len(pieces)
+    return [pieces[0]] + [
+        lax.ppermute(pieces[place], "rcv", [(source, source ^ place) for source in range(blocks)])
+        for place in range(1, blocks)
+    ]
+
+
+def exchange(array, devices):
+    pairs = array.reshape(devices, array.shape[0] // (2 * devices), 2, S)
+    return lax.all_to_all(pairs, ALL, split_axis=0, concat_axis=0, tiled=True).reshape(array.shape)
 
 
 def local(freq_parts, rcv_parts, primaries_start, surface_operator, data_spectra, shrinkage):
@@ -151,44 +229,51 @@
     rows = R // rcv_parts
     half, wide = (devices * 2 * PARTS, S), (devices * 2 * WIDE, S)
     bf16, f32 = jnp.bfloat16, jnp.float32
-    table = transform_table(freq_parts, rcv_parts)
+    rows_half, rows_wide = pltpu.VMEM(half, f32), pltpu.VMEM(wide, f32)
+    table = pltpu.VMEM((2 * NF, T_SIZE), bf16)
+    base = table_base(freq_parts, rcv_parts)
     shrinkage = shrinkage.reshape(1, S)
-    with jax.named_scope("operator"):
-        op = lax.all_to_all(surface_operator, "rcv", split_axis=0, concat_axis=0, tiled=True)
-    with jax.named_scope("recorded"):
-        data = lax.all_to_all(data_spectra.transpose(1, 2, 0, 3), "rcv", split_axis=0, concat_axis=0, tiled=True)
+    me = lax.axis_index("rcv").astype(jnp.int32).reshape(1)
+    op = trade(split(surface_operator, me, rcv_parts, pl.ANY))
+    data = trade(split(data_spectra.transpose(1, 2, 0, 3), me, rcv_parts, pltpu.VMEM))
     primaries = primaries_start
     spectra = call(
-        functools.partial(start_kernel, devices),
+        functools.partial(start_kernel, devices, rcv_parts),
         jax.ShapeDtypeStruct(half, bf16),
-        [half],
-        (primaries, table),
+        [rows_half, table],
+        (primaries, base),
         2 * 1024 * 1024 * 256,
     )
     for iteration in range(ITERS):
-        points = exchange(spectra, devices, f"spectra{iteration}")
-        packed, residual = call(
-            functools.partial(physics_kernel, rcv_parts),
-            (jax.ShapeDtypeStruct(wide, bf16), jax.ShapeDtypeStruct((2 * rcv_parts, 2, rows, S), bf16)),
-            [half, wide],
-            (points, op, data),
+        points = exchange(spectra, devices)
+        returned = rcv_parts if iteration + 1 == ITERS else 0
+        packed, *residual = call(
+            functools.partial(physics_kernel, rcv_parts, returned),
+            [jax.ShapeDtypeStruct(wide, bf16)] + [jax.ShapeDtypeStruct((2, 2, rows, S), bf16)] * returned,
+            [
+                pltpu.VMEM((rcv_parts, 2, 2, rows, NS), bf16),
+                rows_half,
+                rows_wide,
+                pltpu.SemaphoreType.DMA((rcv_parts,)),
+            ],
+            (points, *op, *data),
             4 * 2 * 768 * 512 * 256,
-        )
-        packed = exchange(packed, devices, f"direction{iteration}")
+            [pltpu.VMEM] + [pl.ANY] * rcv_parts + [pltpu.VMEM] * rcv_parts,
+        )
+        packed = exchange(packed, devices)
         shape = jax.ShapeDtypeStruct(primaries.shape, f32)
-        inputs = (packed, table, primaries, shrinkage)
+        inputs = (packed, base, primaries, shrinkage)
         if iteration + 1 < ITERS:
             primaries, spectra = call(
-                functools.partial(middle_kernel, devices),
+                functools.partial(middle_kernel, devices, rcv_parts),
                 (shape, jax.ShapeDtypeStruct(half, bf16)),
-                [wide, half],
+                [rows_wide, table, rows_half],
                 inputs,
                 4 * 1024 * 1024 * 256,
             )
         else:
-            primaries = call(functools.partial(last_kernel, devices), shape, [wide], inputs, 2 * 1024 * 1024 * 256)
-    with jax.named_scope("returned"):
-        residual = lax.all_to_all(residual, "rcv", split_axis=0, concat_axis=0, tiled=True)
+            primaries = call(functools.partial(last_kernel, devices, rcv_parts), shape, [rows_wide, table], inputs, 2 * 1024 * 1024 * 256)
+    residual = join(trade(residual), me)
     return (primaries, residual.transpose(2, 0, 1, 3))
 
 

time: 179 us -> 174 us (0.972)
  blocking collectives: 124 us -> 59 us
  starting transfers between devices: 12.4 us -> 51.3 us
  Pallas kernels: 8.73 us -> 17.8 us
  waiting for transfers between devices: 27.3 us -> 35.3 us
  local copies, waits for them, and re-layouts: 5.87 us -> 9.26 us
    all_to_all x2 -> x0, blocking collectives: 36.7 us -> none  [the longest x1 24.6 us: local(): lax.all_to_all(surface_operator, 'rcv', split_axis=0, concat_axis=0, tile...]
    ppermute x0 -> x21, waiting for transfers between devices: none -> 30.8 us  [trade(): lax.ppermute(pieces[place], 'rcv', [(source, source ^ place) for source i...]
    ppermute x0 -> x21, starting transfers between devices: none -> 29.2 us  [trade(): lax.ppermute(pieces[place], 'rcv', [(source, source ^ place) for source i...]
    all_to_all x3 -> x2, blocking collectives: 87.2 us -> 59 us  [exchange(): lax.all_to_all(pairs, ALL, split_axis=0, concat_axis=0, tiled=True)]
    all_to_all x1 -> x2, waiting for transfers between devices: 22 us -> 4.56 us  [exchange(): lax.all_to_all(pairs, ALL, split_axis=0, concat_axis=0, tiled=True)]
    all_to_all x1 -> x2, starting transfers between devices: 5.89 us -> 22.2 us  [exchange(): lax.all_to_all(pairs, ALL, split_axis=0, concat_axis=0, tiled=True)]
    all_to_all x1 -> x0, starting transfers between devices: 6.56 us -> none  [local(): lax.all_to_all(data_spectra.transpose(1, 2, 0, 3), 'rcv', split_axis=0, c...]
    pallas_call x5, Pallas kernels: 8.73 us -> 15.1 us  [call(): pl.pallas_call(kernel, out_shape=out_shape, in_specs=[pl.BlockSpec(memory...]
  transfers between devices with their start and end apart: 2 -> 23, of which waited for: 2 -> 12; matrix products, arithmetic and copies ran while one was open for 1% -> 1% of each run, Pallas kernels for 0% -> 2%
where the time goes in v3:
time: 174 us
  blocking collectives  59 us (34%)
  starting transfers between devices  51.3 us (29%)
  waiting for transfers between devices  35.3 us (20%)
  Pallas kernels  17.8 us (10%)
  local copies, waits for them, and re-layouts  9.26 us (5%)
    all_to_all x2, blocking collectives, exchange(): lax.all_to_all(pairs, ALL, split_axis=0, concat_axis=0, tiled=True)  59 us
    ppermute x21, waiting for transfers between devices, trade(): lax.ppermute(pieces[place], 'rcv', [(source, source ^ place) for source i...  30.8 us
    ppermute x21, starting transfers between devices, trade(): lax.ppermute(pieces[place], 'rcv', [(source, source ^ place) for source i...  29.2 us
    all_to_all x2, starting transfers between devices, exchange(): lax.all_to_all(pairs, ALL, split_axis=0, concat_axis=0, tiled=True)  22.2 us
    pallas_call x5, Pallas kernels, call(): pl.pallas_call(kernel, out_shape=out_shape, in_specs=[pl.BlockSpec(memory...  15.1 us
    unnamed x56, local copies, waits for them, and re-layouts  9.26 us
    all_to_all x2, waiting for transfers between devices, exchange(): lax.all_to_all(pairs, ALL, split_axis=0, concat_axis=0, tiled=True)  4.56 us
  transfers between devices with their start and end apart: 23, of which 12 were waited for; matrix products, arithmetic and copies ran while one was open for 1% of the time, Pallas kernels for 2%

profile of v3, /device:TPU:1, one launch (start us, length us, event | category | flops | bytes accessed | tf_op | source)
XLA Modules:
  0.0 173.6 jit_solution(11823948977059661475)
XLA Ops:
  0.6 1.0 copy-done
  1.7 1.2 copy-done.3
  2.9 1.8 %shard_map.68 = bf16[2048,128]{1,0:T(8,128)(2,1)} custom-call(f32[2,1024,128]{2,1,0:T(8,128)S(1)} %copy-done.3, f32[2,512,128]{2,1,0:T(8,128)S(1)} %copy-done), custom_call_target="tpu_custom_call" | custom-call | flops 536870912 | bytes 4194304 | tf_op jit(solution)/shard_map/pallas_call | solution.py:49
  4.7 15.6 %all-to-all-start = ((bf16[256,4,2,128]{3,2,1,0:T(2,128)(2,1)}), bf16[256,4,2,128]{3,2,1,0:T(2,128)(2,1)S(1)}, u32[]{:S(2)}, u32[]{:S(2)}) async-start(bf16[256,4,2,128]{3,2,1,0:T(2,128)(2,1)} %bitcast), calls=%async_computation | async-start | bytes 1048576 | tf_op jit(solution)/shard_map/all_to_all | solution.py:224
  20.3 2.1 %shard_map.69 = (bf16[2,2,48,512]{3,2,1,0:T(8,128)(2,1)S(1)}, bf16[2,2,48,512]{3,2,1,0:T(8,128)(2,1)S(1)}, bf16[2,2,48,512]{3,2,1,0:T(8,128)(2,1)S(1)}, bf16[2,2...) custom-call(s32[1]{0:T(128)} %bitcast.2.me_ref, ...), custom_call_target="tpu_custom_call" | custom-call | tf_op jit(solution)/shard_map/pallas_call | solution.py:186
  22.5 2.2 %collective-permute-start = (bf16[2,2,48,512]{3,2,1,0:T(8,128)(2,1)S(1)}, bf16[2,2,48,512]{3,2,1,0:T(8,128)(2,1)S(1)}, u32[]{:S(2)}, u32[]{:S(2)}) collective-permute-start(bf16[2,2,48,512]{3,2,1,0:T(8,128)(2,1)S(1)} %get-tuple-element.30), channel_id=1, source_target_pairs={{0,1},{1,0},{2,3},{3,2},{4,5},{5,4},{6,7},{7,6},{8,9},{9,8},{10,11... | collective-permute-start | bytes 589832 | tf_op jit(solution)/shard_map/ppermute | solution.py:217
  25.7 1.7 collective-permute-start.8
  27.7 2.0 %collective-permute-start.10 = (bf16[2,2,48,128]{3,2,1,0:T(8,128)(2,1)S(1)}, bf16[2,2,48,128]{3,2,1,0:T(8,128)(2,1)S(1)}, u32[]{:S(2)}, u32[]{:S(2)}) collective-permute-start(bf16[2,2,48,128]{3,2,1,0:T(8,128)(2,1)S(1)} %get-tuple-element.41), channel_id=1, source_target_pairs={{0,4},{1,5},{2,6},{3,7},{4,0},{5,1},{6,2},{7,3},{8,12},{9,13},{10,... | collective-permute-start | bytes 147464 | tf_op jit(solution)/shard_map/ppermute | solution.py:217
  29.7 6.0 %collective-permute-done.8.refs_10_ = bf16[2,2,48,128]{3,2,1,0:T(8,128)(2,1)S(1)} collective-permute-done((bf16[2,2,48,128]{3,2,1,0:T(8,128)(2,1)S(1)}, bf16[2,2,48,128]{3,2,1,0:T(8,128)(2,1)S(1)}, u32[]{:S(2)}, u32[]{:S(2)}) %collective-permute-start.8) | collective-permute-done | bytes 49184 | tf_op jit(solution)/shard_map/ppermute | solution.py:217
  35.8 2.5 %collective-permute-start.11 = (bf16[2,2,48,128]{3,2,1,0:T(8,128)(2,1)S(1)}, bf16[2,2,48,128]{3,2,1,0:T(8,128)(2,1)S(1)}, u32[]{:S(2)}, u32[]{:S(2)}) collective-permute-start(bf16[2,2,48,128]{3,2,1,0:T(8,128)(2,1)S(1)} %get-tuple-element.42), channel_id=1, source_target_pairs={{0,5},{1,4},{2,7},{3,6},{4,1},{5,0},{6,3},{7,2},{8,13},{9,12},{10,... | collective-permute-start | bytes 147464 | tf_op jit(solution)/shard_map/ppermute | solution.py:217
  38.2 0.9 collective-permute-start.12
  39.2 2.2 %collective-permute-start.13 = (bf16[2,2,48,128]{3,2,1,0:T(8,128)(2,1)S(1)}, bf16[2,2,48,128]{3,2,1,0:T(8,128)(2,1)S(1)}, u32[]{:S(2)}, u32[]{:S(2)}) collective-permute-start(bf16[2,2,48,128]{3,2,1,0:T(8,128)(2,1)S(1)} %get-tuple-element.44), channel_id=1, source_target_pairs={{0,7},{1,6},{2,5},{3,4},{4,3},{5,2},{6,1},{7,0},{8,15},{9,14},{10,... | collective-permute-start | bytes 147464 | tf_op jit(solution)/shard_map/ppermute | solution.py:217
  41.4 0.9 collective-permute-start.2
  42.6 1.7 collective-permute-start.3
  44.7 1.5 collective-permute-start.4
  46.2 1.5 collective-permute-start.5
  47.7 1.2 collective-permute-start.6
  48.9 5.1 %collective-permute-done.3.refs_4_ = bf16[2,2,48,512]{3,2,1,0:T(8,128)(2,1)S(1)} collective-permute-done((bf16[2,2,48,512]{3,2,1,0:T(8,128)(2,1)S(1)}, bf16[2,2,48,512]{3,2,1,0:T(8,128)(2,1)S(1)}, u32[]{:S(2)}, u32[]{:S(2)}) %collective-permute-start.3) | collective-permute-done | bytes 196640 | tf_op jit(solution)/shard_map/ppermute | solution.py:217
  54.0 4.2 %collective-permute-done.4.refs_5_ = bf16[2,2,48,512]{3,2,1,0:T(8,128)(2,1)S(1)} collective-permute-done((bf16[2,2,48,512]{3,2,1,0:T(8,128)(2,1)S(1)}, bf16[2,2,48,512]{3,2,1,0:T(8,128)(2,1)S(1)}, u32[]{:S(2)}, u32[]{:S(2)}) %collective-permute-start.4) | collective-permute-done | bytes 196640 | tf_op jit(solution)/shard_map/ppermute | solution.py:217
  58.2 4.2 %collective-permute-done.5.refs_6_ = bf16[2,2,48,512]{3,2,1,0:T(8,128)(2,1)S(1)} collective-permute-done((bf16[2,2,48,512]{3,2,1,0:T(8,128)(2,1)S(1)}, bf16[2,2,48,512]{3,2,1,0:T(8,128)(2,1)S(1)}, u32[]{:S(2)}, u32[]{:S(2)}) %collective-permute-start.5) | collective-permute-done | bytes 196640 | tf_op jit(solution)/shard_map/ppermute | solution.py:217
  62.4 4.2 %collective-permute-done.6.refs_7_ = bf16[2,2,48,512]{3,2,1,0:T(8,128)(2,1)S(1)} collective-permute-done((bf16[2,2,48,512]{3,2,1,0:T(8,128)(2,1)S(1)}, bf16[2,2,48,512]{3,2,1,0:T(8,128)(2,1)S(1)}, u32[]{:S(2)}, u32[]{:S(2)}) %collective-permute-start.6) | collective-permute-done | bytes 196640 | tf_op jit(solution)/shard_map/ppermute | solution.py:217
  66.6 3.8 %shard_map.71 = bf16[2560,128]{1,0:T(8,128)(2,1)S(1)} custom-call(bf16[2048,128]{1,0:T(8,128)(2,1)S(1)} %bitcast.16, bf16[2,2,48,512]{3,2,1,0:T(8,128)(2,1)S(1)} %get-tuple-element.29.refs_0_, bf16[2,2,48,512]{3,2,1,0:T(8,128)(2,1)S(1)} %collective-permute-done.refs_1_, bf16[2,2,48,512]{3,2,1,0:T(8,128)(2,1)S(1)} %collective-permute-done.1.refs_2_, ...), custom_call_target="tpu_custom_call" | custom-call | flops 805306368 | bytes 4194304 | tf_op jit(solution)/shard_map/pallas_call | solution.py:49
  70.5 33.1 %all_to_all.20 = bf16[256,5,2,128]{3,2,1,0:T(2,128)(2,1)S(1)} all-to-all(bf16[256,5,2,128]{3,2,1,0:T(2,128)(2,1)S(1)} %bitcast.15), channel_id=1, replica_groups=mesh['freq'=32,'rcv'=8] {'rcv','freq'}, dimensions={0} | all-to-all | bytes 1310720 | tf_op jit(solution)/shard_map/all_to_all | solution.py:224
  103.7 2.1 %shard_map.72 = (f32[2,1024,128]{2,1,0:T(8,128)S(1)}, bf16[2048,128]{1,0:T(8,128)(2,1)S(1)}) custom-call(bf16[2560,128]{1,0:T(8,128)(2,1)S(1)} %bitcast.19, f32[2,512,128]{2,1,0:T(8,128)S(1)} %copy-done.1, f32[2,1024,128]{2,1,0:T(8,128)S(1)} %copy-done.4, f32[1,128]{1,0:T(1,128)S(1)} %bitcast.22), custom_call_target="tpu_custom_call" | custom-call | flops 1073741824 | bytes 4194304 | tf_op jit(solution)/shard_map/pallas_call | solution.py:49
  105.8 25.9 %all_to_all.21 = bf16[256,4,2,128]{3,2,1,0:T(2,128)(2,1)S(1)} all-to-all(bf16[256,4,2,128]{3,2,1,0:T(2,128)(2,1)S(1)} %bitcast.21), channel_id=1, replica_groups=mesh['freq'=32,'rcv'=8] {'rcv','freq'}, dimensions={0} | all-to-all | bytes 1048576 | tf_op jit(solution)/shard_map/all_to_all | solution.py:224
  131.7 5.0 %shard_map.73 = (bf16[2560,128]{1,0:T(8,128)(2,1)}, bf16[2,2,48,128]{3,2,1,0:T(8,128)(2,1)S(1)}, bf16[2,2,48,128]{3,2,1,0:T(8,128)(2,1)S(1)}, bf16[2,2,48,128]{3...) custom-call(bf16[2048,128]{1,0:T(8,128)(2,1)S(1)} %bitcast.20, ...), custom_call_target="tpu_custom_call" | custom-call | flops 805306368 | bytes 4194304 | tf_op jit(solution)/shard_map/pallas_call | solution.py:49
  136.8 0.6 copy-done.15
  137.4 0.6 copy-done.19
  138.0 0.6 copy-done.20
  138.6 0.6 copy-done.21
  139.2 0.6 copy-done.22
  139.9 0.6 copy-done.23
  140.5 0.6 copy-done.24
  141.1 0.6 copy-done.25
  141.7 6.5 %all-to-all-start.3 = ((bf16[256,5,2,128]{3,2,1,0:T(2,128)(2,1)}), bf16[256,5,2,128]{3,2,1,0:T(2,128)(2,1)S(1)}, u32[]{:S(2)}, u32[]{:S(2)}) async-start(bf16[256,5,2,128]{3,2,1,0:T(2,128)(2,1)} %bitcast.9), calls=%async_computation.3 | async-start | bytes 1310720 | tf_op jit(solution)/shard_map/all_to_all | solution.py:224
  148.2 2.4 %collective-permute-start.14 = (bf16[2,2,48,128]{3,2,1,0:T(8,128)(2,1)}, bf16[2,2,48,128]{3,2,1,0:T(8,128)(2,1)S(1)}, u32[]{:S(2)}, u32[]{:S(2)}) collective-permute-start(bf16[2,2,48,128]{3,2,1,0:T(8,128)(2,1)} %copy-done.25), channel_id=1, source_target_pairs={{0,1},{1,0},{2,3},{3,2},{4,5},{5,4},{6,7},{7,6},{8,9},{9,8},{10,11... | collective-permute-start | bytes 147464 | tf_op jit(solution)/shard_map/ppermute | solution.py:217
  150.6 1.7 collective-permute-start.16
  152.3 1.1 collective-permute-start.17
  153.4 2.1 %collective-permute-start.18 = (bf16[2,2,48,128]{3,2,1,0:T(8,128)(2,1)}, bf16[2,2,48,128]{3,2,1,0:T(8,128)(2,1)S(1)}, u32[]{:S(2)}, u32[]{:S(2)}) collective-permute-start(bf16[2,2,48,128]{3,2,1,0:T(8,128)(2,1)} %copy-done.21), channel_id=1, source_target_pairs={{0,5},{1,4},{2,7},{3,6},{4,1},{5,0},{6,3},{7,2},{8,13},{9,12},{10,... | collective-permute-start | bytes 147464 | tf_op jit(solution)/shard_map/ppermute | solution.py:217
  155.6 0.9 collective-permute-start.19
  156.5 2.1 %collective-permute-start.20 = (bf16[2,2,48,128]{3,2,1,0:T(8,128)(2,1)}, bf16[2,2,48,128]{3,2,1,0:T(8,128)(2,1)S(1)}, u32[]{:S(2)}, u32[]{:S(2)}) collective-permute-start(bf16[2,2,48,128]{3,2,1,0:T(8,128)(2,1)} %copy-done.19), channel_id=1, source_target_pairs={{0,7},{1,6},{2,5},{3,4},{4,3},{5,2},{6,1},{7,0},{8,15},{9,14},{10,... | collective-permute-start | bytes 147464 | tf_op jit(solution)/shard_map/ppermute | solution.py:217
  158.5 2.4 %collective-permute-done.18.refs_5_ = bf16[2,2,48,128]{3,2,1,0:T(8,128)(2,1)S(1)} collective-permute-done((bf16[2,2,48,128]{3,2,1,0:T(8,128)(2,1)}, bf16[2,2,48,128]{3,2,1,0:T(8,128)(2,1)S(1)}, u32[]{:S(2)}, u32[]{:S(2)}) %collective-permute-start.18) | collective-permute-done | bytes 49184 | tf_op jit(solution)/shard_map/ppermute | solution.py:217
  160.9 1.9 %collective-permute-done.19.refs_6_ = bf16[2,2,48,128]{3,2,1,0:T(8,128)(2,1)S(1)} collective-permute-done((bf16[2,2,48,128]{3,2,1,0:T(8,128)(2,1)}, bf16[2,2,48,128]{3,2,1,0:T(8,128)(2,1)S(1)}, u32[]{:S(2)}, u32[]{:S(2)}) %collective-permute-start.19) | collective-permute-done | bytes 49184 | tf_op jit(solution)/shard_map/ppermute | solution.py:217
  162.8 2.0 %collective-permute-done.20.refs_7_ = bf16[2,2,48,128]{3,2,1,0:T(8,128)(2,1)S(1)} collective-permute-done((bf16[2,2,48,128]{3,2,1,0:T(8,128)(2,1)}, bf16[2,2,48,128]{3,2,1,0:T(8,128)(2,1)S(1)}, u32[]{:S(2)}, u32[]{:S(2)}) %collective-permute-start.20) | collective-permute-done | bytes 49184 | tf_op jit(solution)/shard_map/ppermute | solution.py:217
  164.8 0.8 copy-done.16
  165.7 1.1 copy.8
  166.7 4.6 %all-to-all-done.3 = bf16[256,5,2,128]{3,2,1,0:T(2,128)(2,1)S(1)} async-done(((bf16[256,5,2,128]{3,2,1,0:T(2,128)(2,1)}), bf16[256,5,2,128]{3,2,1,0:T(2,128)(2,1)S(1)}, u32[]{:S(2)}, u32[]{:S(2)}) %all-to-all-start.3) | async-done | bytes 655392 | tf_op jit(solution)/shard_map/all_to_all | solution.py:224
  171.3 2.3 %shard_map.74 = f32[2,1024,128]{2,1,0:T(8,128)} custom-call(bf16[2560,128]{1,0:T(8,128)(2,1)S(1)} %bitcast.14, f32[2,512,128]{2,1,0:T(8,128)S(1)} %copy-done.1, f32[2,1024,128]{2,1,0:T(8,128)S(1)} %get-tuple-element.47.primaries_ref, f32[1,128]{1,0:T(1,128)S(1)} %bitcast.23), custom_call_target="tpu_custom_call" | custom-call | flops 536870912 | bytes 4194304 | tf_op jit(solution)/shard_map/pallas_call | solution.py:49
  (64 shorter events, 2.1 us)
Async XLA Ops:
  0.6 1.0 copy-start
  1.7 1.2 copy-start.3
  2.9 17.4 %copy-start.2 = (bf16[16,2,48,512]{3,2,1,0:T(8,128)(2,1)S(1)}, bf16[16,2,48,512]{3,2,1,0:T(8,128)(2,1)}, u32[]{:S(2)}) copy-start(bf16[16,2,48,512]{3,2,1,0:T(8,128)(2,1)} %whole_ref.1) | copy-start | bytes 4718596
  4.7 20.0 %copy-start.26 = (bf16[48,16,2,128]{3,2,1,0:T(2,128)(2,1)S(1)}, bf16[48,16,2,128]{3,2,1,0:T(2,128)(2,1)}, u32[]{:S(2)}) copy-start(bf16[48,16,2,128]{3,2,1,0:T(2,128)(2,1)} %param.7) | copy-start | bytes 1179652
  4.7 62.0 %all-to-all-start = ((bf16[256,4,2,128]{3,2,1,0:T(2,128)(2,1)}), bf16[256,4,2,128]{3,2,1,0:T(2,128)(2,1)S(1)}, u32[]{:S(2)}, u32[]{:S(2)}) async-start(bf16[256,4,2,128]{3,2,1,0:T(2,128)(2,1)} %bitcast), calls=%async_computation | async-start | bytes 1048576 | tf_op jit(solution)/shard_map/all_to_all | solution.py:224
  22.5 23.7 %collective-permute-start = (bf16[2,2,48,512]{3,2,1,0:T(8,128)(2,1)S(1)}, bf16[2,2,48,512]{3,2,1,0:T(8,128)(2,1)S(1)}, u32[]{:S(2)}, u32[]{:S(2)}) collective-permute-start(bf16[2,2,48,512]{3,2,1,0:T(8,128)(2,1)S(1)} %get-tuple-element.30), channel_id=1, source_target_pairs={{0,1},{1,0},{2,3},{3,2},{4,5},{5,4},{6,7},{7,6},{8,9},{9,8},{10,11... | collective-permute-start | bytes 589832 | tf_op jit(solution)/shard_map/ppermute | solution.py:217
  24.7 23.0 %collective-permute-start.1 = (bf16[2,2,48,512]{3,2,1,0:T(8,128)(2,1)S(1)}, bf16[2,2,48,512]{3,2,1,0:T(8,128)(2,1)S(1)}, u32[]{:S(2)}, u32[]{:S(2)}) collective-permute-start(bf16[2,2,48,512]{3,2,1,0:T(8,128)(2,1)S(1)} %get-tuple-element.31), channel_id=1, source_target_pairs={{0,2},{1,3},{2,0},{3,1},{4,6},{5,7},{6,4},{7,5},{8,10},{9,11},{10,... | collective-permute-start | bytes 589832 | tf_op jit(solution)/shard_map/ppermute | solution.py:217
  25.5 2.2 %collective-permute-start.7 = (bf16[2,2,48,128]{3,2,1,0:T(8,128)(2,1)S(1)}, bf16[2,2,48,128]{3,2,1,0:T(8,128)(2,1)S(1)}, u32[]{:S(2)}, u32[]{:S(2)}) collective-permute-start(bf16[2,2,48,128]{3,2,1,0:T(8,128)(2,1)S(1)} %get-tuple-element.38), channel_id=1, source_target_pairs={{0,1},{1,0},{2,3},{3,2},{4,5},{5,4},{6,7},{7,6},{8,9},{9,8},{10,11... | collective-permute-start | bytes 147464 | tf_op jit(solution)/shard_map/ppermute | solution.py:217
  25.7 10.1 %collective-permute-start.8 = (bf16[2,2,48,128]{3,2,1,0:T(8,128)(2,1)S(1)}, bf16[2,2,48,128]{3,2,1,0:T(8,128)(2,1)S(1)}, u32[]{:S(2)}, u32[]{:S(2)}) collective-permute-start(bf16[2,2,48,128]{3,2,1,0:T(8,128)(2,1)S(1)} %get-tuple-element.39), channel_id=1, source_target_pairs={{0,2},{1,3},{2,0},{3,1},{4,6},{5,7},{6,4},{7,5},{8,10},{9,11},{10,... | collective-permute-start | bytes 147464 | tf_op jit(solution)/shard_map/ppermute | solution.py:217
  27.4 10.8 %collective-permute-start.9 = (bf16[2,2,48,128]{3,2,1,0:T(8,128)(2,1)S(1)}, bf16[2,2,48,128]{3,2,1,0:T(8,128)(2,1)S(1)}, u32[]{:S(2)}, u32[]{:S(2)}) collective-permute-start(bf16[2,2,48,128]{3,2,1,0:T(8,128)(2,1)S(1)} %get-tuple-element.40), channel_id=1, source_target_pairs={{0,3},{1,2},{2,1},{3,0},{4,7},{5,6},{6,5},{7,4},{8,11},{9,10},{10,... | collective-permute-start | bytes 147464 | tf_op jit(solution)/shard_map/ppermute | solution.py:217
  27.7 11.5 %collective-permute-start.10 = (bf16[2,2,48,128]{3,2,1,0:T(8,128)(2,1)S(1)}, bf16[2,2,48,128]{3,2,1,0:T(8,128)(2,1)S(1)}, u32[]{:S(2)}, u32[]{:S(2)}) collective-permute-start(bf16[2,2,48,128]{3,2,1,0:T(8,128)(2,1)S(1)} %get-tuple-element.41), channel_id=1, source_target_pairs={{0,4},{1,5},{2,6},{3,7},{4,0},{5,1},{6,2},{7,3},{8,12},{9,13},{10,... | collective-permute-start | bytes 147464 | tf_op jit(solution)/shard_map/ppermute | solution.py:217
  35.8 5.7 %collective-permute-start.11 = (bf16[2,2,48,128]{3,2,1,0:T(8,128)(2,1)S(1)}, bf16[2,2,48,128]{3,2,1,0:T(8,128)(2,1)S(1)}, u32[]{:S(2)}, u32[]{:S(2)}) collective-permute-start(bf16[2,2,48,128]{3,2,1,0:T(8,128)(2,1)S(1)} %get-tuple-element.42), channel_id=1, source_target_pairs={{0,5},{1,4},{2,7},{3,6},{4,1},{5,0},{6,3},{7,2},{8,13},{9,12},{10,... | collective-permute-start | bytes 147464 | tf_op jit(solution)/shard_map/ppermute | solution.py:217
  38.2 4.4 %collective-permute-start.12 = (bf16[2,2,48,128]{3,2,1,0:T(8,128)(2,1)S(1)}, bf16[2,2,48,128]{3,2,1,0:T(8,128)(2,1)S(1)}, u32[]{:S(2)}, u32[]{:S(2)}) collective-permute-start(bf16[2,2,48,128]{3,2,1,0:T(8,128)(2,1)S(1)} %get-tuple-element.43), channel_id=1, source_target_pairs={{0,6},{1,7},{2,4},{3,5},{4,2},{5,3},{6,0},{7,1},{8,14},{9,15},{10,... | collective-permute-start | bytes 147464 | tf_op jit(solution)/shard_map/ppermute | solution.py:217
  39.2 5.4 %collective-permute-start.13 = (bf16[2,2,48,128]{3,2,1,0:T(8,128)(2,1)S(1)}, bf16[2,2,48,128]{3,2,1,0:T(8,128)(2,1)S(1)}, u32[]{:S(2)}, u32[]{:S(2)}) collective-permute-start(bf16[2,2,48,128]{3,2,1,0:T(8,128)(2,1)S(1)} %get-tuple-element.44), channel_id=1, source_target_pairs={{0,7},{1,6},{2,5},{3,4},{4,3},{5,2},{6,1},{7,0},{8,15},{9,14},{10,... | collective-permute-start | bytes 147464 | tf_op jit(solution)/shard_map/ppermute | solution.py:217
  41.4 29.0 %copy-start.9 = (bf16[2,2,48,128]{3,2,1,0:T(8,128)(2,1)}, bf16[2,2,48,128]{3,2,1,0:T(8,128)(2,1)S(1)}, u32[]{:S(2)}) copy-start(bf16[2,2,48,128]{3,2,1,0:T(8,128)(2,1)S(1)} %collective-permute-done.11.refs_13_) | copy-start | bytes 147460
  41.4 7.5 %collective-permute-start.2 = (bf16[2,2,48,512]{3,2,1,0:T(8,128)(2,1)S(1)}, bf16[2,2,48,512]{3,2,1,0:T(8,128)(2,1)S(1)}, u32[]{:S(2)}, u32[]{:S(2)}) collective-permute-start(bf16[2,2,48,512]{3,2,1,0:T(8,128)(2,1)S(1)} %get-tuple-element.32), channel_id=1, source_target_pairs={{0,3},{1,2},{2,1},{3,0},{4,7},{5,6},{6,5},{7,4},{8,11},{9,10},{10,... | collective-permute-start | bytes 589832 | tf_op jit(solution)/shard_map/ppermute | solution.py:217
  42.6 27.8 %copy-start.11 = (bf16[2,2,48,128]{3,2,1,0:T(8,128)(2,1)}, bf16[2,2,48,128]{3,2,1,0:T(8,128)(2,1)S(1)}, u32[]{:S(2)}) copy-start(bf16[2,2,48,128]{3,2,1,0:T(8,128)(2,1)S(1)} %collective-permute-done.12.refs_14_) | copy-start | bytes 147460
  42.6 11.3 %collective-permute-start.3 = (bf16[2,2,48,512]{3,2,1,0:T(8,128)(2,1)S(1)}, bf16[2,2,48,512]{3,2,1,0:T(8,128)(2,1)S(1)}, u32[]{:S(2)}, u32[]{:S(2)}) collective-permute-start(bf16[2,2,48,512]{3,2,1,0:T(8,128)(2,1)S(1)} %get-tuple-element.33), channel_id=1, source_target_pairs={{0,4},{1,5},{2,6},{3,7},{4,0},{5,1},{6,2},{7,3},{8,12},{9,13},{10,... | collective-permute-start | bytes 589832 | tf_op jit(solution)/shard_map/ppermute | solution.py:217
  44.7 25.8 %copy-start.13 = (bf16[2,2,48,128]{3,2,1,0:T(8,128)(2,1)}, bf16[2,2,48,128]{3,2,1,0:T(8,128)(2,1)S(1)}, u32[]{:S(2)}) copy-start(bf16[2,2,48,128]{3,2,1,0:T(8,128)(2,1)S(1)} %collective-permute-done.13.refs_15_) | copy-start | bytes 147460
  44.7 13.5 %collective-permute-start.4 = (bf16[2,2,48,512]{3,2,1,0:T(8,128)(2,1)S(1)}, bf16[2,2,48,512]{3,2,1,0:T(8,128)(2,1)S(1)}, u32[]{:S(2)}, u32[]{:S(2)}) collective-permute-start(bf16[2,2,48,512]{3,2,1,0:T(8,128)(2,1)S(1)} %get-tuple-element.34), channel_id=1, source_target_pairs={{0,5},{1,4},{2,7},{3,6},{4,1},{5,0},{6,3},{7,2},{8,13},{9,12},{10,... | collective-permute-start | bytes 589832 | tf_op jit(solution)/shard_map/ppermute | solution.py:217
  46.2 16.2 %collective-permute-start.5 = (bf16[2,2,48,512]{3,2,1,0:T(8,128)(2,1)S(1)}, bf16[2,2,48,512]{3,2,1,0:T(8,128)(2,1)S(1)}, u32[]{:S(2)}, u32[]{:S(2)}) collective-permute-start(bf16[2,2,48,512]{3,2,1,0:T(8,128)(2,1)S(1)} %get-tuple-element.35), channel_id=1, source_target_pairs={{0,6},{1,7},{2,4},{3,5},{4,2},{5,3},{6,0},{7,1},{8,14},{9,15},{10,... | collective-permute-start | bytes 589832 | tf_op jit(solution)/shard_map/ppermute | solution.py:217
  47.7 18.9 %collective-permute-start.6 = (bf16[2,2,48,512]{3,2,1,0:T(8,128)(2,1)S(1)}, bf16[2,2,48,512]{3,2,1,0:T(8,128)(2,1)S(1)}, u32[]{:S(2)}, u32[]{:S(2)}) collective-permute-start(bf16[2,2,48,512]{3,2,1,0:T(8,128)(2,1)S(1)} %get-tuple-element.36), channel_id=1, source_target_pairs={{0,7},{1,6},{2,5},{3,4},{4,3},{5,2},{6,1},{7,0},{8,15},{9,14},{10,... | collective-permute-start | bytes 589832 | tf_op jit(solution)/shard_map/ppermute | solution.py:217
  62.4 8.1 %copy-start.5 = (bf16[2,2,48,512]{3,2,1,0:T(8,128)(2,1)}, bf16[2,2,48,512]{3,2,1,0:T(8,128)(2,1)S(1)}, u32[]{:S(2)}) copy-start(bf16[2,2,48,512]{3,2,1,0:T(8,128)(2,1)S(1)} %collective-permute-done.5.refs_6_) | copy-start | bytes 589828
  66.6 3.9 %copy-start.7 = (bf16[2,2,48,512]{3,2,1,0:T(8,128)(2,1)}, bf16[2,2,48,512]{3,2,1,0:T(8,128)(2,1)S(1)}, u32[]{:S(2)}) copy-start(bf16[2,2,48,512]{3,2,1,0:T(8,128)(2,1)S(1)} %collective-permute-done.6.refs_7_) | copy-start | bytes 589828
  66.6 37.0 %copy-start.1 = (f32[2,512,128]{2,1,0:T(8,128)S(1)}, f32[2,512,128]{2,1,0:T(8,128)}, u32[]{:S(2)}) copy-start(f32[2,512,128]{2,1,0:T(8,128)} %constant.6.clone.base_ref) | copy-start | bytes 1572868
  66.6 37.0 %copy-start.4 = (f32[2,1024,128]{2,1,0:T(8,128)S(1)}, f32[2,1024,128]{2,1,0:T(8,128)}, u32[]{:S(2)}) copy-start(f32[2,1024,128]{2,1,0:T(8,128)} %primaries_ref.3) | copy-start | bytes 3145732
  66.6 37.0 %copy-start.17 = (f32[128]{0:T(128)S(1)}, f32[128]{0:T(128)}, u32[]{:S(2)}) copy-start(f32[128]{0:T(128)} %param.8) | copy-start | bytes 1540
  103.6 28.1 %copy-start.6 = (bf16[2,2,48,512]{3,2,1,0:T(8,128)(2,1)S(1)}, bf16[2,2,48,512]{3,2,1,0:T(8,128)(2,1)}, u32[]{:S(2)}) copy-start(bf16[2,2,48,512]{3,2,1,0:T(8,128)(2,1)} %copy-done.5) | copy-start | bytes 589828
  103.6 28.1 %copy-start.8 = (bf16[2,2,48,512]{3,2,1,0:T(8,128)(2,1)S(1)}, bf16[2,2,48,512]{3,2,1,0:T(8,128)(2,1)}, u32[]{:S(2)}) copy-start(bf16[2,2,48,512]{3,2,1,0:T(8,128)(2,1)} %copy-done.7) | copy-start | bytes 589828
  103.6 28.1 %copy-start.10 = (bf16[2,2,48,128]{3,2,1,0:T(8,128)(2,1)S(1)}, bf16[2,2,48,128]{3,2,1,0:T(8,128)(2,1)}, u32[]{:S(2)}) copy-start(bf16[2,2,48,128]{3,2,1,0:T(8,128)(2,1)} %copy-done.9) | copy-start | bytes 147460
  103.6 28.1 %copy-start.12 = (bf16[2,2,48,128]{3,2,1,0:T(8,128)(2,1)S(1)}, bf16[2,2,48,128]{3,2,1,0:T(8,128)(2,1)}, u32[]{:S(2)}) copy-start(bf16[2,2,48,128]{3,2,1,0:T(8,128)(2,1)} %copy-done.11) | copy-start | bytes 147460
  103.6 28.1 %copy-start.14 = (bf16[2,2,48,128]{3,2,1,0:T(8,128)(2,1)S(1)}, bf16[2,2,48,128]{3,2,1,0:T(8,128)(2,1)}, u32[]{:S(2)}) copy-start(bf16[2,2,48,128]{3,2,1,0:T(8,128)(2,1)} %copy-done.13) | copy-start | bytes 147460
  136.8 0.6 copy-start.15
  137.4 0.6 copy-start.19
  138.0 0.6 copy-start.20
  139.9 0.6 copy-start.23
  140.5 0.6 copy-start.24
  141.1 0.6 copy-start.25
  141.7 29.6 %copy-start.18 = (f32[128]{0:T(128)S(1)}, f32[128]{0:T(128)}, u32[]{:S(2)}) copy-start(f32[128]{0:T(128)} %param.8) | copy-start | bytes 1540
  141.7 29.6 %all-to-all-start.3 = ((bf16[256,5,2,128]{3,2,1,0:T(2,128)(2,1)}), bf16[256,5,2,128]{3,2,1,0:T(2,128)(2,1)S(1)}, u32[]{:S(2)}, u32[]{:S(2)}) async-start(bf16[256,5,2,128]{3,2,1,0:T(2,128)(2,1)} %bitcast.9), calls=%async_computation.3 | async-start | bytes 1310720 | tf_op jit(solution)/shard_map/all_to_all | solution.py:224
  148.2 7.4 %collective-permute-start.14 = (bf16[2,2,48,128]{3,2,1,0:T(8,128)(2,1)}, bf16[2,2,48,128]{3,2,1,0:T(8,128)(2,1)S(1)}, u32[]{:S(2)}, u32[]{:S(2)}) collective-permute-start(bf16[2,2,48,128]{3,2,1,0:T(8,128)(2,1)} %copy-done.25), channel_id=1, source_target_pairs={{0,1},{1,0},{2,3},{3,2},{4,5},{5,4},{6,7},{7,6},{8,9},{9,8},{10,11... | collective-permute-start | bytes 147464 | tf_op jit(solution)/shard_map/ppermute | solution.py:217
  150.6 5.9 %collective-permute-start.15 = (bf16[2,2,48,128]{3,2,1,0:T(8,128)(2,1)}, bf16[2,2,48,128]{3,2,1,0:T(8,128)(2,1)S(1)}, u32[]{:S(2)}, u32[]{:S(2)}) collective-permute-start(bf16[2,2,48,128]{3,2,1,0:T(8,128)(2,1)} %copy-done.24), channel_id=1, source_target_pairs={{0,2},{1,3},{2,0},{3,1},{4,6},{5,7},{6,4},{7,5},{8,10},{9,11},{10,... | collective-permute-start | bytes 147464 | tf_op jit(solution)/shard_map/ppermute | solution.py:217
  150.6 7.9 %collective-permute-start.16 = (bf16[2,2,48,128]{3,2,1,0:T(8,128)(2,1)}, bf16[2,2,48,128]{3,2,1,0:T(8,128)(2,1)S(1)}, u32[]{:S(2)}, u32[]{:S(2)}) collective-permute-start(bf16[2,2,48,128]{3,2,1,0:T(8,128)(2,1)} %copy-done.23), channel_id=1, source_target_pairs={{0,3},{1,2},{2,1},{3,0},{4,7},{5,6},{6,5},{7,4},{8,11},{9,10},{10,... | collective-permute-start | bytes 147464 | tf_op jit(solution)/shard_map/ppermute | solution.py:217
  152.3 6.2 %collective-permute-start.17 = (bf16[2,2,48,128]{3,2,1,0:T(8,128)(2,1)}, bf16[2,2,48,128]{3,2,1,0:T(8,128)(2,1)S(1)}, u32[]{:S(2)}, u32[]{:S(2)}) collective-permute-start(bf16[2,2,48,128]{3,2,1,0:T(8,128)(2,1)} %copy-done.22), channel_id=1, source_target_pairs={{0,4},{1,5},{2,6},{3,7},{4,0},{5,1},{6,2},{7,3},{8,12},{9,13},{10,... | collective-permute-start | bytes 147464 | tf_op jit(solution)/shard_map/ppermute | solution.py:217
  153.4 7.5 %collective-permute-start.18 = (bf16[2,2,48,128]{3,2,1,0:T(8,128)(2,1)}, bf16[2,2,48,128]{3,2,1,0:T(8,128)(2,1)S(1)}, u32[]{:S(2)}, u32[]{:S(2)}) collective-permute-start(bf16[2,2,48,128]{3,2,1,0:T(8,128)(2,1)} %copy-done.21), channel_id=1, source_target_pairs={{0,5},{1,4},{2,7},{3,6},{4,1},{5,0},{6,3},{7,2},{8,13},{9,12},{10,... | collective-permute-start | bytes 147464 | tf_op jit(solution)/shard_map/ppermute | solution.py:217
  155.6 7.3 %collective-permute-start.19 = (bf16[2,2,48,128]{3,2,1,0:T(8,128)(2,1)}, bf16[2,2,48,128]{3,2,1,0:T(8,128)(2,1)S(1)}, u32[]{:S(2)}, u32[]{:S(2)}) collective-permute-start(bf16[2,2,48,128]{3,2,1,0:T(8,128)(2,1)} %copy-done.20), channel_id=1, source_target_pairs={{0,6},{1,7},{2,4},{3,5},{4,2},{5,3},{6,0},{7,1},{8,14},{9,15},{10,... | collective-permute-start | bytes 147464 | tf_op jit(solution)/shard_map/ppermute | solution.py:217
  156.5 8.4 %collective-permute-start.20 = (bf16[2,2,48,128]{3,2,1,0:T(8,128)(2,1)}, bf16[2,2,48,128]{3,2,1,0:T(8,128)(2,1)S(1)}, u32[]{:S(2)}, u32[]{:S(2)}) collective-permute-start(bf16[2,2,48,128]{3,2,1,0:T(8,128)(2,1)} %copy-done.19), channel_id=1, source_target_pairs={{0,7},{1,6},{2,5},{3,4},{4,3},{5,2},{6,1},{7,0},{8,15},{9,14},{10,... | collective-permute-start | bytes 147464 | tf_op jit(solution)/shard_map/ppermute | solution.py:217
  164.8 0.8 copy-start.16
  (2 other events, 1.2 us)

commit v4 on v3

--- a/solution.py
+++ b/solution.py
@@ -45,12 +45,12 @@
                     table_ref[pl.ds((2 * place + part) * owners + owner * run, run), columns] = value.astype(jnp.bfloat16)
 
 
-def call(kernel, out_shape, scratch, inputs, flops, spaces=None):
+def call(kernel, out_shape, scratch, inputs, flops, spaces=None, out_spaces=None):
     return pl.pallas_call(
         kernel,
         out_shape=out_shape,
         in_specs=[pl.BlockSpec(memory_space=space) for space in spaces or [pltpu.VMEM] * len(inputs)],
-        out_specs=jax.tree.map(lambda _: pl.BlockSpec(memory_space=pltpu.VMEM), out_shape),
+        out_specs=[pl.BlockSpec(memory_space=space) for space in out_spaces or [pltpu.VMEM] * len(out_shape)],
         scratch_shapes=scratch,
         compiler_params=pltpu.CompilerParams(vmem_limit_bytes=32 * 2**20),
         cost_estimate=pl.CostEstimate(flops=flops, bytes_accessed=4 * 2**20, transcendentals=0),
@@ -65,10 +65,32 @@
     spectra_ref[...] = rows_ref[...].astype(jnp.bfloat16)
 
 
-def start_kernel(owners, rcv_parts, primaries_ref, base_ref, spectra_ref, rows_ref, table_ref):
-    fill_table(base_ref, table_ref, owners, rcv_parts)
-    low = jnp.concatenate([primaries_ref[0].astype(jnp.bfloat16), primaries_ref[1].astype(jnp.bfloat16)], axis=1)
+def start_kernel(owners, blocks, me_ref, op_ref, primaries_ref, base_ref, *refs):
+    pieces, spectra_ref = refs[:blocks], refs[blocks]
+    held_ref, traces_ref, angles_ref, table_ref, rows_ref, sem = refs[blocks + 1:]
+    targets = [pieces[0]] + [held_ref.at[place] for place in range(1, blocks)]
+    fetch_base = pltpu.make_async_copy(base_ref, angles_ref, sem.at[2, 0])
+    fetch_traces = pltpu.make_async_copy(primaries_ref, traces_ref, sem.at[2, 1])
+    fetches = [
+        pltpu.make_async_copy(op_ref.at[pl.ds(2 * (me_ref[0] ^ place), 2)], targets[place], sem.at[0, place])
+        for place in range(blocks)
+    ]
+    stores = [pltpu.make_async_copy(targets[place], pieces[place], sem.at[1, place]) for place in range(1, blocks)]
+    fetch_base.start()
+    fetch_traces.start()
+    for fetch in fetches:
+        fetch.start()
+    fetch_base.wait()
+    fill_table(angles_ref, table_ref, owners, blocks)
+    fetch_traces.wait()
+    for place in range(blocks):
+        fetches[place].wait()
+        if place:
+            stores[place - 1].start()
+    low = jnp.concatenate([traces_ref[0].astype(jnp.bfloat16), traces_ref[1].astype(jnp.bfloat16)], axis=1)
     transform(table_ref, low, rows_ref, spectra_ref, owners)
+    for store in stores:
+        store.wait()
 
 
 def split_three(value):
@@ -79,24 +101,20 @@
 
 
 def physics_kernel(blocks, returned, points_ref, *refs):
-    sources, data_refs = refs[:blocks], refs[blocks:2 * blocks]
+    op_refs, data_refs = refs[:blocks], refs[blocks:2 * blocks]
     packed_ref = refs[2 * blocks]
-    residual_refs = refs[2 * blocks + 1:2 * blocks + 1 + returned]
-    op_ref, rows_ref, wide_ref, sem = refs[2 * blocks + 1 + returned:]
-    rows = op_ref.shape[3]
-    copies = [pltpu.make_async_copy(source, op_ref.at[a], sem.at[a]) for a, source in enumerate(sources)]
-    for copy in copies:
-        copy.start()
+    returned_refs = refs[2 * blocks + 1:2 * blocks + 1 + returned]
+    residual_ref, rows_ref, wide_ref, sem = refs[2 * blocks + 1 + returned:]
+    rows = op_refs[0].shape[2]
+    copies = []
     rows_ref[...] = points_ref[...].astype(jnp.float32)
-    for copy in copies:
-        copy.wait()
     residual_sq = jnp.zeros((1, 1), jnp.float32)
     direction_sq = jnp.zeros((1, 1), jnp.float32)
     for k in range(2):
         spectra = jnp.concatenate(
             [rows_ref[pl.ds(2 * k + c, NS, stride=PARTS), :].astype(jnp.bfloat16) for c in range(2)], axis=1
         )
-        op = jnp.concatenate([op_ref[a, k].reshape(2 * rows, NS) for a in range(blocks)], axis=0)
+        op = jnp.concatenate([op_refs[a][k].reshape(2 * rows, NS) for a in range(blocks)], axis=0)
         product = jnp.dot(op, spectra, preferred_element_type=jnp.float32).reshape(blocks, 2, rows, 2 * S)
         stacked = []
         for a in range(blocks):
@@ -105,13 +123,16 @@
             real = (data_refs[a][k, 0].astype(jnp.float32) - real).astype(jnp.bfloat16)
             imag = (data_refs[a][k, 1].astype(jnp.float32) - imag).astype(jnp.bfloat16)
             if returned:
-                residual_refs[a][k, 0] = real
-                residual_refs[a][k, 1] = imag
+                residual_ref[a, k, 0] = real
+                residual_ref[a, k, 1] = imag
             wide_real = real.astype(jnp.float32)
             wide_imag = imag.astype(jnp.float32)
             residual_sq += jnp.sum(wide_real * wide_real + wide_imag * wide_imag, keepdims=True)
             stacked.append(jnp.concatenate([real, imag], axis=1))
             stacked.append(jnp.concatenate([imag, -real], axis=1))
+        for a, out in enumerate(returned_refs):
+            copies.append(pltpu.make_async_copy(residual_ref.at[a, k], out.at[k], sem.at[k, a]))
+            copies[-1].start()
         direction = lax.dot_general(
             op, jnp.concatenate(stacked, axis=0), (((0,), (0,)), ((), ())), preferred_element_type=jnp.float32
         )
@@ -124,9 +145,13 @@
         sums = jnp.where(lane == place, piece, sums)
     wide_ref[pl.ds(PARTS, NS, stride=WIDE), :] = jnp.broadcast_to(sums[:1], (NS, S))
     packed_ref[...] = wide_ref[...].astype(jnp.bfloat16)
-
-
-def update(owners, packed_ref, table_ref, primaries_ref, shrinkage_ref, wide_ref, new_ref):
+    for copy in copies:
+        copy.wait()
+
+
+def update(owners, packed_ref, table_ref, primaries_ref, shrinkage_ref, wide_ref, held_ref, sem):
+    fetch = pltpu.make_async_copy(primaries_ref, held_ref, sem.at[0])
+    fetch.start()
     wide_ref[...] = packed_ref[...].astype(jnp.float32)
     totals = jnp.sum(wide_ref[pl.ds(PARTS, owners, stride=2 * WIDE), :], axis=0, keepdims=True)
     lane = lax.broadcasted_iota(jnp.int32, (1, S), 1)
@@ -144,51 +169,58 @@
     direction = jnp.concatenate(sides, axis=1)
     lows = []
     block = 256
+    fetch.wait()
     for start in range(0, T_SIZE, block):
         change = lax.dot_general(
             table_ref[:, pl.ds(start, block)], direction, (((0,), (0,)), ((), ())), preferred_element_type=jnp.float32
         )
         halves = []
         for point in range(2):
-            moved = primaries_ref[point, pl.ds(start, block), :] + step_size * change[:, point * S:(point + 1) * S]
+            moved = held_ref[point, pl.ds(start, block), :] + step_size * change[:, point * S:(point + 1) * S]
             new = moved - jnp.clip(moved, -threshold, threshold)
-            new_ref[point, pl.ds(start, block), :] = new
+            held_ref[point, pl.ds(start, block), :] = new
             halves.append(new.astype(jnp.bfloat16))
         lows.append(jnp.concatenate(halves, axis=1))
     return lows
 
 
-def middle_kernel(owners, rcv_parts, packed_ref, base_ref, primaries_ref, shrinkage_ref, new_ref, spectra_ref, wide_ref, table_ref, rows_ref):
+def middle_kernel(owners, packed_ref, table_ref, primaries_ref, shrinkage_ref, new_ref, spectra_ref, *scratch):
+    wide_ref, held_ref, rows_ref, sem = scratch
+    lows = update(owners, packed_ref, table_ref, primaries_ref, shrinkage_ref, wide_ref, held_ref, sem)
+    store = pltpu.make_async_copy(held_ref, new_ref, sem.at[1])
+    store.start()
+    transform(table_ref, jnp.concatenate(lows, axis=0), rows_ref, spectra_ref, owners)
+    store.wait()
+
+
+def last_kernel(owners, packed_ref, table_ref, primaries_ref, shrinkage_ref, new_ref, wide_ref, held_ref, sem):
+    update(owners, packed_ref, table_ref, primaries_ref, shrinkage_ref, wide_ref, held_ref, sem)
+    store = pltpu.make_async_copy(held_ref, new_ref, sem.at[1])
+    store.start()
+    store.wait()
+
+
+def table_kernel(owners, rcv_parts, base_ref, first_ref, second_ref, table_ref, sem):
     fill_table(base_ref, table_ref, owners, rcv_parts)
-    lows = update(owners, packed_ref, table_ref, primaries_ref, shrinkage_ref, wide_ref, new_ref)
-    transform(table_ref, jnp.concatenate(lows, axis=0), rows_ref, spectra_ref, owners)
-
-
-def last_kernel(owners, rcv_parts, packed_ref, base_ref, primaries_ref, shrinkage_ref, new_ref, wide_ref, table_ref):
-    fill_table(base_ref, table_ref, owners, rcv_parts)
-    update(owners, packed_ref, table_ref, primaries_ref, shrinkage_ref, wide_ref, new_ref)
-
-
-def split_kernel(blocks, me_ref, whole_ref, *refs):
-    pieces, sem = refs[:blocks], refs[blocks]
-    copies = [
-        pltpu.make_async_copy(whole_ref.at[pl.ds(2 * (me_ref[0] ^ place), 2)], piece, sem.at[place])
-        for place, piece in enumerate(pieces)
-    ]
-    for copy in copies:
-        copy.start()
-    for copy in copies:
-        copy.wait()
-
-
-def split(whole, me, blocks, space):
-    piece = jax.ShapeDtypeStruct((2,) + whole.shape[1:], whole.dtype)
+    stores = [pltpu.make_async_copy(table_ref, whole, sem.at[i]) for i, whole in enumerate((first_ref, second_ref))]
+    for store in stores:
+        store.start()
+    for store in stores:
+        store.wait()
+
+
+def pick_kernel(me_ref, whole_ref, *pieces):
+    for place, piece in enumerate(pieces):
+        piece[...] = whole_ref[pl.ds(2 * (me_ref[0] ^ place), 2)]
+
+
+def pick(whole, me, blocks):
+    shape = (2,) + whole.shape[1:]
     return pl.pallas_call(
-        functools.partial(split_kernel, blocks),
-        out_shape=[piece] * blocks,
-        in_specs=[pl.BlockSpec(memory_space=pltpu.SMEM), pl.BlockSpec(memory_space=pl.ANY)],
-        out_specs=[pl.BlockSpec(memory_space=space)] * blocks,
-        scratch_shapes=[pltpu.SemaphoreType.DMA((blocks,))],
+        pick_kernel,
+        out_shape=[jax.ShapeDtypeStruct(shape, whole.dtype)] * blocks,
+        in_specs=[pl.BlockSpec(memory_space=pltpu.SMEM), pl.BlockSpec(memory_space=pltpu.VMEM)],
+        out_specs=[pl.BlockSpec(memory_space=pltpu.VMEM)] * blocks,
         compiler_params=pltpu.CompilerParams(vmem_limit_bytes=8 * 2**20),
     )(me, whole)
 
@@ -213,10 +245,10 @@
 
 def trade(pieces):
     blocks = len(pieces)
-    return [pieces[0]] + [
-        lax.ppermute(pieces[place], "rcv", [(source, source ^ place) for source in range(blocks)])
-        for place in range(1, blocks)
-    ]
+    traded = [pieces[0]]
+    for place in range(1, blocks):
+        traded.append(lax.ppermute(pieces[place], "rcv", [(source, source ^ place) for source in range(blocks)]))
+    return traded
 
 
 def exchange(array, devices):
@@ -234,45 +266,79 @@
     base = table_base(freq_parts, rcv_parts)
     shrinkage = shrinkage.reshape(1, S)
     me = lax.axis_index("rcv").astype(jnp.int32).reshape(1)
-    op = trade(split(surface_operator, me, rcv_parts, pl.ANY))
-    data = trade(split(data_spectra.transpose(1, 2, 0, 3), me, rcv_parts, pltpu.VMEM))
+    data = trade(pick(data_spectra.transpose(1, 2, 0, 3), me, rcv_parts))
     primaries = primaries_start
-    spectra = call(
+    piece = (2, 2, rows, NS)
+    *op, spectra = call(
         functools.partial(start_kernel, devices, rcv_parts),
-        jax.ShapeDtypeStruct(half, bf16),
-        [rows_half, table],
-        (primaries, base),
+        [jax.ShapeDtypeStruct(piece, bf16)]
+        + [pltpu.HBM(piece, bf16)] * (rcv_parts - 1)
+        + [jax.ShapeDtypeStruct(half, bf16)],
+        [
+            pltpu.VMEM((rcv_parts,) + piece, bf16),
+            pltpu.VMEM(primaries.shape, f32),
+            pltpu.VMEM(base.shape, f32),
+            table,
+            rows_half,
+            pltpu.SemaphoreType.DMA((3, rcv_parts)),
+        ],
+        (me, *(pltpu.with_memory_space_constraint(array, pltpu.HBM) for array in (surface_operator, primaries, base))),
         2 * 1024 * 1024 * 256,
+        [pltpu.SMEM] + [pltpu.HBM] * 3,
+        [pltpu.VMEM] + [pltpu.HBM] * (rcv_parts - 1) + [pltpu.VMEM],
+    )
+    op = trade(op)
+    tables = call(
+        functools.partial(table_kernel, devices, rcv_parts),
+        [pltpu.HBM((2 * NF, T_SIZE), bf16)] * 2,
+        [table, pltpu.SemaphoreType.DMA((2,))],
+        (base,),
+        2**20,
+        None,
+        [pltpu.HBM] * 2,
     )
     for iteration in range(ITERS):
         points = exchange(spectra, devices)
         returned = rcv_parts if iteration + 1 == ITERS else 0
         packed, *residual = call(
             functools.partial(physics_kernel, rcv_parts, returned),
-            [jax.ShapeDtypeStruct(wide, bf16)] + [jax.ShapeDtypeStruct((2, 2, rows, S), bf16)] * returned,
+            [jax.ShapeDtypeStruct(wide, bf16)] + [pltpu.HBM((2, 2, rows, S), bf16)] * returned,
             [
-                pltpu.VMEM((rcv_parts, 2, 2, rows, NS), bf16),
+                pltpu.VMEM((rcv_parts, 2, 2, rows, S), bf16),
                 rows_half,
                 rows_wide,
-                pltpu.SemaphoreType.DMA((rcv_parts,)),
+                pltpu.SemaphoreType.DMA((2, rcv_parts)),
             ],
             (points, *op, *data),
             4 * 2 * 768 * 512 * 256,
-            [pltpu.VMEM] + [pl.ANY] * rcv_parts + [pltpu.VMEM] * rcv_parts,
+            [pltpu.VMEM] * (1 + 2 * rcv_parts),
+            [pltpu.VMEM] + [pltpu.HBM] * returned,
         )
         packed = exchange(packed, devices)
-        shape = jax.ShapeDtypeStruct(primaries.shape, f32)
-        inputs = (packed, base, primaries, shrinkage)
+        shape = pltpu.HBM(primaries.shape, f32)
+        inputs = (packed, tables[iteration], pltpu.with_memory_space_constraint(primaries, pltpu.HBM), shrinkage)
+        spaces = [pltpu.VMEM, pltpu.VMEM, pltpu.HBM, pltpu.VMEM]
+        held = [rows_wide, pltpu.VMEM(primaries.shape, f32)]
         if iteration + 1 < ITERS:
             primaries, spectra = call(
-                functools.partial(middle_kernel, devices, rcv_parts),
-                (shape, jax.ShapeDtypeStruct(half, bf16)),
-                [rows_wide, table, rows_half],
+                functools.partial(middle_kernel, devices),
+                [shape, jax.ShapeDtypeStruct(half, bf16)],
+                held + [rows_half, pltpu.SemaphoreType.DMA((2,))],
                 inputs,
                 4 * 1024 * 1024 * 256,
+                spaces,
+                [pltpu.HBM, pltpu.VMEM],
             )
         else:
-            primaries = call(functools.partial(last_kernel, devices, rcv_parts), shape, [rows_wide, table], inputs, 2 * 1024 * 1024 * 256)
+            primaries, = call(
+                functools.partial(last_kernel, devices),
+                [shape],
+                held + [pltpu.SemaphoreType.DMA((2,))],
+                inputs,
+                2 * 1024 * 1024 * 256,
+                spaces,
+                [pltpu.HBM],
+            )
     residual = join(trade(residual), me)
     return (primaries, residual.transpose(2, 0, 1, 3))
 

time: 174 us -> 168 us (0.966)
  blocking collectives: 59 us -> 25.9 us
  waiting for transfers between devices: 35.3 us -> 56.9 us
  starting transfers between devices: 51.3 us -> 62.4 us
  local copies, waits for them, and re-layouts: 9.26 us -> 3.62 us
    all_to_all x2 -> x1, blocking collectives: 59 us -> 25.9 us  [exchange(): lax.all_to_all(pairs, ALL, split_axis=0, concat_axis=0, tiled=True)]
    all_to_all x2 -> x3, waiting for transfers between devices: 4.56 us -> 25 us  [exchange(): lax.all_to_all(pairs, ALL, split_axis=0, concat_axis=0, tiled=True)]
    all_to_all x2 -> x3, starting transfers between devices: 22.2 us -> 33.5 us  [exchange(): lax.all_to_all(pairs, ALL, split_axis=0, concat_axis=0, tiled=True)]
    unnamed x56 -> x18, local copies, waits for them, and re-layouts: 9.26 us -> 3.62 us
    pallas_call x5 -> x6, Pallas kernels: 15.1 us -> 18 us  [call(): pl.pallas_call(kernel, out_shape=out_shape, in_specs=[pl.BlockSpec(memory...]
    pallas_call x2 -> x1, Pallas kernels: 2.72 us -> 0.03 us  [pick(): pl.pallas_call(pick_kernel, out_shape=[jax.ShapeDtypeStruct(shape, whole....]
  transfers between devices with their start and end apart: 23 -> 24, of which waited for: 12 -> 14; matrix products, arithmetic and copies ran while one was open for 1% -> 1% of each run, Pallas kernels for 2% -> 1%
where the time goes in v4:
time: 168 us
  starting transfers between devices  62.4 us (37%)
  waiting for transfers between devices  56.9 us (34%)
  blocking collectives  25.9 us (15%)
  Pallas kernels  18 us (11%)
  local copies, waits for them, and re-layouts  3.62 us (2%)
    all_to_all x3, starting transfers between devices, exchange(): lax.all_to_all(pairs, ALL, split_axis=0, concat_axis=0, tiled=True)  33.5 us
    ppermute x21, waiting for transfers between devices, trade(): lax.ppermute(pieces[place], 'rcv', [(source, source ^ place) for source i...  31.9 us
    ppermute x21, starting transfers between devices, trade(): lax.ppermute(pieces[place], 'rcv', [(source, source ^ place) for source i...  28.9 us
    all_to_all x1, blocking collectives, exchange(): lax.all_to_all(pairs, ALL, split_axis=0, concat_axis=0, tiled=True)  25.9 us
    all_to_all x3, waiting for transfers between devices, exchange(): lax.all_to_all(pairs, ALL, split_axis=0, concat_axis=0, tiled=True)  25 us
    pallas_call x6, Pallas kernels, call(): pl.pallas_call(kernel, out_shape=out_shape, in_specs=[pl.BlockSpec(memory...  18 us
    unnamed x18, local copies, waits for them, and re-layouts  3.62 us
  transfers between devices with their start and end apart: 24, of which 14 were waited for; matrix products, arithmetic and copies ran while one was open for 1% of the time, Pallas kernels for 1%

profile of v4, /device:TPU:1, one launch (start us, length us, event | category | flops | bytes accessed | tf_op | source)
XLA Modules:
  0.0 167.9 jit_solution(15140624154430538601)
XLA Ops:
  0.6 3.7 %shard_map.68 = (bf16[2,2,48,512]{3,2,1,0:T(8,128)(2,1)S(1)}, bf16[2,2,48,512]{3,2,1,0:T(8,128)(2,1)}, bf16[2,2,48,512]{3,2,1,0:T(8,128)(2,1)}, bf16[2,2,48,512]...) custom-call(s32[1]{0:T(128)} %bitcast.me_ref, ...), custom_call_target="tpu_custom_call" | custom-call | flops 536870912 | bytes 4194304 | tf_op jit(solution)/shard_map/pallas_call | solution.py:49
  4.3 15.7 %all-to-all-start = ((bf16[256,4,2,128]{3,2,1,0:T(2,128)(2,1)}), bf16[256,4,2,128]{3,2,1,0:T(2,128)(2,1)S(1)}, u32[]{:S(2)}, u32[]{:S(2)}) async-start(bf16[256,4,2,128]{3,2,1,0:T(2,128)(2,1)} %bitcast.1), calls=%async_computation | async-start | bytes 1048576 | tf_op jit(solution)/shard_map/all_to_all | solution.py:256
  20.0 2.2 %collective-permute-start = (bf16[2,2,48,512]{3,2,1,0:T(8,128)(2,1)}, bf16[2,2,48,512]{3,2,1,0:T(8,128)(2,1)S(1)}, u32[]{:S(2)}, u32[]{:S(2)}) collective-permute-start(bf16[2,2,48,512]{3,2,1,0:T(8,128)(2,1)} %get-tuple-element.34), channel_id=1, source_target_pairs={{0,1},{1,0},{2,3},{3,2},{4,5},{5,4},{6,7},{7,6},{8,9},{9,8},{10,11... | collective-permute-start | bytes 589832 | tf_op jit(solution)/shard_map/ppermute | solution.py:250
  22.2 0.0 collective-permute-start.1
  22.2 0.2 copy.10
  22.4 0.2 collective-permute-start.7
  22.7 1.7 %collective-permute-start.8 = (bf16[2,2,48,128]{3,2,1,0:T(8,128)(2,1)S(1)}, bf16[2,2,48,128]{3,2,1,0:T(8,128)(2,1)S(1)}, u32[]{:S(2)}, u32[]{:S(2)}) collective-permute-start(bf16[2,2,48,128]{3,2,1,0:T(8,128)(2,1)S(1)} %get-tuple-element.43), channel_id=1, source_target_pairs={{0,2},{1,3},{2,0},{3,1},{4,6},{5,7},{6,4},{7,5},{8,10},{9,11},{10,... | collective-permute-start | bytes 147464 | tf_op jit(solution)/shard_map/ppermute | solution.py:250
  24.4 0.3 collective-permute-start.9
  24.7 2.0 %collective-permute-start.10 = (bf16[2,2,48,128]{3,2,1,0:T(8,128)(2,1)S(1)}, bf16[2,2,48,128]{3,2,1,0:T(8,128)(2,1)S(1)}, u32[]{:S(2)}, u32[]{:S(2)}) collective-permute-start(bf16[2,2,48,128]{3,2,1,0:T(8,128)(2,1)S(1)} %get-tuple-element.45), channel_id=1, source_target_pairs={{0,4},{1,5},{2,6},{3,7},{4,0},{5,1},{6,2},{7,3},{8,12},{9,13},{10,... | collective-permute-start | bytes 147464 | tf_op jit(solution)/shard_map/ppermute | solution.py:250
  26.7 6.4 %collective-permute-done.8.refs_10_ = bf16[2,2,48,128]{3,2,1,0:T(8,128)(2,1)S(1)} collective-permute-done((bf16[2,2,48,128]{3,2,1,0:T(8,128)(2,1)S(1)}, bf16[2,2,48,128]{3,2,1,0:T(8,128)(2,1)S(1)}, u32[]{:S(2)}, u32[]{:S(2)}) %collective-permute-start.8) | collective-permute-done | bytes 49184 | tf_op jit(solution)/shard_map/ppermute | solution.py:250
  33.1 2.5 %collective-permute-start.11 = (bf16[2,2,48,128]{3,2,1,0:T(8,128)(2,1)S(1)}, bf16[2,2,48,128]{3,2,1,0:T(8,128)(2,1)S(1)}, u32[]{:S(2)}, u32[]{:S(2)}) collective-permute-start(bf16[2,2,48,128]{3,2,1,0:T(8,128)(2,1)S(1)} %get-tuple-element.46), channel_id=1, source_target_pairs={{0,5},{1,4},{2,7},{3,6},{4,1},{5,0},{6,3},{7,2},{8,13},{9,12},{10,... | collective-permute-start | bytes 147464 | tf_op jit(solution)/shard_map/ppermute | solution.py:250
  35.7 0.5 collective-permute-done.9.refs_11_
  36.1 0.9 collective-permute-start.12
  37.0 0.1 collective-permute-done.10.refs_12_
  37.2 2.4 %collective-permute-start.13 = (bf16[2,2,48,128]{3,2,1,0:T(8,128)(2,1)S(1)}, bf16[2,2,48,128]{3,2,1,0:T(8,128)(2,1)S(1)}, u32[]{:S(2)}, u32[]{:S(2)}) collective-permute-start(bf16[2,2,48,128]{3,2,1,0:T(8,128)(2,1)S(1)} %get-tuple-element.48), channel_id=1, source_target_pairs={{0,7},{1,6},{2,5},{3,4},{4,3},{5,2},{6,1},{7,0},{8,15},{9,14},{10,... | collective-permute-start | bytes 147464 | tf_op jit(solution)/shard_map/ppermute | solution.py:250
  39.5 0.5 collective-permute-start.2
  40.1 0.8 collective-permute-done.12.refs_14_
  40.8 1.2 collective-permute-start.3
  42.1 0.4 collective-permute-done.13.refs_15_
  42.5 1.6 collective-permute-start.4
  44.1 1.2 collective-permute-start.5
  45.3 1.8 %collective-permute-start.6 = (bf16[2,2,48,512]{3,2,1,0:T(8,128)(2,1)S(1)}, bf16[2,2,48,512]{3,2,1,0:T(8,128)(2,1)S(1)}, u32[]{:S(2)}, u32[]{:S(2)}) collective-permute-start(bf16[2,2,48,512]{3,2,1,0:T(8,128)(2,1)S(1)} %copy-done.6), channel_id=1, source_target_pairs={{0,7},{1,6},{2,5},{3,4},{4,3},{5,2},{6,1},{7,0},{8,15},{9,14},{10,... | collective-permute-start | bytes 589832 | tf_op jit(solution)/shard_map/ppermute | solution.py:250
  47.1 4.6 %collective-permute-done.3.refs_4_ = bf16[2,2,48,512]{3,2,1,0:T(8,128)(2,1)S(1)} collective-permute-done((bf16[2,2,48,512]{3,2,1,0:T(8,128)(2,1)}, bf16[2,2,48,512]{3,2,1,0:T(8,128)(2,1)S(1)}, u32[]{:S(2)}, u32[]{:S(2)}) %collective-permute-start.3) | collective-permute-done | bytes 196640 | tf_op jit(solution)/shard_map/ppermute | solution.py:250
  51.6 4.3 %collective-permute-done.4.refs_5_ = bf16[2,2,48,512]{3,2,1,0:T(8,128)(2,1)S(1)} collective-permute-done((bf16[2,2,48,512]{3,2,1,0:T(8,128)(2,1)}, bf16[2,2,48,512]{3,2,1,0:T(8,128)(2,1)S(1)}, u32[]{:S(2)}, u32[]{:S(2)}) %collective-permute-start.4) | collective-permute-done | bytes 196640 | tf_op jit(solution)/shard_map/ppermute | solution.py:250
  56.0 4.3 %collective-permute-done.5.refs_6_ = bf16[2,2,48,512]{3,2,1,0:T(8,128)(2,1)S(1)} collective-permute-done((bf16[2,2,48,512]{3,2,1,0:T(8,128)(2,1)S(1)}, bf16[2,2,48,512]{3,2,1,0:T(8,128)(2,1)S(1)}, u32[]{:S(2)}, u32[]{:S(2)}) %collective-permute-start.5) | collective-permute-done | bytes 196640 | tf_op jit(solution)/shard_map/ppermute | solution.py:250
  60.2 4.2 %collective-permute-done.6.refs_7_ = bf16[2,2,48,512]{3,2,1,0:T(8,128)(2,1)S(1)} collective-permute-done((bf16[2,2,48,512]{3,2,1,0:T(8,128)(2,1)S(1)}, bf16[2,2,48,512]{3,2,1,0:T(8,128)(2,1)S(1)}, u32[]{:S(2)}, u32[]{:S(2)}) %collective-permute-start.6) | collective-permute-done | bytes 196640 | tf_op jit(solution)/shard_map/ppermute | solution.py:250
  64.5 2.6 %shard_map.70 = bf16[2560,128]{1,0:T(8,128)(2,1)} custom-call(bf16[2048,128]{1,0:T(8,128)(2,1)S(1)} %bitcast.15, bf16[2,2,48,512]{3,2,1,0:T(8,128)(2,1)S(1)} %get-tuple-element.33.refs_0_, bf16[2,2,48,512]{3,2,1,0:T(8,128)(2,1)S(1)} %collective-permute-done.refs_1_, bf16[2,2,48,512]{3,2,1,0:T(8,128)(2,1)S(1)} %collective-permute-done.1.refs_2_, ...), custom_call_target="tpu_custom_call" | custom-call | flops 805306368 | bytes 4194304 | tf_op jit(solution)/shard_map/pallas_call | solution.py:49
  67.1 11.3 %all-to-all-start.1 = ((bf16[256,5,2,128]{3,2,1,0:T(2,128)(2,1)}), bf16[256,5,2,128]{3,2,1,0:T(2,128)(2,1)S(1)}, u32[]{:S(2)}, u32[]{:S(2)}) async-start(bf16[256,5,2,128]{3,2,1,0:T(2,128)(2,1)} %bitcast.4), calls=%async_computation.1 | async-start | bytes 1310720 | tf_op jit(solution)/shard_map/all_to_all | solution.py:256
  78.4 2.4 %shard_map.71 = (bf16[1024,1024]{1,0:T(8,128)(2,1)}, bf16[1024,1024]{1,0:T(8,128)(2,1)}) custom-call(f32[2,512,128]{2,1,0:T(8,128)S(1)} %copy-done.1), custom_call_target="tpu_custom_call" | custom-call | flops 1048576 | bytes 4194304 | tf_op jit(solution)/shard_map/pallas_call | solution.py:49
  80.9 20.5 %all-to-all-done.1 = bf16[256,5,2,128]{3,2,1,0:T(2,128)(2,1)S(1)} async-done(((bf16[256,5,2,128]{3,2,1,0:T(2,128)(2,1)}), bf16[256,5,2,128]{3,2,1,0:T(2,128)(2,1)S(1)}, u32[]{:S(2)}, u32[]{:S(2)}) %all-to-all-start.1) | async-done | bytes 655392 | tf_op jit(solution)/shard_map/all_to_all | solution.py:256
  101.3 1.6 copy-done.4
  102.9 3.1 %shard_map.72 = (f32[2,1024,128]{2,1,0:T(8,128)}, bf16[2048,128]{1,0:T(8,128)(2,1)S(1)}) custom-call(bf16[2560,128]{1,0:T(8,128)(2,1)S(1)} %bitcast.18, bf16[1024,1024]{1,0:T(8,128)(2,1)S(1)} %copy-done.4, f32[2,1024,128]{2,1,0:T(8,128)} %primaries_ref.3, f32[1,128]{1,0:T(1,128)S(1)} %bitcast.21), custom_call_target="tpu_custom_call" | custom-call | flops 1073741824 | bytes 4194304 | tf_op jit(solution)/shard_map/pallas_call | solution.py:49
  106.0 25.9 %all_to_all.20 = bf16[256,4,2,128]{3,2,1,0:T(2,128)(2,1)S(1)} all-to-all(bf16[256,4,2,128]{3,2,1,0:T(2,128)(2,1)S(1)} %bitcast.20), channel_id=1, replica_groups=mesh['freq'=32,'rcv'=8] {'rcv','freq'}, dimensions={0} | all-to-all | bytes 1048576 | tf_op jit(solution)/shard_map/all_to_all | solution.py:256
  131.9 3.1 %shard_map.73 = (bf16[2560,128]{1,0:T(8,128)(2,1)}, bf16[2,2,48,128]{3,2,1,0:T(8,128)(2,1)}, bf16[2,2,48,128]{3,2,1,0:T(8,128)(2,1)}, bf16[2,2,48,128]{3,2,1,0:T...) custom-call(bf16[2048,128]{1,0:T(8,128)(2,1)S(1)} %bitcast.19, ...), custom_call_target="tpu_custom_call" | custom-call | flops 805306368 | bytes 4194304 | tf_op jit(solution)/shard_map/pallas_call | solution.py:49
  135.1 6.5 %all-to-all-start.3 = ((bf16[256,5,2,128]{3,2,1,0:T(2,128)(2,1)}), bf16[256,5,2,128]{3,2,1,0:T(2,128)(2,1)S(1)}, u32[]{:S(2)}, u32[]{:S(2)}) async-start(bf16[256,5,2,128]{3,2,1,0:T(2,128)(2,1)} %bitcast.9), calls=%async_computation.3 | async-start | bytes 1310720 | tf_op jit(solution)/shard_map/all_to_all | solution.py:256
  141.6 2.4 %collective-permute-start.14 = (bf16[2,2,48,128]{3,2,1,0:T(8,128)(2,1)}, bf16[2,2,48,128]{3,2,1,0:T(8,128)(2,1)S(1)}, u32[]{:S(2)}, u32[]{:S(2)}) collective-permute-start(bf16[2,2,48,128]{3,2,1,0:T(8,128)(2,1)} %get-tuple-element.55), channel_id=1, source_target_pairs={{0,1},{1,0},{2,3},{3,2},{4,5},{5,4},{6,7},{7,6},{8,9},{9,8},{10,11... | collective-permute-start | bytes 147464 | tf_op jit(solution)/shard_map/ppermute | solution.py:250
  144.0 1.7 %collective-permute-start.16 = (bf16[2,2,48,128]{3,2,1,0:T(8,128)(2,1)}, bf16[2,2,48,128]{3,2,1,0:T(8,128)(2,1)S(1)}, u32[]{:S(2)}, u32[]{:S(2)}) collective-permute-start(bf16[2,2,48,128]{3,2,1,0:T(8,128)(2,1)} %get-tuple-element.57), channel_id=1, source_target_pairs={{0,3},{1,2},{2,1},{3,0},{4,7},{5,6},{6,5},{7,4},{8,11},{9,10},{10,... | collective-permute-start | bytes 147464 | tf_op jit(solution)/shard_map/ppermute | solution.py:250
  145.7 1.1 collective-permute-start.17
  146.8 2.1 %collective-permute-start.18 = (bf16[2,2,48,128]{3,2,1,0:T(8,128)(2,1)}, bf16[2,2,48,128]{3,2,1,0:T(8,128)(2,1)S(1)}, u32[]{:S(2)}, u32[]{:S(2)}) collective-permute-start(bf16[2,2,48,128]{3,2,1,0:T(8,128)(2,1)} %get-tuple-element.59), channel_id=1, source_target_pairs={{0,5},{1,4},{2,7},{3,6},{4,1},{5,0},{6,3},{7,2},{8,13},{9,12},{10,... | collective-permute-start | bytes 147464 | tf_op jit(solution)/shard_map/ppermute | solution.py:250
  149.0 0.9 collective-permute-start.19
  149.8 2.1 %collective-permute-start.20 = (bf16[2,2,48,128]{3,2,1,0:T(8,128)(2,1)}, bf16[2,2,48,128]{3,2,1,0:T(8,128)(2,1)S(1)}, u32[]{:S(2)}, u32[]{:S(2)}) collective-permute-start(bf16[2,2,48,128]{3,2,1,0:T(8,128)(2,1)} %get-tuple-element.61), channel_id=1, source_target_pairs={{0,7},{1,6},{2,5},{3,4},{4,3},{5,2},{6,1},{7,0},{8,15},{9,14},{10,... | collective-permute-start | bytes 147464 | tf_op jit(solution)/shard_map/ppermute | solution.py:250
  151.9 2.4 %collective-permute-done.18.refs_5_ = bf16[2,2,48,128]{3,2,1,0:T(8,128)(2,1)S(1)} collective-permute-done((bf16[2,2,48,128]{3,2,1,0:T(8,128)(2,1)}, bf16[2,2,48,128]{3,2,1,0:T(8,128)(2,1)S(1)}, u32[]{:S(2)}, u32[]{:S(2)}) %collective-permute-start.18) | collective-permute-done | bytes 49184 | tf_op jit(solution)/shard_map/ppermute | solution.py:250
  154.3 1.9 %collective-permute-done.19.refs_6_ = bf16[2,2,48,128]{3,2,1,0:T(8,128)(2,1)S(1)} collective-permute-done((bf16[2,2,48,128]{3,2,1,0:T(8,128)(2,1)}, bf16[2,2,48,128]{3,2,1,0:T(8,128)(2,1)S(1)}, u32[]{:S(2)}, u32[]{:S(2)}) %collective-permute-start.19) | collective-permute-done | bytes 49184 | tf_op jit(solution)/shard_map/ppermute | solution.py:250
  156.2 2.0 %collective-permute-done.20.refs_7_ = bf16[2,2,48,128]{3,2,1,0:T(8,128)(2,1)S(1)} collective-permute-done((bf16[2,2,48,128]{3,2,1,0:T(8,128)(2,1)}, bf16[2,2,48,128]{3,2,1,0:T(8,128)(2,1)S(1)}, u32[]{:S(2)}, u32[]{:S(2)}) %collective-permute-start.20) | collective-permute-done | bytes 49184 | tf_op jit(solution)/shard_map/ppermute | solution.py:250
  158.2 0.8 copy-done.2
  159.0 1.1 copy.8
  160.1 4.6 %all-to-all-done.3 = bf16[256,5,2,128]{3,2,1,0:T(2,128)(2,1)S(1)} async-done(((bf16[256,5,2,128]{3,2,1,0:T(2,128)(2,1)}), bf16[256,5,2,128]{3,2,1,0:T(2,128)(2,1)S(1)}, u32[]{:S(2)}, u32[]{:S(2)}) %all-to-all-start.3) | async-done | bytes 655392 | tf_op jit(solution)/shard_map/all_to_all | solution.py:256
  164.7 3.0 %shard_map.74 = f32[2,1024,128]{2,1,0:T(8,128)} custom-call(bf16[2560,128]{1,0:T(8,128)(2,1)S(1)} %bitcast.14, bf16[1024,1024]{1,0:T(8,128)(2,1)S(1)} %copy-done, f32[2,1024,128]{2,1,0:T(8,128)} %get-tuple-element.53.primaries_ref, f32[1,128]{1,0:T(1,128)S(1)} %bitcast.22), custom_call_target="tpu_custom_call" | custom-call | flops 536870912 | bytes 4194304 | tf_op jit(solution)/shard_map/pallas_call | solution.py:49
  (27 shorter events, 0.1 us)
Async XLA Ops:
  0.6 21.6 %copy-start.5 = (bf16[48,16,2,128]{3,2,1,0:T(2,128)(2,1)S(1)}, bf16[48,16,2,128]{3,2,1,0:T(2,128)(2,1)}, u32[]{:S(2)}) copy-start(bf16[48,16,2,128]{3,2,1,0:T(2,128)(2,1)} %param.7) | copy-start | bytes 1179652
  4.3 39.8 %copy-start.7 = (bf16[2,2,48,512]{3,2,1,0:T(8,128)(2,1)S(1)}, bf16[2,2,48,512]{3,2,1,0:T(8,128)(2,1)}, u32[]{:S(2)}) copy-start(bf16[2,2,48,512]{3,2,1,0:T(8,128)(2,1)} %get-tuple-element.39) | copy-start | bytes 589828
  4.3 41.0 %copy-start.6 = (bf16[2,2,48,512]{3,2,1,0:T(8,128)(2,1)S(1)}, bf16[2,2,48,512]{3,2,1,0:T(8,128)(2,1)}, u32[]{:S(2)}) copy-start(bf16[2,2,48,512]{3,2,1,0:T(8,128)(2,1)} %get-tuple-element.40) | copy-start | bytes 589828
  4.3 60.1 %all-to-all-start = ((bf16[256,4,2,128]{3,2,1,0:T(2,128)(2,1)}), bf16[256,4,2,128]{3,2,1,0:T(2,128)(2,1)S(1)}, u32[]{:S(2)}, u32[]{:S(2)}) async-start(bf16[256,4,2,128]{3,2,1,0:T(2,128)(2,1)} %bitcast.1), calls=%async_computation | async-start | bytes 1048576 | tf_op jit(solution)/shard_map/all_to_all | solution.py:256
  20.0 24.1 %collective-permute-start = (bf16[2,2,48,512]{3,2,1,0:T(8,128)(2,1)}, bf16[2,2,48,512]{3,2,1,0:T(8,128)(2,1)S(1)}, u32[]{:S(2)}, u32[]{:S(2)}) collective-permute-start(bf16[2,2,48,512]{3,2,1,0:T(8,128)(2,1)} %get-tuple-element.34), channel_id=1, source_target_pairs={{0,1},{1,0},{2,3},{3,2},{4,5},{5,4},{6,7},{7,6},{8,9},{9,8},{10,11... | collective-permute-start | bytes 589832 | tf_op jit(solution)/shard_map/ppermute | solution.py:250
  22.2 23.1 %collective-permute-start.1 = (bf16[2,2,48,512]{3,2,1,0:T(8,128)(2,1)}, bf16[2,2,48,512]{3,2,1,0:T(8,128)(2,1)S(1)}, u32[]{:S(2)}, u32[]{:S(2)}) collective-permute-start(bf16[2,2,48,512]{3,2,1,0:T(8,128)(2,1)} %get-tuple-element.35), channel_id=1, source_target_pairs={{0,2},{1,3},{2,0},{3,1},{4,6},{5,7},{6,4},{7,5},{8,10},{9,11},{10,... | collective-permute-start | bytes 589832 | tf_op jit(solution)/shard_map/ppermute | solution.py:250
  22.4 2.2 %collective-permute-start.7 = (bf16[2,2,48,128]{3,2,1,0:T(8,128)(2,1)S(1)}, bf16[2,2,48,128]{3,2,1,0:T(8,128)(2,1)S(1)}, u32[]{:S(2)}, u32[]{:S(2)}) collective-permute-start(bf16[2,2,48,128]{3,2,1,0:T(8,128)(2,1)S(1)} %get-tuple-element.42), channel_id=1, source_target_pairs={{0,1},{1,0},{2,3},{3,2},{4,5},{5,4},{6,7},{7,6},{8,9},{9,8},{10,11... | collective-permute-start | bytes 147464 | tf_op jit(solution)/shard_map/ppermute | solution.py:250
  22.7 10.5 %collective-permute-start.8 = (bf16[2,2,48,128]{3,2,1,0:T(8,128)(2,1)S(1)}, bf16[2,2,48,128]{3,2,1,0:T(8,128)(2,1)S(1)}, u32[]{:S(2)}, u32[]{:S(2)}) collective-permute-start(bf16[2,2,48,128]{3,2,1,0:T(8,128)(2,1)S(1)} %get-tuple-element.43), channel_id=1, source_target_pairs={{0,2},{1,3},{2,0},{3,1},{4,6},{5,7},{6,4},{7,5},{8,10},{9,11},{10,... | collective-permute-start | bytes 147464 | tf_op jit(solution)/shard_map/ppermute | solution.py:250
  24.4 11.8 %collective-permute-start.9 = (bf16[2,2,48,128]{3,2,1,0:T(8,128)(2,1)S(1)}, bf16[2,2,48,128]{3,2,1,0:T(8,128)(2,1)S(1)}, u32[]{:S(2)}, u32[]{:S(2)}) collective-permute-start(bf16[2,2,48,128]{3,2,1,0:T(8,128)(2,1)S(1)} %get-tuple-element.44), channel_id=1, source_target_pairs={{0,3},{1,2},{2,1},{3,0},{4,7},{5,6},{6,5},{7,4},{8,11},{9,10},{10,... | collective-permute-start | bytes 147464 | tf_op jit(solution)/shard_map/ppermute | solution.py:250
  24.7 12.5 %collective-permute-start.10 = (bf16[2,2,48,128]{3,2,1,0:T(8,128)(2,1)S(1)}, bf16[2,2,48,128]{3,2,1,0:T(8,128)(2,1)S(1)}, u32[]{:S(2)}, u32[]{:S(2)}) collective-permute-start(bf16[2,2,48,128]{3,2,1,0:T(8,128)(2,1)S(1)} %get-tuple-element.45), channel_id=1, source_target_pairs={{0,4},{1,5},{2,6},{3,7},{4,0},{5,1},{6,2},{7,3},{8,12},{9,13},{10,... | collective-permute-start | bytes 147464 | tf_op jit(solution)/shard_map/ppermute | solution.py:250
  33.1 6.4 %collective-permute-start.11 = (bf16[2,2,48,128]{3,2,1,0:T(8,128)(2,1)S(1)}, bf16[2,2,48,128]{3,2,1,0:T(8,128)(2,1)S(1)}, u32[]{:S(2)}, u32[]{:S(2)}) collective-permute-start(bf16[2,2,48,128]{3,2,1,0:T(8,128)(2,1)S(1)} %get-tuple-element.46), channel_id=1, source_target_pairs={{0,5},{1,4},{2,7},{3,6},{4,1},{5,0},{6,3},{7,2},{8,13},{9,12},{10,... | collective-permute-start | bytes 147464 | tf_op jit(solution)/shard_map/ppermute | solution.py:250
  36.1 4.7 %collective-permute-start.12 = (bf16[2,2,48,128]{3,2,1,0:T(8,128)(2,1)S(1)}, bf16[2,2,48,128]{3,2,1,0:T(8,128)(2,1)S(1)}, u32[]{:S(2)}, u32[]{:S(2)}) collective-permute-start(bf16[2,2,48,128]{3,2,1,0:T(8,128)(2,1)S(1)} %get-tuple-element.47), channel_id=1, source_target_pairs={{0,6},{1,7},{2,4},{3,5},{4,2},{5,3},{6,0},{7,1},{8,14},{9,15},{10,... | collective-permute-start | bytes 147464 | tf_op jit(solution)/shard_map/ppermute | solution.py:250
  37.2 5.3 %collective-permute-start.13 = (bf16[2,2,48,128]{3,2,1,0:T(8,128)(2,1)S(1)}, bf16[2,2,48,128]{3,2,1,0:T(8,128)(2,1)S(1)}, u32[]{:S(2)}, u32[]{:S(2)}) collective-permute-start(bf16[2,2,48,128]{3,2,1,0:T(8,128)(2,1)S(1)} %get-tuple-element.48), channel_id=1, source_target_pairs={{0,7},{1,6},{2,5},{3,4},{4,3},{5,2},{6,1},{7,0},{8,15},{9,14},{10,... | collective-permute-start | bytes 147464 | tf_op jit(solution)/shard_map/ppermute | solution.py:250
  39.5 7.5 %collective-permute-start.2 = (bf16[2,2,48,512]{3,2,1,0:T(8,128)(2,1)}, bf16[2,2,48,512]{3,2,1,0:T(8,128)(2,1)S(1)}, u32[]{:S(2)}, u32[]{:S(2)}) collective-permute-start(bf16[2,2,48,512]{3,2,1,0:T(8,128)(2,1)} %get-tuple-element.36), channel_id=1, source_target_pairs={{0,3},{1,2},{2,1},{3,0},{4,7},{5,6},{6,5},{7,4},{8,11},{9,10},{10,... | collective-permute-start | bytes 589832 | tf_op jit(solution)/shard_map/ppermute | solution.py:250
  40.8 10.8 %collective-permute-start.3 = (bf16[2,2,48,512]{3,2,1,0:T(8,128)(2,1)}, bf16[2,2,48,512]{3,2,1,0:T(8,128)(2,1)S(1)}, u32[]{:S(2)}, u32[]{:S(2)}) collective-permute-start(bf16[2,2,48,512]{3,2,1,0:T(8,128)(2,1)} %get-tuple-element.37), channel_id=1, source_target_pairs={{0,4},{1,5},{2,6},{3,7},{4,0},{5,1},{6,2},{7,3},{8,12},{9,13},{10,... | collective-permute-start | bytes 589832 | tf_op jit(solution)/shard_map/ppermute | solution.py:250
  42.5 13.5 %collective-permute-start.4 = (bf16[2,2,48,512]{3,2,1,0:T(8,128)(2,1)}, bf16[2,2,48,512]{3,2,1,0:T(8,128)(2,1)S(1)}, u32[]{:S(2)}, u32[]{:S(2)}) collective-permute-start(bf16[2,2,48,512]{3,2,1,0:T(8,128)(2,1)} %get-tuple-element.38), channel_id=1, source_target_pairs={{0,5},{1,4},{2,7},{3,6},{4,1},{5,0},{6,3},{7,2},{8,13},{9,12},{10,... | collective-permute-start | bytes 589832 | tf_op jit(solution)/shard_map/ppermute | solution.py:250
  44.1 16.1 %collective-permute-start.5 = (bf16[2,2,48,512]{3,2,1,0:T(8,128)(2,1)S(1)}, bf16[2,2,48,512]{3,2,1,0:T(8,128)(2,1)S(1)}, u32[]{:S(2)}, u32[]{:S(2)}) collective-permute-start(bf16[2,2,48,512]{3,2,1,0:T(8,128)(2,1)S(1)} %copy-done.7), channel_id=1, source_target_pairs={{0,6},{1,7},{2,4},{3,5},{4,2},{5,3},{6,0},{7,1},{8,14},{9,15},{10,... | collective-permute-start | bytes 589832 | tf_op jit(solution)/shard_map/ppermute | solution.py:250
  45.3 19.1 %collective-permute-start.6 = (bf16[2,2,48,512]{3,2,1,0:T(8,128)(2,1)S(1)}, bf16[2,2,48,512]{3,2,1,0:T(8,128)(2,1)S(1)}, u32[]{:S(2)}, u32[]{:S(2)}) collective-permute-start(bf16[2,2,48,512]{3,2,1,0:T(8,128)(2,1)S(1)} %copy-done.6), channel_id=1, source_target_pairs={{0,7},{1,6},{2,5},{3,4},{4,3},{5,2},{6,1},{7,0},{8,15},{9,14},{10,... | collective-permute-start | bytes 589832 | tf_op jit(solution)/shard_map/ppermute | solution.py:250
  64.5 14.0 %copy-start.1 = (f32[2,512,128]{2,1,0:T(8,128)S(1)}, f32[2,512,128]{2,1,0:T(8,128)}, u32[]{:S(2)}) copy-start(f32[2,512,128]{2,1,0:T(8,128)} %constant.6.clone.base_ref) | copy-start | bytes 1572868
  64.5 36.9 %copy-start.3 = (f32[128]{0:T(128)S(1)}, f32[128]{0:T(128)}, u32[]{:S(2)}) copy-start(f32[128]{0:T(128)} %param.8) | copy-start | bytes 1540
  67.1 34.3 %all-to-all-start.1 = ((bf16[256,5,2,128]{3,2,1,0:T(2,128)(2,1)}), bf16[256,5,2,128]{3,2,1,0:T(2,128)(2,1)S(1)}, u32[]{:S(2)}, u32[]{:S(2)}) async-start(bf16[256,5,2,128]{3,2,1,0:T(2,128)(2,1)} %bitcast.4), calls=%async_computation.1 | async-start | bytes 1310720 | tf_op jit(solution)/shard_map/all_to_all | solution.py:256
  101.3 1.6 copy-start.4
  135.1 29.6 %copy-start = (bf16[1024,1024]{1,0:T(8,128)(2,1)S(1)}, bf16[1024,1024]{1,0:T(8,128)(2,1)}, u32[]{:S(2)}) copy-start(bf16[1024,1024]{1,0:T(8,128)(2,1)} %get-tuple-element.52.table_ref) | copy-start | bytes 6291460
  135.1 29.6 %all-to-all-start.3 = ((bf16[256,5,2,128]{3,2,1,0:T(2,128)(2,1)}), bf16[256,5,2,128]{3,2,1,0:T(2,128)(2,1)S(1)}, u32[]{:S(2)}, u32[]{:S(2)}) async-start(bf16[256,5,2,128]{3,2,1,0:T(2,128)(2,1)} %bitcast.9), calls=%async_computation.3 | async-start | bytes 1310720 | tf_op jit(solution)/shard_map/all_to_all | solution.py:256
  141.6 7.4 %collective-permute-start.14 = (bf16[2,2,48,128]{3,2,1,0:T(8,128)(2,1)}, bf16[2,2,48,128]{3,2,1,0:T(8,128)(2,1)S(1)}, u32[]{:S(2)}, u32[]{:S(2)}) collective-permute-start(bf16[2,2,48,128]{3,2,1,0:T(8,128)(2,1)} %get-tuple-element.55), channel_id=1, source_target_pairs={{0,1},{1,0},{2,3},{3,2},{4,5},{5,4},{6,7},{7,6},{8,9},{9,8},{10,11... | collective-permute-start | bytes 147464 | tf_op jit(solution)/shard_map/ppermute | solution.py:250
  144.0 5.9 %collective-permute-start.15 = (bf16[2,2,48,128]{3,2,1,0:T(8,128)(2,1)}, bf16[2,2,48,128]{3,2,1,0:T(8,128)(2,1)S(1)}, u32[]{:S(2)}, u32[]{:S(2)}) collective-permute-start(bf16[2,2,48,128]{3,2,1,0:T(8,128)(2,1)} %get-tuple-element.56), channel_id=1, source_target_pairs={{0,2},{1,3},{2,0},{3,1},{4,6},{5,7},{6,4},{7,5},{8,10},{9,11},{10,... | collective-permute-start | bytes 147464 | tf_op jit(solution)/shard_map/ppermute | solution.py:250
  144.0 7.9 %collective-permute-start.16 = (bf16[2,2,48,128]{3,2,1,0:T(8,128)(2,1)}, bf16[2,2,48,128]{3,2,1,0:T(8,128)(2,1)S(1)}, u32[]{:S(2)}, u32[]{:S(2)}) collective-permute-start(bf16[2,2,48,128]{3,2,1,0:T(8,128)(2,1)} %get-tuple-element.57), channel_id=1, source_target_pairs={{0,3},{1,2},{2,1},{3,0},{4,7},{5,6},{6,5},{7,4},{8,11},{9,10},{10,... | collective-permute-start | bytes 147464 | tf_op jit(solution)/shard_map/ppermute | solution.py:250
  145.7 6.2 %collective-permute-start.17 = (bf16[2,2,48,128]{3,2,1,0:T(8,128)(2,1)}, bf16[2,2,48,128]{3,2,1,0:T(8,128)(2,1)S(1)}, u32[]{:S(2)}, u32[]{:S(2)}) collective-permute-start(bf16[2,2,48,128]{3,2,1,0:T(8,128)(2,1)} %get-tuple-element.58), channel_id=1, source_target_pairs={{0,4},{1,5},{2,6},{3,7},{4,0},{5,1},{6,2},{7,3},{8,12},{9,13},{10,... | collective-permute-start | bytes 147464 | tf_op jit(solution)/shard_map/ppermute | solution.py:250
  146.8 7.5 %collective-permute-start.18 = (bf16[2,2,48,128]{3,2,1,0:T(8,128)(2,1)}, bf16[2,2,48,128]{3,2,1,0:T(8,128)(2,1)S(1)}, u32[]{:S(2)}, u32[]{:S(2)}) collective-permute-start(bf16[2,2,48,128]{3,2,1,0:T(8,128)(2,1)} %get-tuple-element.59), channel_id=1, source_target_pairs={{0,5},{1,4},{2,7},{3,6},{4,1},{5,0},{6,3},{7,2},{8,13},{9,12},{10,... | collective-permute-start | bytes 147464 | tf_op jit(solution)/shard_map/ppermute | solution.py:250
  149.0 7.3 %collective-permute-start.19 = (bf16[2,2,48,128]{3,2,1,0:T(8,128)(2,1)}, bf16[2,2,48,128]{3,2,1,0:T(8,128)(2,1)S(1)}, u32[]{:S(2)}, u32[]{:S(2)}) collective-permute-start(bf16[2,2,48,128]{3,2,1,0:T(8,128)(2,1)} %get-tuple-element.60), channel_id=1, source_target_pairs={{0,6},{1,7},{2,4},{3,5},{4,2},{5,3},{6,0},{7,1},{8,14},{9,15},{10,... | collective-permute-start | bytes 147464 | tf_op jit(solution)/shard_map/ppermute | solution.py:250
  149.8 8.4 %collective-permute-start.20 = (bf16[2,2,48,128]{3,2,1,0:T(8,128)(2,1)}, bf16[2,2,48,128]{3,2,1,0:T(8,128)(2,1)S(1)}, u32[]{:S(2)}, u32[]{:S(2)}) collective-permute-start(bf16[2,2,48,128]{3,2,1,0:T(8,128)(2,1)} %get-tuple-element.61), channel_id=1, source_target_pairs={{0,7},{1,6},{2,5},{3,4},{4,3},{5,2},{6,1},{7,0},{8,15},{9,14},{10,... | collective-permute-start | bytes 147464 | tf_op jit(solution)/shard_map/ppermute | solution.py:250
  158.2 0.8 copy-start.2

commit v5 on v4

--- a/solution.py
+++ b/solution.py
@@ -18,6 +18,7 @@
 NF = 512
 ALL = ("rcv", "freq")
 LANES = 128
+EARLY = (4, 6, 2, 5, 7, 3, 1)
 PARTS = 4
 WIDE = PARTS + 1
 
@@ -65,28 +66,40 @@
     spectra_ref[...] = rows_ref[...].astype(jnp.bfloat16)
 
 
-def start_kernel(owners, blocks, me_ref, op_ref, primaries_ref, base_ref, *refs):
+def start_kernel(owners, blocks, me_ref, op_ref, data_ref, primaries_ref, base_ref, *refs):
     pieces, spectra_ref = refs[:blocks], refs[blocks]
-    held_ref, traces_ref, angles_ref, table_ref, rows_ref, sem = refs[blocks + 1:]
-    targets = [pieces[0]] + [held_ref.at[place] for place in range(1, blocks)]
-    fetch_base = pltpu.make_async_copy(base_ref, angles_ref, sem.at[2, 0])
-    fetch_traces = pltpu.make_async_copy(primaries_ref, traces_ref, sem.at[2, 1])
+    op_held, data_held, data_rows, piece_held, traces_ref, angles_ref, table_ref, rows_ref, sem = refs[blocks + 1:]
+    frequencies = 2 * blocks
+    rows = data_ref.shape[0] // (2 * frequencies)
+    part = PARTS * rows
     fetches = [
-        pltpu.make_async_copy(op_ref.at[pl.ds(2 * (me_ref[0] ^ place), 2)], targets[place], sem.at[0, place])
-        for place in range(blocks)
+        pltpu.make_async_copy(source, target, sem.at[blocks + place])
+        for place, (source, target) in enumerate(
+            ((base_ref, angles_ref), (data_ref, data_held), (op_ref, op_held), (primaries_ref, traces_ref))
+        )
     ]
-    stores = [pltpu.make_async_copy(targets[place], pieces[place], sem.at[1, place]) for place in range(1, blocks)]
-    fetch_base.start()
-    fetch_traces.start()
+    fetch_base, fetch_data, fetch_op, fetch_traces = fetches
     for fetch in fetches:
         fetch.start()
     fetch_base.wait()
     fill_table(angles_ref, table_ref, owners, blocks)
+    fetch_data.wait()
+    data_rows[...] = data_held[...].astype(jnp.float32)
+    fetch_op.wait()
+    stores = []
+    for place in EARLY + (0,):
+        owner = me_ref[0] ^ place
+        target = piece_held.at[place] if place else pieces[0]
+        block = op_held[pl.ds(2 * owner, 2)].reshape(part, NS)
+        for tile in range(NS // LANES):
+            target[pl.ds(tile * part, part), :] = block[:, tile * LANES:(tile + 1) * LANES]
+        for row in range(PARTS):
+            recorded = data_rows[pl.ds(PARTS * owner + row, rows, stride=2 * frequencies), :]
+            target[pl.ds(NS // LANES * part + row * rows, rows), :] = recorded.astype(jnp.bfloat16)
+        if place:
+            stores.append(pltpu.make_async_copy(target, pieces[place], sem.at[place]))
+            stores[-1].start()
     fetch_traces.wait()
-    for place in range(blocks):
-        fetches[place].wait()
-        if place:
-            stores[place - 1].start()
     low = jnp.concatenate([traces_ref[0].astype(jnp.bfloat16), traces_ref[1].astype(jnp.bfloat16)], axis=1)
     transform(table_ref, low, rows_ref, spectra_ref, owners)
     for store in stores:
@@ -100,13 +113,10 @@
     return [high, middle, rest - middle]
 
 
-def physics_kernel(blocks, returned, points_ref, *refs):
-    op_refs, data_refs = refs[:blocks], refs[blocks:2 * blocks]
-    packed_ref = refs[2 * blocks]
-    returned_refs = refs[2 * blocks + 1:2 * blocks + 1 + returned]
-    residual_ref, rows_ref, wide_ref, sem = refs[2 * blocks + 1 + returned:]
-    rows = op_refs[0].shape[2]
-    copies = []
+def physics_kernel(blocks, rows, points_ref, *refs):
+    pieces = refs[:blocks]
+    packed_ref, *residual_refs, rows_ref, wide_ref = refs[blocks:]
+    part = PARTS * rows
     rows_ref[...] = points_ref[...].astype(jnp.float32)
     residual_sq = jnp.zeros((1, 1), jnp.float32)
     direction_sq = jnp.zeros((1, 1), jnp.float32)
@@ -114,15 +124,26 @@
         spectra = jnp.concatenate(
             [rows_ref[pl.ds(2 * k + c, NS, stride=PARTS), :].astype(jnp.bfloat16) for c in range(2)], axis=1
         )
-        op = jnp.concatenate([op_refs[a][k].reshape(2 * rows, NS) for a in range(blocks)], axis=0)
+        op = jnp.concatenate(
+            [
+                jnp.concatenate(
+                    [piece[pl.ds(tile * part + 2 * k * rows, 2 * rows), :] for tile in range(NS // LANES)], axis=1
+                )
+                for piece in pieces
+            ],
+            axis=0,
+        )
         product = jnp.dot(op, spectra, preferred_element_type=jnp.float32).reshape(blocks, 2, rows, 2 * S)
         stacked = []
         for a in range(blocks):
             real = product[a, 0, :, :S] - product[a, 1, :, S:]
             imag = product[a, 0, :, S:] + product[a, 1, :, :S]
-            real = (data_refs[a][k, 0].astype(jnp.float32) - real).astype(jnp.bfloat16)
-            imag = (data_refs[a][k, 1].astype(jnp.float32) - imag).astype(jnp.bfloat16)
-            if returned:
+            recorded = [
+                pieces[a][pl.ds(NS // LANES * part + (2 * k + c) * rows, rows), :] for c in range(2)
+            ]
+            real = (recorded[0].astype(jnp.float32) - real).astype(jnp.bfloat16)
+            imag = (recorded[1].astype(jnp.float32) - imag).astype(jnp.bfloat16)
+            for residual_ref in residual_refs:
                 residual_ref[a, k, 0] = real
                 residual_ref[a, k, 1] = imag
             wide_real = real.astype(jnp.float32)
@@ -130,9 +151,6 @@
             residual_sq += jnp.sum(wide_real * wide_real + wide_imag * wide_imag, keepdims=True)
             stacked.append(jnp.concatenate([real, imag], axis=1))
             stacked.append(jnp.concatenate([imag, -real], axis=1))
-        for a, out in enumerate(returned_refs):
-            copies.append(pltpu.make_async_copy(residual_ref.at[a, k], out.at[k], sem.at[k, a]))
-            copies[-1].start()
         direction = lax.dot_general(
             op, jnp.concatenate(stacked, axis=0), (((0,), (0,)), ((), ())), preferred_element_type=jnp.float32
         )
@@ -145,13 +163,9 @@
         sums = jnp.where(lane == place, piece, sums)
     wide_ref[pl.ds(PARTS, NS, stride=WIDE), :] = jnp.broadcast_to(sums[:1], (NS, S))
     packed_ref[...] = wide_ref[...].astype(jnp.bfloat16)
-    for copy in copies:
-        copy.wait()
-
-
-def update(owners, packed_ref, table_ref, primaries_ref, shrinkage_ref, wide_ref, held_ref, sem):
-    fetch = pltpu.make_async_copy(primaries_ref, held_ref, sem.at[0])
-    fetch.start()
+
+
+def update(owners, packed_ref, table_ref, held_ref, shrinkage_ref, wide_ref, fetch, finish):
     wide_ref[...] = packed_ref[...].astype(jnp.float32)
     totals = jnp.sum(wide_ref[pl.ds(PARTS, owners, stride=2 * WIDE), :], axis=0, keepdims=True)
     lane = lax.broadcasted_iota(jnp.int32, (1, S), 1)
@@ -167,37 +181,47 @@
         ]
         sides.append(jnp.concatenate(pieces, axis=0))
     direction = jnp.concatenate(sides, axis=1)
-    lows = []
-    block = 256
-    fetch.wait()
+    block = T_SIZE // 4
     for start in range(0, T_SIZE, block):
         change = lax.dot_general(
             table_ref[:, pl.ds(start, block)], direction, (((0,), (0,)), ((), ())), preferred_element_type=jnp.float32
         )
-        halves = []
+        if fetch and not start:
+            fetch.wait()
+        news = []
         for point in range(2):
             moved = held_ref[point, pl.ds(start, block), :] + step_size * change[:, point * S:(point + 1) * S]
-            new = moved - jnp.clip(moved, -threshold, threshold)
-            held_ref[point, pl.ds(start, block), :] = new
-            halves.append(new.astype(jnp.bfloat16))
-        lows.append(jnp.concatenate(halves, axis=1))
-    return lows
-
-
-def middle_kernel(owners, packed_ref, table_ref, primaries_ref, shrinkage_ref, new_ref, spectra_ref, *scratch):
-    wide_ref, held_ref, rows_ref, sem = scratch
-    lows = update(owners, packed_ref, table_ref, primaries_ref, shrinkage_ref, wide_ref, held_ref, sem)
-    store = pltpu.make_async_copy(held_ref, new_ref, sem.at[1])
-    store.start()
+            news.append(moved - jnp.clip(moved, -threshold, threshold))
+        finish(pl.ds(start, block), news)
+
+
+def middle_kernel(owners, packed_ref, table_ref, primaries_ref, shrinkage_ref, new_ref, spectra_ref, wide_ref, rows_ref):
+    lows = []
+
+    def finish(window, news):
+        for point, new in enumerate(news):
+            new_ref[point, window, :] = new
+        lows.append(jnp.concatenate([new.astype(jnp.bfloat16) for new in news], axis=1))
+
+    update(owners, packed_ref, table_ref, primaries_ref, shrinkage_ref, wide_ref, None, finish)
     transform(table_ref, jnp.concatenate(lows, axis=0), rows_ref, spectra_ref, owners)
-    store.wait()
 
 
 def last_kernel(owners, packed_ref, table_ref, primaries_ref, shrinkage_ref, new_ref, wide_ref, held_ref, sem):
-    update(owners, packed_ref, table_ref, primaries_ref, shrinkage_ref, wide_ref, held_ref, sem)
-    store = pltpu.make_async_copy(held_ref, new_ref, sem.at[1])
-    store.start()
-    store.wait()
+    fetch = pltpu.make_async_copy(primaries_ref, held_ref, sem.at[4])
+    fetch.start()
+    stores = []
+
+    def finish(window, news):
+        for point, new in enumerate(news):
+            held_ref[point, window, :] = new
+        part = (slice(None), window)
+        stores.append(pltpu.make_async_copy(held_ref.at[part], new_ref.at[part], sem.at[len(stores)]))
+        stores[-1].start()
+
+    update(owners, packed_ref, table_ref, held_ref, shrinkage_ref, wide_ref, fetch, finish)
+    for store in stores:
+        store.wait()
 
 
 def table_kernel(owners, rcv_parts, base_ref, first_ref, second_ref, table_ref, sem):
@@ -209,20 +233,13 @@
         store.wait()
 
 
-def pick_kernel(me_ref, whole_ref, *pieces):
-    for place, piece in enumerate(pieces):
-        piece[...] = whole_ref[pl.ds(2 * (me_ref[0] ^ place), 2)]
-
-
-def pick(whole, me, blocks):
-    shape = (2,) + whole.shape[1:]
-    return pl.pallas_call(
-        pick_kernel,
-        out_shape=[jax.ShapeDtypeStruct(shape, whole.dtype)] * blocks,
-        in_specs=[pl.BlockSpec(memory_space=pltpu.SMEM), pl.BlockSpec(memory_space=pltpu.VMEM)],
-        out_specs=[pl.BlockSpec(memory_space=pltpu.VMEM)] * blocks,
-        compiler_params=pltpu.CompilerParams(vmem_limit_bytes=8 * 2**20),
-    )(me, whole)
+def hand_out_kernel(whole_ref, *refs):
+    *pieces, sem = refs
+    copies = [pltpu.make_async_copy(whole_ref.at[a], piece, sem.at[a]) for a, piece in enumerate(pieces)]
+    for copy in copies:
+        copy.start()
+    for copy in copies:
+        copy.wait()
 
 
 def join_kernel(blocks, me_ref, *refs):
@@ -266,28 +283,32 @@
     base = table_base(freq_parts, rcv_parts)
     shrinkage = shrinkage.reshape(1, S)
     me = lax.axis_index("rcv").astype(jnp.int32).reshape(1)
-    data = trade(pick(data_spectra.transpose(1, 2, 0, 3), me, rcv_parts))
     primaries = primaries_start
-    piece = (2, 2, rows, NS)
-    *op, spectra = call(
+    piece = (PARTS * rows * (NS // LANES + 1), LANES)
+    recorded = data_spectra.reshape(-1, S)
+    arrays = (surface_operator, recorded, primaries, base)
+    *pieces, spectra = call(
         functools.partial(start_kernel, devices, rcv_parts),
         [jax.ShapeDtypeStruct(piece, bf16)]
         + [pltpu.HBM(piece, bf16)] * (rcv_parts - 1)
         + [jax.ShapeDtypeStruct(half, bf16)],
         [
+            pltpu.VMEM(surface_operator.shape, bf16),
+            pltpu.VMEM(recorded.shape, bf16),
+            pltpu.VMEM(recorded.shape, f32),
             pltpu.VMEM((rcv_parts,) + piece, bf16),
             pltpu.VMEM(primaries.shape, f32),
             pltpu.VMEM(base.shape, f32),
             table,
             rows_half,
-            pltpu.SemaphoreType.DMA((3, rcv_parts)),
+            pltpu.SemaphoreType.DMA((rcv_parts + 4,)),
         ],
-        (me, *(pltpu.with_memory_space_constraint(array, pltpu.HBM) for array in (surface_operator, primaries, base))),
+        (me, *(pltpu.with_memory_space_constraint(array, pltpu.HBM) for array in arrays)),
         2 * 1024 * 1024 * 256,
-        [pltpu.SMEM] + [pltpu.HBM] * 3,
+        [pltpu.SMEM] + [pltpu.HBM] * 4,
         [pltpu.VMEM] + [pltpu.HBM] * (rcv_parts - 1) + [pltpu.VMEM],
     )
-    op = trade(op)
+    pieces = trade(pieces)
     tables = call(
         functools.partial(table_kernel, devices, rcv_parts),
         [pltpu.HBM((2 * NF, T_SIZE), bf16)] * 2,
@@ -299,46 +320,43 @@
     )
     for iteration in range(ITERS):
         points = exchange(spectra, devices)
-        returned = rcv_parts if iteration + 1 == ITERS else 0
         packed, *residual = call(
-            functools.partial(physics_kernel, rcv_parts, returned),
-            [jax.ShapeDtypeStruct(wide, bf16)] + [pltpu.HBM((2, 2, rows, S), bf16)] * returned,
-            [
-                pltpu.VMEM((rcv_parts, 2, 2, rows, S), bf16),
-                rows_half,
-                rows_wide,
-                pltpu.SemaphoreType.DMA((2, rcv_parts)),
-            ],
-            (points, *op, *data),
+            functools.partial(physics_kernel, rcv_parts, rows),
+            [jax.ShapeDtypeStruct(wide, bf16)]
+            + [jax.ShapeDtypeStruct((rcv_parts, 2, 2, rows, S), bf16)] * (iteration + 1 == ITERS),
+            [rows_half, rows_wide],
+            (points, *pieces),
             4 * 2 * 768 * 512 * 256,
-            [pltpu.VMEM] * (1 + 2 * rcv_parts),
-            [pltpu.VMEM] + [pltpu.HBM] * returned,
         )
         packed = exchange(packed, devices)
-        shape = pltpu.HBM(primaries.shape, f32)
-        inputs = (packed, tables[iteration], pltpu.with_memory_space_constraint(primaries, pltpu.HBM), shrinkage)
-        spaces = [pltpu.VMEM, pltpu.VMEM, pltpu.HBM, pltpu.VMEM]
-        held = [rows_wide, pltpu.VMEM(primaries.shape, f32)]
         if iteration + 1 < ITERS:
             primaries, spectra = call(
                 functools.partial(middle_kernel, devices),
-                [shape, jax.ShapeDtypeStruct(half, bf16)],
-                held + [rows_half, pltpu.SemaphoreType.DMA((2,))],
-                inputs,
+                [jax.ShapeDtypeStruct(primaries.shape, f32), jax.ShapeDtypeStruct(half, bf16)],
+                [rows_wide, rows_half],
+                (packed, tables[iteration], primaries, shrinkage),
                 4 * 1024 * 1024 * 256,
-                spaces,
-                [pltpu.HBM, pltpu.VMEM],
             )
         else:
             primaries, = call(
                 functools.partial(last_kernel, devices),
-                [shape],
-                held + [pltpu.SemaphoreType.DMA((2,))],
-                inputs,
+                [pltpu.HBM(primaries.shape, f32)],
+                [rows_wide, pltpu.VMEM(primaries.shape, f32), pltpu.SemaphoreType.DMA((5,))],
+                (packed, tables[iteration], pltpu.with_memory_space_constraint(primaries, pltpu.HBM), shrinkage),
                 2 * 1024 * 1024 * 256,
-                spaces,
+                [pltpu.VMEM, pltpu.VMEM, pltpu.HBM, pltpu.VMEM],
                 [pltpu.HBM],
             )
+    residual, = residual
+    residual = call(
+        hand_out_kernel,
+        [pltpu.HBM(residual.shape[1:], bf16)] * rcv_parts,
+        [pltpu.SemaphoreType.DMA((rcv_parts,))],
+        (residual,),
+        2**20,
+        None,
+        [pltpu.HBM] * rcv_parts,
+    )
     residual = join(trade(residual), me)
     return (primaries, residual.transpose(2, 0, 1, 3))
 

time: 168 us -> 160 us (0.952)
  starting transfers between devices: 62.4 us -> 53.7 us
  local copies, waits for them, and re-layouts: 3.62 us -> 8.42 us
  waiting for transfers between devices: 56.9 us -> 53.6 us
    ppermute x21 -> x14, starting transfers between devices: 28.9 us -> 21 us  [trade(): lax.ppermute(pieces[place], 'rcv', [(source, source ^ place) for source i...]
    unnamed x18 -> x49, local copies, waits for them, and re-layouts: 3.62 us -> 8.42 us
    ppermute x21 -> x14, waiting for transfers between devices: 31.9 us -> 29.4 us  [trade(): lax.ppermute(pieces[place], 'rcv', [(source, source ^ place) for source i...]
    pallas_call x6 -> x7, Pallas kernels: 18 us -> 16.7 us  [call(): pl.pallas_call(kernel, out_shape=out_shape, in_specs=[pl.BlockSpec(memory...]
  transfers between devices with their start and end apart: 24 -> 17, of which waited for: 14 -> 10; matrix products, arithmetic and copies ran while one was open for 1% -> 1% of each run, Pallas kernels for 1% -> 2%
where the time goes in v5:
time: 160 us; the launch traced here: 159 us
  starting transfers between devices  53.7 us (34%)
  waiting for transfers between devices  53.6 us (34%)
  blocking collectives  25.9 us (16%)
  Pallas kernels  16.7 us (10%)
  local copies, waits for them, and re-layouts  8.42 us (5%)
    all_to_all x3, starting transfers between devices, exchange(): lax.all_to_all(pairs, ALL, split_axis=0, concat_axis=0, tiled=True)  32.7 us
    ppermute x14, waiting for transfers between devices, trade(): lax.ppermute(pieces[place], 'rcv', [(source, source ^ place) for source i...  29.4 us
    all_to_all x1, blocking collectives, exchange(): lax.all_to_all(pairs, ALL, split_axis=0, concat_axis=0, tiled=True)  25.9 us
    all_to_all x3, waiting for transfers between devices, exchange(): lax.all_to_all(pairs, ALL, split_axis=0, concat_axis=0, tiled=True)  24.2 us
    ppermute x14, starting transfers between devices, trade(): lax.ppermute(pieces[place], 'rcv', [(source, source ^ place) for source i...  21 us
    pallas_call x7, Pallas kernels, call(): pl.pallas_call(kernel, out_shape=out_shape, in_specs=[pl.BlockSpec(memory...  16.7 us
    unnamed x49, local copies, waits for them, and re-layouts  8.42 us
  transfers between devices with their start and end apart: 17, of which 10 were waited for; matrix products, arithmetic and copies ran while one was open for 1% of the time, Pallas kernels for 2%

profile of v5, /device:TPU:1, one launch (start us, length us, event | category | flops | bytes accessed | tf_op | source)
XLA Modules:
  0.0 159.3 jit_solution(13439346394025131188)
XLA Ops:
  0.6 4.1 %shard_map.68 = (bf16[960,128]{1,0:T(8,128)(2,1)S(1)}, bf16[960,128]{1,0:T(8,128)(2,1)}, bf16[960,128]{1,0:T(8,128)(2,1)}, bf16[960,128]{1,0:T(8,128)(2,1)}, bf1...) custom-call(s32[1]{0:T(128)} %bitcast.me_ref, ...), custom_call_target="tpu_custom_call" | custom-call | flops 536870912 | bytes 4194304 | tf_op jit(solution)/shard_map/pallas_call | solution.py:50
  4.8 15.6 %all-to-all-start = ((bf16[256,4,2,128]{3,2,1,0:T(2,128)(2,1)}), bf16[256,4,2,128]{3,2,1,0:T(2,128)(2,1)S(1)}, u32[]{:S(2)}, u32[]{:S(2)}) async-start(bf16[256,4,2,128]{3,2,1,0:T(2,128)(2,1)} %bitcast.2), calls=%async_computation | async-start | bytes 1048576 | tf_op jit(solution)/shard_map/all_to_all | solution.py:273
  20.4 2.2 %collective-permute-start = (bf16[960,128]{1,0:T(8,128)(2,1)}, bf16[960,128]{1,0:T(8,128)(2,1)S(1)}, u32[]{:S(2)}, u32[]{:S(2)}) collective-permute-start(bf16[960,128]{1,0:T(8,128)(2,1)} %get-tuple-element.27), channel_id=1, source_target_pairs={{0,1},{1,0},{2,3},{3,2},{4,5},{5,4},{6,7},{7,6},{8,9},{9,8},{10,11... | collective-permute-start | bytes 737288 | tf_op jit(solution)/shard_map/ppermute | solution.py:267
  22.7 0.0 collective-permute-start.1
  22.7 1.7 %collective-permute-start.2 = (bf16[960,128]{1,0:T(8,128)(2,1)}, bf16[960,128]{1,0:T(8,128)(2,1)S(1)}, u32[]{:S(2)}, u32[]{:S(2)}) collective-permute-start(bf16[960,128]{1,0:T(8,128)(2,1)} %get-tuple-element.29), channel_id=1, source_target_pairs={{0,3},{1,2},{2,1},{3,0},{4,7},{5,6},{6,5},{7,4},{8,11},{9,10},{10,... | collective-permute-start | bytes 737288 | tf_op jit(solution)/shard_map/ppermute | solution.py:267
  24.4 1.1 collective-permute-start.3
  25.5 2.1 %collective-permute-start.4 = (bf16[960,128]{1,0:T(8,128)(2,1)}, bf16[960,128]{1,0:T(8,128)(2,1)S(1)}, u32[]{:S(2)}, u32[]{:S(2)}) collective-permute-start(bf16[960,128]{1,0:T(8,128)(2,1)} %get-tuple-element.31), channel_id=1, source_target_pairs={{0,5},{1,4},{2,7},{3,6},{4,1},{5,0},{6,3},{7,2},{8,13},{9,12},{10,... | collective-permute-start | bytes 737288 | tf_op jit(solution)/shard_map/ppermute | solution.py:267
  27.7 0.0 collective-permute-done.refs_1_
  27.7 0.9 collective-permute-start.5
  28.5 5.0 %collective-permute-done.1.refs_2_ = bf16[960,128]{1,0:T(8,128)(2,1)S(1)} collective-permute-done((bf16[960,128]{1,0:T(8,128)(2,1)}, bf16[960,128]{1,0:T(8,128)(2,1)S(1)}, u32[]{:S(2)}, u32[]{:S(2)}) %collective-permute-start.1) | collective-permute-done | bytes 245792 | tf_op jit(solution)/shard_map/ppermute | solution.py:267
  33.6 2.6 %collective-permute-start.6 = (bf16[960,128]{1,0:T(8,128)(2,1)}, bf16[960,128]{1,0:T(8,128)(2,1)S(1)}, u32[]{:S(2)}, u32[]{:S(2)}) collective-permute-start(bf16[960,128]{1,0:T(8,128)(2,1)} %get-tuple-element.33), channel_id=1, source_target_pairs={{0,7},{1,6},{2,5},{3,4},{4,3},{5,2},{6,1},{7,0},{8,15},{9,14},{10,... | collective-permute-start | bytes 737288 | tf_op jit(solution)/shard_map/ppermute | solution.py:267
  36.1 5.1 %collective-permute-done.2.refs_3_ = bf16[960,128]{1,0:T(8,128)(2,1)S(1)} collective-permute-done((bf16[960,128]{1,0:T(8,128)(2,1)}, bf16[960,128]{1,0:T(8,128)(2,1)S(1)}, u32[]{:S(2)}, u32[]{:S(2)}) %collective-permute-start.2) | collective-permute-done | bytes 245792 | tf_op jit(solution)/shard_map/ppermute | solution.py:267
  41.2 5.4 %collective-permute-done.3.refs_4_ = bf16[960,128]{1,0:T(8,128)(2,1)S(1)} collective-permute-done((bf16[960,128]{1,0:T(8,128)(2,1)}, bf16[960,128]{1,0:T(8,128)(2,1)S(1)}, u32[]{:S(2)}, u32[]{:S(2)}) %collective-permute-start.3) | collective-permute-done | bytes 245792 | tf_op jit(solution)/shard_map/ppermute | solution.py:267
  46.6 5.4 %collective-permute-done.4.refs_5_ = bf16[960,128]{1,0:T(8,128)(2,1)S(1)} collective-permute-done((bf16[960,128]{1,0:T(8,128)(2,1)}, bf16[960,128]{1,0:T(8,128)(2,1)S(1)}, u32[]{:S(2)}, u32[]{:S(2)}) %collective-permute-start.4) | collective-permute-done | bytes 245792 | tf_op jit(solution)/shard_map/ppermute | solution.py:267
  52.0 0.7 copy-done.12
  52.6 0.7 copy-done.15
  53.4 2.2 %collective-permute-done.6.refs_7_ = bf16[960,128]{1,0:T(8,128)(2,1)S(1)} collective-permute-done((bf16[960,128]{1,0:T(8,128)(2,1)}, bf16[960,128]{1,0:T(8,128)(2,1)S(1)}, u32[]{:S(2)}, u32[]{:S(2)}) %collective-permute-start.6) | collective-permute-done | bytes 245792 | tf_op jit(solution)/shard_map/ppermute | solution.py:267
  55.5 0.7 copy-done.18
  56.2 0.0 all-to-all-done
  56.2 0.9 copy-done.13
  57.2 0.9 copy-done.16
  58.1 0.9 copy-done.19
  59.1 2.5 %shard_map.69 = bf16[2560,128]{1,0:T(8,128)(2,1)} custom-call(bf16[2048,128]{1,0:T(8,128)(2,1)S(1)} %bitcast.13, bf16[960,128]{1,0:T(8,128)(2,1)S(1)} %get-tuple-element.26.refs_0_, bf16[960,128]{1,0:T(8,128)(2,1)S(1)} %collective-permute-done.refs_1_, bf16[960,128]{1,0:T(8,128)(2,1)S(1)} %collective-permute-done.1.refs_2_, ...), custom_call_target="tpu_custom_call" | custom-call | flops 805306368 | bytes 4194304 | tf_op jit(solution)/shard_map/pallas_call | solution.py:50
  61.5 10.6 %all-to-all-start.1 = ((bf16[256,5,2,128]{3,2,1,0:T(2,128)(2,1)}), bf16[256,5,2,128]{3,2,1,0:T(2,128)(2,1)S(1)}, u32[]{:S(2)}, u32[]{:S(2)}) async-start(bf16[256,5,2,128]{3,2,1,0:T(2,128)(2,1)} %bitcast.4), calls=%async_computation.1 | async-start | bytes 1310720 | tf_op jit(solution)/shard_map/all_to_all | solution.py:273
  72.1 2.4 %shard_map.70 = (bf16[1024,1024]{1,0:T(8,128)(2,1)}, bf16[1024,1024]{1,0:T(8,128)(2,1)}) custom-call(f32[2,512,128]{2,1,0:T(8,128)S(1)} %copy-done.1), custom_call_target="tpu_custom_call" | custom-call | flops 1048576 | bytes 4194304 | tf_op jit(solution)/shard_map/pallas_call | solution.py:50
  74.5 20.5 %all-to-all-done.1 = bf16[256,5,2,128]{3,2,1,0:T(2,128)(2,1)S(1)} async-done(((bf16[256,5,2,128]{3,2,1,0:T(2,128)(2,1)}), bf16[256,5,2,128]{3,2,1,0:T(2,128)(2,1)S(1)}, u32[]{:S(2)}, u32[]{:S(2)}) %all-to-all-start.1) | async-done | bytes 655392 | tf_op jit(solution)/shard_map/all_to_all | solution.py:273
  95.0 1.6 copy-done.23
  96.7 0.0 copy-start.14
  96.7 1.7 %shard_map.71 = (f32[2,1024,128]{2,1,0:T(8,128)S(1)}, bf16[2048,128]{1,0:T(8,128)(2,1)S(1)}) custom-call(bf16[2560,128]{1,0:T(8,128)(2,1)S(1)} %bitcast.15, bf16[1024,1024]{1,0:T(8,128)(2,1)S(1)} %copy-done.23, f32[2,1024,128]{2,1,0:T(8,128)S(1)} %copy-done.3, f32[1,128]{1,0:T(1,128)S(1)} %bitcast.18), custom_call_target="tpu_custom_call" | custom-call | flops 1073741824 | bytes 4194304 | tf_op jit(solution)/shard_map/pallas_call | solution.py:50
  98.4 25.9 %all_to_all.20 = bf16[256,4,2,128]{3,2,1,0:T(2,128)(2,1)S(1)} all-to-all(bf16[256,4,2,128]{3,2,1,0:T(2,128)(2,1)S(1)} %bitcast.17), channel_id=1, replica_groups=mesh['freq'=32,'rcv'=8] {'rcv','freq'}, dimensions={0} | all-to-all | bytes 1048576 | tf_op jit(solution)/shard_map/all_to_all | solution.py:273
  124.4 2.5 %shard_map.72 = (bf16[2560,128]{1,0:T(8,128)(2,1)}, bf16[8,2,2,48,128]{4,3,2,1,0:T(8,128)(2,1)S(1)}) custom-call(bf16[2048,128]{1,0:T(8,128)(2,1)S(1)} %bitcast.16, bf16[960,128]{1,0:T(8,128)(2,1)S(1)} %get-tuple-element.26.refs_0_, bf16[960,128]{1,0:T(8,128)(2,1)S(1)} %copy-done.5, bf16[960,128]{1,0:T(8,128)(2,1)S(1)} %copy-done.7, ...), custom_call_target="tpu_custom_call" | custom-call | flops 805306368 | bytes 4194304 | tf_op jit(solution)/shard_map/pallas_call | solution.py:50
  126.8 6.5 %all-to-all-start.3 = ((bf16[256,5,2,128]{3,2,1,0:T(2,128)(2,1)}), bf16[256,5,2,128]{3,2,1,0:T(2,128)(2,1)S(1)}, u32[]{:S(2)}, u32[]{:S(2)}) async-start(bf16[256,5,2,128]{3,2,1,0:T(2,128)(2,1)} %bitcast.9), calls=%async_computation.3 | async-start | bytes 1310720 | tf_op jit(solution)/shard_map/all_to_all | solution.py:273
  133.3 0.8 shard_map.74
  134.2 2.4 %collective-permute-start.7 = (bf16[2,2,48,128]{3,2,1,0:T(8,128)(2,1)}, bf16[2,2,48,128]{3,2,1,0:T(8,128)(2,1)S(1)}, u32[]{:S(2)}, u32[]{:S(2)}) collective-permute-start(bf16[2,2,48,128]{3,2,1,0:T(8,128)(2,1)} %get-tuple-element.41), channel_id=1, source_target_pairs={{0,1},{1,0},{2,3},{3,2},{4,5},{5,4},{6,7},{7,6},{8,9},{9,8},{10,11... | collective-permute-start | bytes 147464 | tf_op jit(solution)/shard_map/ppermute | solution.py:267
  136.5 1.7 %collective-permute-start.9 = (bf16[2,2,48,128]{3,2,1,0:T(8,128)(2,1)}, bf16[2,2,48,128]{3,2,1,0:T(8,128)(2,1)S(1)}, u32[]{:S(2)}, u32[]{:S(2)}) collective-permute-start(bf16[2,2,48,128]{3,2,1,0:T(8,128)(2,1)} %get-tuple-element.43), channel_id=1, source_target_pairs={{0,3},{1,2},{2,1},{3,0},{4,7},{5,6},{6,5},{7,4},{8,11},{9,10},{10,... | collective-permute-start | bytes 147464 | tf_op jit(solution)/shard_map/ppermute | solution.py:267
  138.3 1.1 collective-permute-start.10
  139.4 2.1 %collective-permute-start.11 = (bf16[2,2,48,128]{3,2,1,0:T(8,128)(2,1)}, bf16[2,2,48,128]{3,2,1,0:T(8,128)(2,1)S(1)}, u32[]{:S(2)}, u32[]{:S(2)}) collective-permute-start(bf16[2,2,48,128]{3,2,1,0:T(8,128)(2,1)} %get-tuple-element.45), channel_id=1, source_target_pairs={{0,5},{1,4},{2,7},{3,6},{4,1},{5,0},{6,3},{7,2},{8,13},{9,12},{10,... | collective-permute-start | bytes 147464 | tf_op jit(solution)/shard_map/ppermute | solution.py:267
  141.5 0.9 collective-permute-start.12
  142.4 2.1 %collective-permute-start.13 = (bf16[2,2,48,128]{3,2,1,0:T(8,128)(2,1)}, bf16[2,2,48,128]{3,2,1,0:T(8,128)(2,1)S(1)}, u32[]{:S(2)}, u32[]{:S(2)}) collective-permute-start(bf16[2,2,48,128]{3,2,1,0:T(8,128)(2,1)} %get-tuple-element.47), channel_id=1, source_target_pairs={{0,7},{1,6},{2,5},{3,4},{4,3},{5,2},{6,1},{7,0},{8,15},{9,14},{10,... | collective-permute-start | bytes 147464 | tf_op jit(solution)/shard_map/ppermute | solution.py:267
  144.5 0.0 collective-permute-done.9.refs_3_
  144.5 0.0 collective-permute-done.10.refs_4_
  144.5 2.5 %collective-permute-done.11.refs_5_ = bf16[2,2,48,128]{3,2,1,0:T(8,128)(2,1)S(1)} collective-permute-done((bf16[2,2,48,128]{3,2,1,0:T(8,128)(2,1)}, bf16[2,2,48,128]{3,2,1,0:T(8,128)(2,1)S(1)}, u32[]{:S(2)}, u32[]{:S(2)}) %collective-permute-start.11) | collective-permute-done | bytes 49184 | tf_op jit(solution)/shard_map/ppermute | solution.py:267
  147.0 1.9 %collective-permute-done.12.refs_6_ = bf16[2,2,48,128]{3,2,1,0:T(8,128)(2,1)S(1)} collective-permute-done((bf16[2,2,48,128]{3,2,1,0:T(8,128)(2,1)}, bf16[2,2,48,128]{3,2,1,0:T(8,128)(2,1)S(1)}, u32[]{:S(2)}, u32[]{:S(2)}) %collective-permute-start.12) | collective-permute-done | bytes 49184 | tf_op jit(solution)/shard_map/ppermute | solution.py:267
  149.0 1.8 %collective-permute-done.13.refs_7_ = bf16[2,2,48,128]{3,2,1,0:T(8,128)(2,1)S(1)} collective-permute-done((bf16[2,2,48,128]{3,2,1,0:T(8,128)(2,1)}, bf16[2,2,48,128]{3,2,1,0:T(8,128)(2,1)S(1)}, u32[]{:S(2)}, u32[]{:S(2)}) %collective-permute-start.13) | collective-permute-done | bytes 49184 | tf_op jit(solution)/shard_map/ppermute | solution.py:267
  150.8 0.8 copy-done.21
  151.7 1.1 copy.7
  152.7 3.7 %all-to-all-done.3 = bf16[256,5,2,128]{3,2,1,0:T(2,128)(2,1)S(1)} async-done(((bf16[256,5,2,128]{3,2,1,0:T(2,128)(2,1)}), bf16[256,5,2,128]{3,2,1,0:T(2,128)(2,1)S(1)}, u32[]{:S(2)}, u32[]{:S(2)}) %all-to-all-start.3) | async-done | bytes 655392 | tf_op jit(solution)/shard_map/all_to_all | solution.py:273
  156.4 2.7 %shard_map.73 = f32[2,1024,128]{2,1,0:T(8,128)} custom-call(bf16[2560,128]{1,0:T(8,128)(2,1)S(1)} %bitcast.12, bf16[1024,1024]{1,0:T(8,128)(2,1)S(1)} %copy-done, f32[2,1024,128]{2,1,0:T(8,128)} %copy-done.2, f32[1,128]{1,0:T(1,128)S(1)} %bitcast.19), custom_call_target="tpu_custom_call" | custom-call | flops 536870912 | bytes 4194304 | tf_op jit(solution)/shard_map/pallas_call | solution.py:50
  (44 shorter events, 0.1 us)
Async XLA Ops:
  4.8 51.4 %all-to-all-start = ((bf16[256,4,2,128]{3,2,1,0:T(2,128)(2,1)}), bf16[256,4,2,128]{3,2,1,0:T(2,128)(2,1)S(1)}, u32[]{:S(2)}, u32[]{:S(2)}) async-start(bf16[256,4,2,128]{3,2,1,0:T(2,128)(2,1)} %bitcast.2), calls=%async_computation | async-start | bytes 1048576 | tf_op jit(solution)/shard_map/all_to_all | solution.py:273
  20.4 7.2 %collective-permute-start = (bf16[960,128]{1,0:T(8,128)(2,1)}, bf16[960,128]{1,0:T(8,128)(2,1)S(1)}, u32[]{:S(2)}, u32[]{:S(2)}) collective-permute-start(bf16[960,128]{1,0:T(8,128)(2,1)} %get-tuple-element.27), channel_id=1, source_target_pairs={{0,1},{1,0},{2,3},{3,2},{4,5},{5,4},{6,7},{7,6},{8,9},{9,8},{10,11... | collective-permute-start | bytes 737288 | tf_op jit(solution)/shard_map/ppermute | solution.py:267
  22.7 10.9 %collective-permute-start.1 = (bf16[960,128]{1,0:T(8,128)(2,1)}, bf16[960,128]{1,0:T(8,128)(2,1)S(1)}, u32[]{:S(2)}, u32[]{:S(2)}) collective-permute-start(bf16[960,128]{1,0:T(8,128)(2,1)} %get-tuple-element.28), channel_id=1, source_target_pairs={{0,2},{1,3},{2,0},{3,1},{4,6},{5,7},{6,4},{7,5},{8,10},{9,11},{10,... | collective-permute-start | bytes 737288 | tf_op jit(solution)/shard_map/ppermute | solution.py:267
  22.7 18.5 %collective-permute-start.2 = (bf16[960,128]{1,0:T(8,128)(2,1)}, bf16[960,128]{1,0:T(8,128)(2,1)S(1)}, u32[]{:S(2)}, u32[]{:S(2)}) collective-permute-start(bf16[960,128]{1,0:T(8,128)(2,1)} %get-tuple-element.29), channel_id=1, source_target_pairs={{0,3},{1,2},{2,1},{3,0},{4,7},{5,6},{6,5},{7,4},{8,11},{9,10},{10,... | collective-permute-start | bytes 737288 | tf_op jit(solution)/shard_map/ppermute | solution.py:267
  24.4 22.2 %collective-permute-start.3 = (bf16[960,128]{1,0:T(8,128)(2,1)}, bf16[960,128]{1,0:T(8,128)(2,1)S(1)}, u32[]{:S(2)}, u32[]{:S(2)}) collective-permute-start(bf16[960,128]{1,0:T(8,128)(2,1)} %get-tuple-element.30), channel_id=1, source_target_pairs={{0,4},{1,5},{2,6},{3,7},{4,0},{5,1},{6,2},{7,3},{8,12},{9,13},{10,... | collective-permute-start | bytes 737288 | tf_op jit(solution)/shard_map/ppermute | solution.py:267
  25.5 26.4 %collective-permute-start.4 = (bf16[960,128]{1,0:T(8,128)(2,1)}, bf16[960,128]{1,0:T(8,128)(2,1)S(1)}, u32[]{:S(2)}, u32[]{:S(2)}) collective-permute-start(bf16[960,128]{1,0:T(8,128)(2,1)} %get-tuple-element.31), channel_id=1, source_target_pairs={{0,5},{1,4},{2,7},{3,6},{4,1},{5,0},{6,3},{7,2},{8,13},{9,12},{10,... | collective-permute-start | bytes 737288 | tf_op jit(solution)/shard_map/ppermute | solution.py:267
  27.7 33.8 %copy-start.4 = (bf16[960,128]{1,0:T(8,128)(2,1)}, bf16[960,128]{1,0:T(8,128)(2,1)S(1)}, u32[]{:S(2)}) copy-start(bf16[960,128]{1,0:T(8,128)(2,1)S(1)} %collective-permute-done.refs_1_) | copy-start | bytes 737284
  27.7 25.0 %collective-permute-start.5 = (bf16[960,128]{1,0:T(8,128)(2,1)}, bf16[960,128]{1,0:T(8,128)(2,1)S(1)}, u32[]{:S(2)}, u32[]{:S(2)}) collective-permute-start(bf16[960,128]{1,0:T(8,128)(2,1)} %get-tuple-element.32), channel_id=1, source_target_pairs={{0,6},{1,7},{2,4},{3,5},{4,2},{5,3},{6,0},{7,1},{8,14},{9,15},{10,... | collective-permute-start | bytes 737288 | tf_op jit(solution)/shard_map/ppermute | solution.py:267
  33.6 27.9 %copy-start.6 = (bf16[960,128]{1,0:T(8,128)(2,1)}, bf16[960,128]{1,0:T(8,128)(2,1)S(1)}, u32[]{:S(2)}) copy-start(bf16[960,128]{1,0:T(8,128)(2,1)S(1)} %collective-permute-done.1.refs_2_) | copy-start | bytes 737284
  33.6 21.9 %collective-permute-start.6 = (bf16[960,128]{1,0:T(8,128)(2,1)}, bf16[960,128]{1,0:T(8,128)(2,1)S(1)}, u32[]{:S(2)}, u32[]{:S(2)}) collective-permute-start(bf16[960,128]{1,0:T(8,128)(2,1)} %get-tuple-element.33), channel_id=1, source_target_pairs={{0,7},{1,6},{2,5},{3,4},{4,3},{5,2},{6,1},{7,0},{8,15},{9,14},{10,... | collective-permute-start | bytes 737288 | tf_op jit(solution)/shard_map/ppermute | solution.py:267
  41.2 20.3 %copy-start.8 = (bf16[960,128]{1,0:T(8,128)(2,1)}, bf16[960,128]{1,0:T(8,128)(2,1)S(1)}, u32[]{:S(2)}) copy-start(bf16[960,128]{1,0:T(8,128)(2,1)S(1)} %collective-permute-done.2.refs_3_) | copy-start | bytes 737284
  46.6 15.0 %copy-start.10 = (bf16[960,128]{1,0:T(8,128)(2,1)}, bf16[960,128]{1,0:T(8,128)(2,1)S(1)}, u32[]{:S(2)}) copy-start(bf16[960,128]{1,0:T(8,128)(2,1)S(1)} %collective-permute-done.3.refs_4_) | copy-start | bytes 737284
  51.9 0.7 copy-start.12
  52.6 0.7 copy-start.15
  55.5 0.7 copy-start.18
  56.2 0.9 copy-start.13
  57.2 0.9 copy-start.16
  58.1 0.9 copy-start.19
  59.1 13.1 %copy-start.1 = (f32[2,512,128]{2,1,0:T(8,128)S(1)}, f32[2,512,128]{2,1,0:T(8,128)}, u32[]{:S(2)}) copy-start(f32[2,512,128]{2,1,0:T(8,128)} %constant.6.clone.base_ref) | copy-start | bytes 1572868
  59.1 36.0 %copy-start.3 = (f32[2,1024,128]{2,1,0:T(8,128)S(1)}, f32[2,1024,128]{2,1,0:T(8,128)}, u32[]{:S(2)}) copy-start(f32[2,1024,128]{2,1,0:T(8,128)} %primaries_ref.3) | copy-start | bytes 3145732
  59.1 36.0 %copy-start.22 = (f32[128]{0:T(128)S(1)}, f32[128]{0:T(128)}, u32[]{:S(2)}) copy-start(f32[128]{0:T(128)} %param.8) | copy-start | bytes 1540
  61.5 33.5 %all-to-all-start.1 = ((bf16[256,5,2,128]{3,2,1,0:T(2,128)(2,1)}), bf16[256,5,2,128]{3,2,1,0:T(2,128)(2,1)S(1)}, u32[]{:S(2)}, u32[]{:S(2)}) async-start(bf16[256,5,2,128]{3,2,1,0:T(2,128)(2,1)} %bitcast.4), calls=%async_computation.1 | async-start | bytes 1310720 | tf_op jit(solution)/shard_map/all_to_all | solution.py:273
  95.0 1.6 copy-start.23
  96.6 27.7 %copy-start.5 = (bf16[960,128]{1,0:T(8,128)(2,1)S(1)}, bf16[960,128]{1,0:T(8,128)(2,1)}, u32[]{:S(2)}) copy-start(bf16[960,128]{1,0:T(8,128)(2,1)} %copy-done.4) | copy-start | bytes 737284
  96.6 27.7 %copy-start.7 = (bf16[960,128]{1,0:T(8,128)(2,1)S(1)}, bf16[960,128]{1,0:T(8,128)(2,1)}, u32[]{:S(2)}) copy-start(bf16[960,128]{1,0:T(8,128)(2,1)} %copy-done.6) | copy-start | bytes 737284
  96.6 27.7 %copy-start.9 = (bf16[960,128]{1,0:T(8,128)(2,1)S(1)}, bf16[960,128]{1,0:T(8,128)(2,1)}, u32[]{:S(2)}) copy-start(bf16[960,128]{1,0:T(8,128)(2,1)} %copy-done.8) | copy-start | bytes 737284
  96.6 27.7 %copy-start.11 = (bf16[960,128]{1,0:T(8,128)(2,1)S(1)}, bf16[960,128]{1,0:T(8,128)(2,1)}, u32[]{:S(2)}) copy-start(bf16[960,128]{1,0:T(8,128)(2,1)} %copy-done.10) | copy-start | bytes 737284
  96.7 27.7 %copy-start.14 = (bf16[960,128]{1,0:T(8,128)(2,1)S(1)}, bf16[960,128]{1,0:T(8,128)(2,1)}, u32[]{:S(2)}) copy-start(bf16[960,128]{1,0:T(8,128)(2,1)} %copy-done.12) | copy-start | bytes 737284
  96.7 27.7 %copy-start.17 = (bf16[960,128]{1,0:T(8,128)(2,1)S(1)}, bf16[960,128]{1,0:T(8,128)(2,1)}, u32[]{:S(2)}) copy-start(bf16[960,128]{1,0:T(8,128)(2,1)} %copy-done.15) | copy-start | bytes 737284
  96.7 27.7 %copy-start.20 = (bf16[960,128]{1,0:T(8,128)(2,1)S(1)}, bf16[960,128]{1,0:T(8,128)(2,1)}, u32[]{:S(2)}) copy-start(bf16[960,128]{1,0:T(8,128)(2,1)} %copy-done.18) | copy-start | bytes 737284
  98.4 25.9 %copy-start.2 = (f32[2,1024,128]{2,1,0:T(8,128)}, f32[2,1024,128]{2,1,0:T(8,128)S(1)}, u32[]{:S(2)}) copy-start(f32[2,1024,128]{2,1,0:T(8,128)S(1)} %get-tuple-element.38.primaries_ref) | copy-start | bytes 3145732
  126.8 29.6 %copy-start = (bf16[1024,1024]{1,0:T(8,128)(2,1)S(1)}, bf16[1024,1024]{1,0:T(8,128)(2,1)}, u32[]{:S(2)}) copy-start(bf16[1024,1024]{1,0:T(8,128)(2,1)} %get-tuple-element.37.table_ref) | copy-start | bytes 6291460
  126.8 29.6 %all-to-all-start.3 = ((bf16[256,5,2,128]{3,2,1,0:T(2,128)(2,1)}), bf16[256,5,2,128]{3,2,1,0:T(2,128)(2,1)S(1)}, u32[]{:S(2)}, u32[]{:S(2)}) async-start(bf16[256,5,2,128]{3,2,1,0:T(2,128)(2,1)} %bitcast.9), calls=%async_computation.3 | async-start | bytes 1310720 | tf_op jit(solution)/shard_map/all_to_all | solution.py:273
  134.2 7.4 %collective-permute-start.7 = (bf16[2,2,48,128]{3,2,1,0:T(8,128)(2,1)}, bf16[2,2,48,128]{3,2,1,0:T(8,128)(2,1)S(1)}, u32[]{:S(2)}, u32[]{:S(2)}) collective-permute-start(bf16[2,2,48,128]{3,2,1,0:T(8,128)(2,1)} %get-tuple-element.41), channel_id=1, source_target_pairs={{0,1},{1,0},{2,3},{3,2},{4,5},{5,4},{6,7},{7,6},{8,9},{9,8},{10,11... | collective-permute-start | bytes 147464 | tf_op jit(solution)/shard_map/ppermute | solution.py:267
  136.5 5.9 %collective-permute-start.8 = (bf16[2,2,48,128]{3,2,1,0:T(8,128)(2,1)}, bf16[2,2,48,128]{3,2,1,0:T(8,128)(2,1)S(1)}, u32[]{:S(2)}, u32[]{:S(2)}) collective-permute-start(bf16[2,2,48,128]{3,2,1,0:T(8,128)(2,1)} %get-tuple-element.42), channel_id=1, source_target_pairs={{0,2},{1,3},{2,0},{3,1},{4,6},{5,7},{6,4},{7,5},{8,10},{9,11},{10,... | collective-permute-start | bytes 147464 | tf_op jit(solution)/shard_map/ppermute | solution.py:267
  136.5 7.9 %collective-permute-start.9 = (bf16[2,2,48,128]{3,2,1,0:T(8,128)(2,1)}, bf16[2,2,48,128]{3,2,1,0:T(8,128)(2,1)S(1)}, u32[]{:S(2)}, u32[]{:S(2)}) collective-permute-start(bf16[2,2,48,128]{3,2,1,0:T(8,128)(2,1)} %get-tuple-element.43), channel_id=1, source_target_pairs={{0,3},{1,2},{2,1},{3,0},{4,7},{5,6},{6,5},{7,4},{8,11},{9,10},{10,... | collective-permute-start | bytes 147464 | tf_op jit(solution)/shard_map/ppermute | solution.py:267
  138.3 6.3 %collective-permute-start.10 = (bf16[2,2,48,128]{3,2,1,0:T(8,128)(2,1)}, bf16[2,2,48,128]{3,2,1,0:T(8,128)(2,1)S(1)}, u32[]{:S(2)}, u32[]{:S(2)}) collective-permute-start(bf16[2,2,48,128]{3,2,1,0:T(8,128)(2,1)} %get-tuple-element.44), channel_id=1, source_target_pairs={{0,4},{1,5},{2,6},{3,7},{4,0},{5,1},{6,2},{7,3},{8,12},{9,13},{10,... | collective-permute-start | bytes 147464 | tf_op jit(solution)/shard_map/ppermute | solution.py:267
  139.4 7.7 %collective-permute-start.11 = (bf16[2,2,48,128]{3,2,1,0:T(8,128)(2,1)}, bf16[2,2,48,128]{3,2,1,0:T(8,128)(2,1)S(1)}, u32[]{:S(2)}, u32[]{:S(2)}) collective-permute-start(bf16[2,2,48,128]{3,2,1,0:T(8,128)(2,1)} %get-tuple-element.45), channel_id=1, source_target_pairs={{0,5},{1,4},{2,7},{3,6},{4,1},{5,0},{6,3},{7,2},{8,13},{9,12},{10,... | collective-permute-start | bytes 147464 | tf_op jit(solution)/shard_map/ppermute | solution.py:267
  141.5 7.4 %collective-permute-start.12 = (bf16[2,2,48,128]{3,2,1,0:T(8,128)(2,1)}, bf16[2,2,48,128]{3,2,1,0:T(8,128)(2,1)S(1)}, u32[]{:S(2)}, u32[]{:S(2)}) collective-permute-start(bf16[2,2,48,128]{3,2,1,0:T(8,128)(2,1)} %get-tuple-element.46), channel_id=1, source_target_pairs={{0,6},{1,7},{2,4},{3,5},{4,2},{5,3},{6,0},{7,1},{8,14},{9,15},{10,... | collective-permute-start | bytes 147464 | tf_op jit(solution)/shard_map/ppermute | solution.py:267
  142.4 8.4 %collective-permute-start.13 = (bf16[2,2,48,128]{3,2,1,0:T(8,128)(2,1)}, bf16[2,2,48,128]{3,2,1,0:T(8,128)(2,1)S(1)}, u32[]{:S(2)}, u32[]{:S(2)}) collective-permute-start(bf16[2,2,48,128]{3,2,1,0:T(8,128)(2,1)} %get-tuple-element.47), channel_id=1, source_target_pairs={{0,7},{1,6},{2,5},{3,4},{4,3},{5,2},{6,1},{7,0},{8,15},{9,14},{10,... | collective-permute-start | bytes 147464 | tf_op jit(solution)/shard_map/ppermute | solution.py:267
  150.8 0.8 copy-start.21

commit v6 on v5

--- a/solution.py
+++ b/solution.py
@@ -68,25 +68,29 @@
 
 def start_kernel(owners, blocks, me_ref, op_ref, data_ref, primaries_ref, base_ref, *refs):
     pieces, spectra_ref = refs[:blocks], refs[blocks]
-    op_held, data_held, data_rows, piece_held, traces_ref, angles_ref, table_ref, rows_ref, sem = refs[blocks + 1:]
+    op_held, data_held, data_rows, piece_held, traces_ref, angles_ref, table_ref, rows_ref, low_ref, sem = refs[blocks + 1:]
     frequencies = 2 * blocks
     rows = data_ref.shape[0] // (2 * frequencies)
     part = PARTS * rows
     fetches = [
         pltpu.make_async_copy(source, target, sem.at[blocks + place])
         for place, (source, target) in enumerate(
-            ((base_ref, angles_ref), (data_ref, data_held), (op_ref, op_held), (primaries_ref, traces_ref))
+            ((base_ref, angles_ref), (primaries_ref, traces_ref), (data_ref, data_held), (op_ref, op_held))
         )
     ]
-    fetch_base, fetch_data, fetch_op, fetch_traces = fetches
+    fetch_base, fetch_traces, fetch_data, fetch_op = fetches
     for fetch in fetches:
         fetch.start()
     fetch_base.wait()
     fill_table(angles_ref, table_ref, owners, blocks)
+    fetch_traces.wait()
+    low = jnp.concatenate([traces_ref[0].astype(jnp.bfloat16), traces_ref[1].astype(jnp.bfloat16)], axis=1)
+    transform(table_ref, low, rows_ref, low_ref, owners)
+    stores = [pltpu.make_async_copy(low_ref, spectra_ref, sem.at[0])]
+    stores[0].start()
     fetch_data.wait()
     data_rows[...] = data_held[...].astype(jnp.float32)
     fetch_op.wait()
-    stores = []
     for place in EARLY + (0,):
         owner = me_ref[0] ^ place
         target = piece_held.at[place] if place else pieces[0]
@@ -99,9 +103,6 @@
         if place:
             stores.append(pltpu.make_async_copy(target, pieces[place], sem.at[place]))
             stores[-1].start()
-    fetch_traces.wait()
-    low = jnp.concatenate([traces_ref[0].astype(jnp.bfloat16), traces_ref[1].astype(jnp.bfloat16)], axis=1)
-    transform(table_ref, low, rows_ref, spectra_ref, owners)
     for store in stores:
         store.wait()
 
@@ -182,12 +183,15 @@
         sides.append(jnp.concatenate(pieces, axis=0))
     direction = jnp.concatenate(sides, axis=1)
     block = T_SIZE // 4
-    for start in range(0, T_SIZE, block):
-        change = lax.dot_general(
+    changes = [
+        lax.dot_general(
             table_ref[:, pl.ds(start, block)], direction, (((0,), (0,)), ((), ())), preferred_element_type=jnp.float32
         )
-        if fetch and not start:
-            fetch.wait()
+        for start in range(0, T_SIZE, block)
+    ]
+    if fetch:
+        fetch.wait()
+    for start, change in zip(range(0, T_SIZE, block), changes):
         news = []
         for point in range(2):
             moved = held_ref[point, pl.ds(start, block), :] + step_size * change[:, point * S:(point + 1) * S]
@@ -291,7 +295,7 @@
         functools.partial(start_kernel, devices, rcv_parts),
         [jax.ShapeDtypeStruct(piece, bf16)]
         + [pltpu.HBM(piece, bf16)] * (rcv_parts - 1)
-        + [jax.ShapeDtypeStruct(half, bf16)],
+        + [pltpu.HBM(half, bf16)],
         [
             pltpu.VMEM(surface_operator.shape, bf16),
             pltpu.VMEM(recorded.shape, bf16),
@@ -301,12 +305,13 @@
             pltpu.VMEM(base.shape, f32),
             table,
             rows_half,
+            pltpu.VMEM(half, bf16),
             pltpu.SemaphoreType.DMA((rcv_parts + 4,)),
         ],
         (me, *(pltpu.with_memory_space_constraint(array, pltpu.HBM) for array in arrays)),
         2 * 1024 * 1024 * 256,
         [pltpu.SMEM] + [pltpu.HBM] * 4,
-        [pltpu.VMEM] + [pltpu.HBM] * (rcv_parts - 1) + [pltpu.VMEM],
+        [pltpu.VMEM] + [pltpu.HBM] * rcv_parts,
     )
     pieces = trade(pieces)
     tables = call(

time: 160 us -> 159 us (level)
  no operation moved by 1% of the time
where the time goes in v6:
time: 159 us; the launch traced here: 158 us
  starting transfers between devices  53.7 us (34%)
  waiting for transfers between devices  53.6 us (34%)
  blocking collectives  25.9 us (16%)
  Pallas kernels  15.9 us (10%)
  local copies, waits for them, and re-layouts  8.42 us (5%)
    all_to_all x3, starting transfers between devices, exchange(): lax.all_to_all(pairs, ALL, split_axis=0, concat_axis=0, tiled=True)  32.7 us
    ppermute x14, waiting for transfers between devices, trade(): lax.ppermute(pieces[place], 'rcv', [(source, source ^ place) for source i...  29.4 us
    all_to_all x1, blocking collectives, exchange(): lax.all_to_all(pairs, ALL, split_axis=0, concat_axis=0, tiled=True)  25.9 us
    all_to_all x3, waiting for transfers between devices, exchange(): lax.all_to_all(pairs, ALL, split_axis=0, concat_axis=0, tiled=True)  24.2 us
    ppermute x14, starting transfers between devices, trade(): lax.ppermute(pieces[place], 'rcv', [(source, source ^ place) for source i...  21 us
    pallas_call x7, Pallas kernels, call(): pl.pallas_call(kernel, out_shape=out_shape, in_specs=[pl.BlockSpec(memory...  15.9 us
    unnamed x49, local copies, waits for them, and re-layouts  8.42 us
  transfers between devices with their start and end apart: 17, of which 10 were waited for; matrix products, arithmetic and copies ran while one was open for 1% of the time, Pallas kernels for 2%

profile of v6, /device:TPU:1, one launch (start us, length us, event | category | flops | bytes accessed | tf_op | source)
XLA Modules:
  0.0 158.5 jit_solution(17192769689585538104)
XLA Ops:
  0.6 3.7 %shard_map.68 = (bf16[960,128]{1,0:T(8,128)(2,1)S(1)}, bf16[960,128]{1,0:T(8,128)(2,1)}, bf16[960,128]{1,0:T(8,128)(2,1)}, bf16[960,128]{1,0:T(8,128)(2,1)}, bf1...) custom-call(s32[1]{0:T(128)} %bitcast.me_ref, ...), custom_call_target="tpu_custom_call" | custom-call | flops 536870912 | bytes 4194304 | tf_op jit(solution)/shard_map/pallas_call | solution.py:50
  4.4 15.6 %all-to-all-start = ((bf16[256,4,2,128]{3,2,1,0:T(2,128)(2,1)}), bf16[256,4,2,128]{3,2,1,0:T(2,128)(2,1)S(1)}, u32[]{:S(2)}, u32[]{:S(2)}) async-start(bf16[256,4,2,128]{3,2,1,0:T(2,128)(2,1)} %bitcast.20), calls=%async_computation | async-start | bytes 1048576 | tf_op jit(solution)/shard_map/all_to_all | solution.py:277
  20.0 2.2 %collective-permute-start = (bf16[960,128]{1,0:T(8,128)(2,1)}, bf16[960,128]{1,0:T(8,128)(2,1)S(1)}, u32[]{:S(2)}, u32[]{:S(2)}) collective-permute-start(bf16[960,128]{1,0:T(8,128)(2,1)} %get-tuple-element.27), channel_id=1, source_target_pairs={{0,1},{1,0},{2,3},{3,2},{4,5},{5,4},{6,7},{7,6},{8,9},{9,8},{10,11... | collective-permute-start | bytes 737288 | tf_op jit(solution)/shard_map/ppermute | solution.py:271
  22.2 0.0 collective-permute-start.1
  22.3 1.7 %collective-permute-start.2 = (bf16[960,128]{1,0:T(8,128)(2,1)}, bf16[960,128]{1,0:T(8,128)(2,1)S(1)}, u32[]{:S(2)}, u32[]{:S(2)}) collective-permute-start(bf16[960,128]{1,0:T(8,128)(2,1)} %get-tuple-element.29), channel_id=1, source_target_pairs={{0,3},{1,2},{2,1},{3,0},{4,7},{5,6},{6,5},{7,4},{8,11},{9,10},{10,... | collective-permute-start | bytes 737288 | tf_op jit(solution)/shard_map/ppermute | solution.py:271
  24.0 1.1 collective-permute-start.3
  25.1 2.1 %collective-permute-start.4 = (bf16[960,128]{1,0:T(8,128)(2,1)}, bf16[960,128]{1,0:T(8,128)(2,1)S(1)}, u32[]{:S(2)}, u32[]{:S(2)}) collective-permute-start(bf16[960,128]{1,0:T(8,128)(2,1)} %get-tuple-element.31), channel_id=1, source_target_pairs={{0,5},{1,4},{2,7},{3,6},{4,1},{5,0},{6,3},{7,2},{8,13},{9,12},{10,... | collective-permute-start | bytes 737288 | tf_op jit(solution)/shard_map/ppermute | solution.py:271
  27.2 0.0 collective-permute-done.refs_1_
  27.3 0.9 collective-permute-start.5
  28.1 5.0 %collective-permute-done.1.refs_2_ = bf16[960,128]{1,0:T(8,128)(2,1)S(1)} collective-permute-done((bf16[960,128]{1,0:T(8,128)(2,1)}, bf16[960,128]{1,0:T(8,128)(2,1)S(1)}, u32[]{:S(2)}, u32[]{:S(2)}) %collective-permute-start.1) | collective-permute-done | bytes 245792 | tf_op jit(solution)/shard_map/ppermute | solution.py:271
  33.2 2.6 %collective-permute-start.6 = (bf16[960,128]{1,0:T(8,128)(2,1)}, bf16[960,128]{1,0:T(8,128)(2,1)S(1)}, u32[]{:S(2)}, u32[]{:S(2)}) collective-permute-start(bf16[960,128]{1,0:T(8,128)(2,1)} %get-tuple-element.33), channel_id=1, source_target_pairs={{0,7},{1,6},{2,5},{3,4},{4,3},{5,2},{6,1},{7,0},{8,15},{9,14},{10,... | collective-permute-start | bytes 737288 | tf_op jit(solution)/shard_map/ppermute | solution.py:271
  35.7 5.1 %collective-permute-done.2.refs_3_ = bf16[960,128]{1,0:T(8,128)(2,1)S(1)} collective-permute-done((bf16[960,128]{1,0:T(8,128)(2,1)}, bf16[960,128]{1,0:T(8,128)(2,1)S(1)}, u32[]{:S(2)}, u32[]{:S(2)}) %collective-permute-start.2) | collective-permute-done | bytes 245792 | tf_op jit(solution)/shard_map/ppermute | solution.py:271
  40.8 5.4 %collective-permute-done.3.refs_4_ = bf16[960,128]{1,0:T(8,128)(2,1)S(1)} collective-permute-done((bf16[960,128]{1,0:T(8,128)(2,1)}, bf16[960,128]{1,0:T(8,128)(2,1)S(1)}, u32[]{:S(2)}, u32[]{:S(2)}) %collective-permute-start.3) | collective-permute-done | bytes 245792 | tf_op jit(solution)/shard_map/ppermute | solution.py:271
  46.1 5.4 %collective-permute-done.4.refs_5_ = bf16[960,128]{1,0:T(8,128)(2,1)S(1)} collective-permute-done((bf16[960,128]{1,0:T(8,128)(2,1)}, bf16[960,128]{1,0:T(8,128)(2,1)S(1)}, u32[]{:S(2)}, u32[]{:S(2)}) %collective-permute-start.4) | collective-permute-done | bytes 245792 | tf_op jit(solution)/shard_map/ppermute | solution.py:271
  51.5 0.7 copy-done.12
  52.2 0.0 collective-permute-done.5.refs_6_
  52.2 0.7 copy-done.15
  52.9 2.2 %collective-permute-done.6.refs_7_ = bf16[960,128]{1,0:T(8,128)(2,1)S(1)} collective-permute-done((bf16[960,128]{1,0:T(8,128)(2,1)}, bf16[960,128]{1,0:T(8,128)(2,1)S(1)}, u32[]{:S(2)}, u32[]{:S(2)}) %collective-permute-start.6) | collective-permute-done | bytes 245792 | tf_op jit(solution)/shard_map/ppermute | solution.py:271
  55.1 0.7 copy-done.18
  55.8 0.9 copy-done.13
  56.7 0.9 copy-done.16
  57.7 0.9 copy-done.19
  58.6 2.5 %shard_map.69 = bf16[2560,128]{1,0:T(8,128)(2,1)} custom-call(bf16[2048,128]{1,0:T(8,128)(2,1)S(1)} %bitcast.13, bf16[960,128]{1,0:T(8,128)(2,1)S(1)} %get-tuple-element.26.refs_0_, bf16[960,128]{1,0:T(8,128)(2,1)S(1)} %collective-permute-done.refs_1_, bf16[960,128]{1,0:T(8,128)(2,1)S(1)} %collective-permute-done.1.refs_2_, ...), custom_call_target="tpu_custom_call" | custom-call | flops 805306368 | bytes 4194304 | tf_op jit(solution)/shard_map/pallas_call | solution.py:50
  61.1 10.6 %all-to-all-start.1 = ((bf16[256,5,2,128]{3,2,1,0:T(2,128)(2,1)}), bf16[256,5,2,128]{3,2,1,0:T(2,128)(2,1)S(1)}, u32[]{:S(2)}, u32[]{:S(2)}) async-start(bf16[256,5,2,128]{3,2,1,0:T(2,128)(2,1)} %bitcast.4), calls=%async_computation.1 | async-start | bytes 1310720 | tf_op jit(solution)/shard_map/all_to_all | solution.py:277
  71.7 2.4 %shard_map.70 = (bf16[1024,1024]{1,0:T(8,128)(2,1)}, bf16[1024,1024]{1,0:T(8,128)(2,1)}) custom-call(f32[2,512,128]{2,1,0:T(8,128)S(1)} %copy-done.1), custom_call_target="tpu_custom_call" | custom-call | flops 1048576 | bytes 4194304 | tf_op jit(solution)/shard_map/pallas_call | solution.py:50
  74.1 20.5 %all-to-all-done.1 = bf16[256,5,2,128]{3,2,1,0:T(2,128)(2,1)S(1)} async-done(((bf16[256,5,2,128]{3,2,1,0:T(2,128)(2,1)}), bf16[256,5,2,128]{3,2,1,0:T(2,128)(2,1)S(1)}, u32[]{:S(2)}, u32[]{:S(2)}) %all-to-all-start.1) | async-done | bytes 655392 | tf_op jit(solution)/shard_map/all_to_all | solution.py:277
  94.6 1.6 %copy-done.23 = bf16[1024,1024]{1,0:T(8,128)(2,1)S(1)} copy-done((bf16[1024,1024]{1,0:T(8,128)(2,1)S(1)}, bf16[1024,1024]{1,0:T(8,128)(2,1)}, u32[]{:S(2)}) %copy-start.23) | copy-done | bytes 2097176
  96.2 0.0 copy-start.14
  96.3 1.8 %shard_map.71 = (f32[2,1024,128]{2,1,0:T(8,128)S(1)}, bf16[2048,128]{1,0:T(8,128)(2,1)S(1)}) custom-call(bf16[2560,128]{1,0:T(8,128)(2,1)S(1)} %bitcast.15, bf16[1024,1024]{1,0:T(8,128)(2,1)S(1)} %copy-done.23, f32[2,1024,128]{2,1,0:T(8,128)S(1)} %copy-done.3, f32[1,128]{1,0:T(1,128)S(1)} %bitcast.18), custom_call_target="tpu_custom_call" | custom-call | flops 1073741824 | bytes 4194304 | tf_op jit(solution)/shard_map/pallas_call | solution.py:50
  98.0 25.9 %all_to_all.20 = bf16[256,4,2,128]{3,2,1,0:T(2,128)(2,1)S(1)} all-to-all(bf16[256,4,2,128]{3,2,1,0:T(2,128)(2,1)S(1)} %bitcast.17), channel_id=1, replica_groups=mesh['freq'=32,'rcv'=8] {'rcv','freq'}, dimensions={0} | all-to-all | bytes 1048576 | tf_op jit(solution)/shard_map/all_to_all | solution.py:277
  124.0 2.5 %shard_map.72 = (bf16[2560,128]{1,0:T(8,128)(2,1)}, bf16[8,2,2,48,128]{4,3,2,1,0:T(8,128)(2,1)S(1)}) custom-call(bf16[2048,128]{1,0:T(8,128)(2,1)S(1)} %bitcast.16, bf16[960,128]{1,0:T(8,128)(2,1)S(1)} %get-tuple-element.26.refs_0_, bf16[960,128]{1,0:T(8,128)(2,1)S(1)} %copy-done.5, bf16[960,128]{1,0:T(8,128)(2,1)S(1)} %copy-done.7, ...), custom_call_target="tpu_custom_call" | custom-call | flops 805306368 | bytes 4194304 | tf_op jit(solution)/shard_map/pallas_call | solution.py:50
  126.5 6.5 %all-to-all-start.3 = ((bf16[256,5,2,128]{3,2,1,0:T(2,128)(2,1)}), bf16[256,5,2,128]{3,2,1,0:T(2,128)(2,1)S(1)}, u32[]{:S(2)}, u32[]{:S(2)}) async-start(bf16[256,5,2,128]{3,2,1,0:T(2,128)(2,1)} %bitcast.9), calls=%async_computation.3 | async-start | bytes 1310720 | tf_op jit(solution)/shard_map/all_to_all | solution.py:277
  133.0 0.8 shard_map.74
  133.8 2.4 %collective-permute-start.7 = (bf16[2,2,48,128]{3,2,1,0:T(8,128)(2,1)}, bf16[2,2,48,128]{3,2,1,0:T(8,128)(2,1)S(1)}, u32[]{:S(2)}, u32[]{:S(2)}) collective-permute-start(bf16[2,2,48,128]{3,2,1,0:T(8,128)(2,1)} %get-tuple-element.41), channel_id=1, source_target_pairs={{0,1},{1,0},{2,3},{3,2},{4,5},{5,4},{6,7},{7,6},{8,9},{9,8},{10,11... | collective-permute-start | bytes 147464 | tf_op jit(solution)/shard_map/ppermute | solution.py:271
  136.2 1.7 %collective-permute-start.9 = (bf16[2,2,48,128]{3,2,1,0:T(8,128)(2,1)}, bf16[2,2,48,128]{3,2,1,0:T(8,128)(2,1)S(1)}, u32[]{:S(2)}, u32[]{:S(2)}) collective-permute-start(bf16[2,2,48,128]{3,2,1,0:T(8,128)(2,1)} %get-tuple-element.43), channel_id=1, source_target_pairs={{0,3},{1,2},{2,1},{3,0},{4,7},{5,6},{6,5},{7,4},{8,11},{9,10},{10,... | collective-permute-start | bytes 147464 | tf_op jit(solution)/shard_map/ppermute | solution.py:271
  137.9 1.1 collective-permute-start.10
  139.0 2.1 %collective-permute-start.11 = (bf16[2,2,48,128]{3,2,1,0:T(8,128)(2,1)}, bf16[2,2,48,128]{3,2,1,0:T(8,128)(2,1)S(1)}, u32[]{:S(2)}, u32[]{:S(2)}) collective-permute-start(bf16[2,2,48,128]{3,2,1,0:T(8,128)(2,1)} %get-tuple-element.45), channel_id=1, source_target_pairs={{0,5},{1,4},{2,7},{3,6},{4,1},{5,0},{6,3},{7,2},{8,13},{9,12},{10,... | collective-permute-start | bytes 147464 | tf_op jit(solution)/shard_map/ppermute | solution.py:271
  141.2 0.9 collective-permute-start.12
  142.0 2.1 %collective-permute-start.13 = (bf16[2,2,48,128]{3,2,1,0:T(8,128)(2,1)}, bf16[2,2,48,128]{3,2,1,0:T(8,128)(2,1)S(1)}, u32[]{:S(2)}, u32[]{:S(2)}) collective-permute-start(bf16[2,2,48,128]{3,2,1,0:T(8,128)(2,1)} %get-tuple-element.47), channel_id=1, source_target_pairs={{0,7},{1,6},{2,5},{3,4},{4,3},{5,2},{6,1},{7,0},{8,15},{9,14},{10,... | collective-permute-start | bytes 147464 | tf_op jit(solution)/shard_map/ppermute | solution.py:271
  144.1 0.0 collective-permute-done.9.refs_3_
  144.1 0.0 collective-permute-done.10.refs_4_
  144.2 2.5 %collective-permute-done.11.refs_5_ = bf16[2,2,48,128]{3,2,1,0:T(8,128)(2,1)S(1)} collective-permute-done((bf16[2,2,48,128]{3,2,1,0:T(8,128)(2,1)}, bf16[2,2,48,128]{3,2,1,0:T(8,128)(2,1)S(1)}, u32[]{:S(2)}, u32[]{:S(2)}) %collective-permute-start.11) | collective-permute-done | bytes 49184 | tf_op jit(solution)/shard_map/ppermute | solution.py:271
  146.7 1.9 %collective-permute-done.12.refs_6_ = bf16[2,2,48,128]{3,2,1,0:T(8,128)(2,1)S(1)} collective-permute-done((bf16[2,2,48,128]{3,2,1,0:T(8,128)(2,1)}, bf16[2,2,48,128]{3,2,1,0:T(8,128)(2,1)S(1)}, u32[]{:S(2)}, u32[]{:S(2)}) %collective-permute-start.12) | collective-permute-done | bytes 49184 | tf_op jit(solution)/shard_map/ppermute | solution.py:271
  148.6 1.8 %collective-permute-done.13.refs_7_ = bf16[2,2,48,128]{3,2,1,0:T(8,128)(2,1)S(1)} collective-permute-done((bf16[2,2,48,128]{3,2,1,0:T(8,128)(2,1)}, bf16[2,2,48,128]{3,2,1,0:T(8,128)(2,1)S(1)}, u32[]{:S(2)}, u32[]{:S(2)}) %collective-permute-start.13) | collective-permute-done | bytes 49184 | tf_op jit(solution)/shard_map/ppermute | solution.py:271
  150.5 0.8 copy-done.21
  151.3 1.1 copy.7
  152.3 3.7 %all-to-all-done.3 = bf16[256,5,2,128]{3,2,1,0:T(2,128)(2,1)S(1)} async-done(((bf16[256,5,2,128]{3,2,1,0:T(2,128)(2,1)}), bf16[256,5,2,128]{3,2,1,0:T(2,128)(2,1)S(1)}, u32[]{:S(2)}, u32[]{:S(2)}) %all-to-all-start.3) | async-done | bytes 655392 | tf_op jit(solution)/shard_map/all_to_all | solution.py:277
  156.0 2.3 %shard_map.73 = f32[2,1024,128]{2,1,0:T(8,128)} custom-call(bf16[2560,128]{1,0:T(8,128)(2,1)S(1)} %bitcast.12, bf16[1024,1024]{1,0:T(8,128)(2,1)S(1)} %copy-done, f32[2,1024,128]{2,1,0:T(8,128)} %copy-done.2, f32[1,128]{1,0:T(1,128)S(1)} %bitcast.19), custom_call_target="tpu_custom_call" | custom-call | flops 536870912 | bytes 4194304 | tf_op jit(solution)/shard_map/pallas_call | solution.py:50
  (44 shorter events, 0.1 us)
Async XLA Ops:
  4.4 51.4 %all-to-all-start = ((bf16[256,4,2,128]{3,2,1,0:T(2,128)(2,1)}), bf16[256,4,2,128]{3,2,1,0:T(2,128)(2,1)S(1)}, u32[]{:S(2)}, u32[]{:S(2)}) async-start(bf16[256,4,2,128]{3,2,1,0:T(2,128)(2,1)} %bitcast.20), calls=%async_computation | async-start | bytes 1048576 | tf_op jit(solution)/shard_map/all_to_all | solution.py:277
  20.0 7.2 %collective-permute-start = (bf16[960,128]{1,0:T(8,128)(2,1)}, bf16[960,128]{1,0:T(8,128)(2,1)S(1)}, u32[]{:S(2)}, u32[]{:S(2)}) collective-permute-start(bf16[960,128]{1,0:T(8,128)(2,1)} %get-tuple-element.27), channel_id=1, source_target_pairs={{0,1},{1,0},{2,3},{3,2},{4,5},{5,4},{6,7},{7,6},{8,9},{9,8},{10,11... | collective-permute-start | bytes 737288 | tf_op jit(solution)/shard_map/ppermute | solution.py:271
  22.2 10.9 %collective-permute-start.1 = (bf16[960,128]{1,0:T(8,128)(2,1)}, bf16[960,128]{1,0:T(8,128)(2,1)S(1)}, u32[]{:S(2)}, u32[]{:S(2)}) collective-permute-start(bf16[960,128]{1,0:T(8,128)(2,1)} %get-tuple-element.28), channel_id=1, source_target_pairs={{0,2},{1,3},{2,0},{3,1},{4,6},{5,7},{6,4},{7,5},{8,10},{9,11},{10,... | collective-permute-start | bytes 737288 | tf_op jit(solution)/shard_map/ppermute | solution.py:271
  22.3 18.5 %collective-permute-start.2 = (bf16[960,128]{1,0:T(8,128)(2,1)}, bf16[960,128]{1,0:T(8,128)(2,1)S(1)}, u32[]{:S(2)}, u32[]{:S(2)}) collective-permute-start(bf16[960,128]{1,0:T(8,128)(2,1)} %get-tuple-element.29), channel_id=1, source_target_pairs={{0,3},{1,2},{2,1},{3,0},{4,7},{5,6},{6,5},{7,4},{8,11},{9,10},{10,... | collective-permute-start | bytes 737288 | tf_op jit(solution)/shard_map/ppermute | solution.py:271
  24.0 22.2 %collective-permute-start.3 = (bf16[960,128]{1,0:T(8,128)(2,1)}, bf16[960,128]{1,0:T(8,128)(2,1)S(1)}, u32[]{:S(2)}, u32[]{:S(2)}) collective-permute-start(bf16[960,128]{1,0:T(8,128)(2,1)} %get-tuple-element.30), channel_id=1, source_target_pairs={{0,4},{1,5},{2,6},{3,7},{4,0},{5,1},{6,2},{7,3},{8,12},{9,13},{10,... | collective-permute-start | bytes 737288 | tf_op jit(solution)/shard_map/ppermute | solution.py:271
  25.1 26.4 %collective-permute-start.4 = (bf16[960,128]{1,0:T(8,128)(2,1)}, bf16[960,128]{1,0:T(8,128)(2,1)S(1)}, u32[]{:S(2)}, u32[]{:S(2)}) collective-permute-start(bf16[960,128]{1,0:T(8,128)(2,1)} %get-tuple-element.31), channel_id=1, source_target_pairs={{0,5},{1,4},{2,7},{3,6},{4,1},{5,0},{6,3},{7,2},{8,13},{9,12},{10,... | collective-permute-start | bytes 737288 | tf_op jit(solution)/shard_map/ppermute | solution.py:271
  27.2 33.9 %copy-start.4 = (bf16[960,128]{1,0:T(8,128)(2,1)}, bf16[960,128]{1,0:T(8,128)(2,1)S(1)}, u32[]{:S(2)}) copy-start(bf16[960,128]{1,0:T(8,128)(2,1)S(1)} %collective-permute-done.refs_1_) | copy-start | bytes 737284
  27.3 25.0 %collective-permute-start.5 = (bf16[960,128]{1,0:T(8,128)(2,1)}, bf16[960,128]{1,0:T(8,128)(2,1)S(1)}, u32[]{:S(2)}, u32[]{:S(2)}) collective-permute-start(bf16[960,128]{1,0:T(8,128)(2,1)} %get-tuple-element.32), channel_id=1, source_target_pairs={{0,6},{1,7},{2,4},{3,5},{4,2},{5,3},{6,0},{7,1},{8,14},{9,15},{10,... | collective-permute-start | bytes 737288 | tf_op jit(solution)/shard_map/ppermute | solution.py:271
  33.2 27.9 %copy-start.6 = (bf16[960,128]{1,0:T(8,128)(2,1)}, bf16[960,128]{1,0:T(8,128)(2,1)S(1)}, u32[]{:S(2)}) copy-start(bf16[960,128]{1,0:T(8,128)(2,1)S(1)} %collective-permute-done.1.refs_2_) | copy-start | bytes 737284
  33.2 21.9 %collective-permute-start.6 = (bf16[960,128]{1,0:T(8,128)(2,1)}, bf16[960,128]{1,0:T(8,128)(2,1)S(1)}, u32[]{:S(2)}, u32[]{:S(2)}) collective-permute-start(bf16[960,128]{1,0:T(8,128)(2,1)} %get-tuple-element.33), channel_id=1, source_target_pairs={{0,7},{1,6},{2,5},{3,4},{4,3},{5,2},{6,1},{7,0},{8,15},{9,14},{10,... | collective-permute-start | bytes 737288 | tf_op jit(solution)/shard_map/ppermute | solution.py:271
  40.8 20.3 %copy-start.8 = (bf16[960,128]{1,0:T(8,128)(2,1)}, bf16[960,128]{1,0:T(8,128)(2,1)S(1)}, u32[]{:S(2)}) copy-start(bf16[960,128]{1,0:T(8,128)(2,1)S(1)} %collective-permute-done.2.refs_3_) | copy-start | bytes 737284
  46.1 15.0 %copy-start.10 = (bf16[960,128]{1,0:T(8,128)(2,1)}, bf16[960,128]{1,0:T(8,128)(2,1)S(1)}, u32[]{:S(2)}) copy-start(bf16[960,128]{1,0:T(8,128)(2,1)S(1)} %collective-permute-done.3.refs_4_) | copy-start | bytes 737284
  51.5 0.7 copy-start.12
  52.2 0.7 copy-start.15
  55.1 0.7 copy-start.18
  55.8 0.9 copy-start.13
  56.7 0.9 copy-start.16
  57.7 0.9 copy-start.19
  58.6 13.1 %copy-start.1 = (f32[2,512,128]{2,1,0:T(8,128)S(1)}, f32[2,512,128]{2,1,0:T(8,128)}, u32[]{:S(2)}) copy-start(f32[2,512,128]{2,1,0:T(8,128)} %constant.6.clone.base_ref) | copy-start | bytes 1572868
  58.6 36.0 %copy-start.3 = (f32[2,1024,128]{2,1,0:T(8,128)S(1)}, f32[2,1024,128]{2,1,0:T(8,128)}, u32[]{:S(2)}) copy-start(f32[2,1024,128]{2,1,0:T(8,128)} %primaries_ref.3) | copy-start | bytes 3145732
  58.6 36.0 %copy-start.22 = (f32[128]{0:T(128)S(1)}, f32[128]{0:T(128)}, u32[]{:S(2)}) copy-start(f32[128]{0:T(128)} %param.8) | copy-start | bytes 1540
  61.1 33.5 %all-to-all-start.1 = ((bf16[256,5,2,128]{3,2,1,0:T(2,128)(2,1)}), bf16[256,5,2,128]{3,2,1,0:T(2,128)(2,1)S(1)}, u32[]{:S(2)}, u32[]{:S(2)}) async-start(bf16[256,5,2,128]{3,2,1,0:T(2,128)(2,1)} %bitcast.4), calls=%async_computation.1 | async-start | bytes 1310720 | tf_op jit(solution)/shard_map/all_to_all | solution.py:277
  94.6 1.6 %copy-start.23 = (bf16[1024,1024]{1,0:T(8,128)(2,1)S(1)}, bf16[1024,1024]{1,0:T(8,128)(2,1)}, u32[]{:S(2)}) copy-start(bf16[1024,1024]{1,0:T(8,128)(2,1)} %get-tuple-element.34.table_ref) | copy-start | bytes 6291460
  96.2 27.7 %copy-start.5 = (bf16[960,128]{1,0:T(8,128)(2,1)S(1)}, bf16[960,128]{1,0:T(8,128)(2,1)}, u32[]{:S(2)}) copy-start(bf16[960,128]{1,0:T(8,128)(2,1)} %copy-done.4) | copy-start | bytes 737284
  96.2 27.7 %copy-start.7 = (bf16[960,128]{1,0:T(8,128)(2,1)S(1)}, bf16[960,128]{1,0:T(8,128)(2,1)}, u32[]{:S(2)}) copy-start(bf16[960,128]{1,0:T(8,128)(2,1)} %copy-done.6) | copy-start | bytes 737284
  96.2 27.7 %copy-start.9 = (bf16[960,128]{1,0:T(8,128)(2,1)S(1)}, bf16[960,128]{1,0:T(8,128)(2,1)}, u32[]{:S(2)}) copy-start(bf16[960,128]{1,0:T(8,128)(2,1)} %copy-done.8) | copy-start | bytes 737284
  96.2 27.7 %copy-start.11 = (bf16[960,128]{1,0:T(8,128)(2,1)S(1)}, bf16[960,128]{1,0:T(8,128)(2,1)}, u32[]{:S(2)}) copy-start(bf16[960,128]{1,0:T(8,128)(2,1)} %copy-done.10) | copy-start | bytes 737284
  96.2 27.7 %copy-start.14 = (bf16[960,128]{1,0:T(8,128)(2,1)S(1)}, bf16[960,128]{1,0:T(8,128)(2,1)}, u32[]{:S(2)}) copy-start(bf16[960,128]{1,0:T(8,128)(2,1)} %copy-done.12) | copy-start | bytes 737284
  96.2 27.7 %copy-start.17 = (bf16[960,128]{1,0:T(8,128)(2,1)S(1)}, bf16[960,128]{1,0:T(8,128)(2,1)}, u32[]{:S(2)}) copy-start(bf16[960,128]{1,0:T(8,128)(2,1)} %copy-done.15) | copy-start | bytes 737284
  96.3 27.7 %copy-start.20 = (bf16[960,128]{1,0:T(8,128)(2,1)S(1)}, bf16[960,128]{1,0:T(8,128)(2,1)}, u32[]{:S(2)}) copy-start(bf16[960,128]{1,0:T(8,128)(2,1)} %copy-done.18) | copy-start | bytes 737284
  98.0 25.9 %copy-start.2 = (f32[2,1024,128]{2,1,0:T(8,128)}, f32[2,1024,128]{2,1,0:T(8,128)S(1)}, u32[]{:S(2)}) copy-start(f32[2,1024,128]{2,1,0:T(8,128)S(1)} %get-tuple-element.38.primaries_ref) | copy-start | bytes 3145732
  126.5 29.6 %copy-start = (bf16[1024,1024]{1,0:T(8,128)(2,1)S(1)}, bf16[1024,1024]{1,0:T(8,128)(2,1)}, u32[]{:S(2)}) copy-start(bf16[1024,1024]{1,0:T(8,128)(2,1)} %get-tuple-element.37.table_ref) | copy-start | bytes 6291460
  126.5 29.6 %all-to-all-start.3 = ((bf16[256,5,2,128]{3,2,1,0:T(2,128)(2,1)}), bf16[256,5,2,128]{3,2,1,0:T(2,128)(2,1)S(1)}, u32[]{:S(2)}, u32[]{:S(2)}) async-start(bf16[256,5,2,128]{3,2,1,0:T(2,128)(2,1)} %bitcast.9), calls=%async_computation.3 | async-start | bytes 1310720 | tf_op jit(solution)/shard_map/all_to_all | solution.py:277
  133.8 7.4 %collective-permute-start.7 = (bf16[2,2,48,128]{3,2,1,0:T(8,128)(2,1)}, bf16[2,2,48,128]{3,2,1,0:T(8,128)(2,1)S(1)}, u32[]{:S(2)}, u32[]{:S(2)}) collective-permute-start(bf16[2,2,48,128]{3,2,1,0:T(8,128)(2,1)} %get-tuple-element.41), channel_id=1, source_target_pairs={{0,1},{1,0},{2,3},{3,2},{4,5},{5,4},{6,7},{7,6},{8,9},{9,8},{10,11... | collective-permute-start | bytes 147464 | tf_op jit(solution)/shard_map/ppermute | solution.py:271
  136.2 5.9 %collective-permute-start.8 = (bf16[2,2,48,128]{3,2,1,0:T(8,128)(2,1)}, bf16[2,2,48,128]{3,2,1,0:T(8,128)(2,1)S(1)}, u32[]{:S(2)}, u32[]{:S(2)}) collective-permute-start(bf16[2,2,48,128]{3,2,1,0:T(8,128)(2,1)} %get-tuple-element.42), channel_id=1, source_target_pairs={{0,2},{1,3},{2,0},{3,1},{4,6},{5,7},{6,4},{7,5},{8,10},{9,11},{10,... | collective-permute-start | bytes 147464 | tf_op jit(solution)/shard_map/ppermute | solution.py:271
  136.2 7.9 %collective-permute-start.9 = (bf16[2,2,48,128]{3,2,1,0:T(8,128)(2,1)}, bf16[2,2,48,128]{3,2,1,0:T(8,128)(2,1)S(1)}, u32[]{:S(2)}, u32[]{:S(2)}) collective-permute-start(bf16[2,2,48,128]{3,2,1,0:T(8,128)(2,1)} %get-tuple-element.43), channel_id=1, source_target_pairs={{0,3},{1,2},{2,1},{3,0},{4,7},{5,6},{6,5},{7,4},{8,11},{9,10},{10,... | collective-permute-start | bytes 147464 | tf_op jit(solution)/shard_map/ppermute | solution.py:271
  137.9 6.3 %collective-permute-start.10 = (bf16[2,2,48,128]{3,2,1,0:T(8,128)(2,1)}, bf16[2,2,48,128]{3,2,1,0:T(8,128)(2,1)S(1)}, u32[]{:S(2)}, u32[]{:S(2)}) collective-permute-start(bf16[2,2,48,128]{3,2,1,0:T(8,128)(2,1)} %get-tuple-element.44), channel_id=1, source_target_pairs={{0,4},{1,5},{2,6},{3,7},{4,0},{5,1},{6,2},{7,3},{8,12},{9,13},{10,... | collective-permute-start | bytes 147464 | tf_op jit(solution)/shard_map/ppermute | solution.py:271
  139.0 7.7 %collective-permute-start.11 = (bf16[2,2,48,128]{3,2,1,0:T(8,128)(2,1)}, bf16[2,2,48,128]{3,2,1,0:T(8,128)(2,1)S(1)}, u32[]{:S(2)}, u32[]{:S(2)}) collective-permute-start(bf16[2,2,48,128]{3,2,1,0:T(8,128)(2,1)} %get-tuple-element.45), channel_id=1, source_target_pairs={{0,5},{1,4},{2,7},{3,6},{4,1},{5,0},{6,3},{7,2},{8,13},{9,12},{10,... | collective-permute-start | bytes 147464 | tf_op jit(solution)/shard_map/ppermute | solution.py:271
  141.2 7.4 %collective-permute-start.12 = (bf16[2,2,48,128]{3,2,1,0:T(8,128)(2,1)}, bf16[2,2,48,128]{3,2,1,0:T(8,128)(2,1)S(1)}, u32[]{:S(2)}, u32[]{:S(2)}) collective-permute-start(bf16[2,2,48,128]{3,2,1,0:T(8,128)(2,1)} %get-tuple-element.46), channel_id=1, source_target_pairs={{0,6},{1,7},{2,4},{3,5},{4,2},{5,3},{6,0},{7,1},{8,14},{9,15},{10,... | collective-permute-start | bytes 147464 | tf_op jit(solution)/shard_map/ppermute | solution.py:271
  142.0 8.4 %collective-permute-start.13 = (bf16[2,2,48,128]{3,2,1,0:T(8,128)(2,1)}, bf16[2,2,48,128]{3,2,1,0:T(8,128)(2,1)S(1)}, u32[]{:S(2)}, u32[]{:S(2)}) collective-permute-start(bf16[2,2,48,128]{3,2,1,0:T(8,128)(2,1)} %get-tuple-element.47), channel_id=1, source_target_pairs={{0,7},{1,6},{2,5},{3,4},{4,3},{5,2},{6,1},{7,0},{8,15},{9,14},{10,... | collective-permute-start | bytes 147464 | tf_op jit(solution)/shard_map/ppermute | solution.py:271
  150.5 0.8 copy-start.21

commit v7 on v6

--- a/solution.py
+++ b/solution.py
@@ -121,6 +121,7 @@
     rows_ref[...] = points_ref[...].astype(jnp.float32)
     residual_sq = jnp.zeros((1, 1), jnp.float32)
     direction_sq = jnp.zeros((1, 1), jnp.float32)
+    ops, products, resids = [], [], []
     for k in range(2):
         spectra = jnp.concatenate(
             [rows_ref[pl.ds(2 * k + c, NS, stride=PARTS), :].astype(jnp.bfloat16) for c in range(2)], axis=1
@@ -135,6 +136,9 @@
             axis=0,
         )
         product = jnp.dot(op, spectra, preferred_element_type=jnp.float32).reshape(blocks, 2, rows, 2 * S)
+        ops.append(op)
+        products.append(product)
+    for k, product in enumerate(products):
         stacked = []
         for a in range(blocks):
             real = product[a, 0, :, :S] - product[a, 1, :, S:]
@@ -152,8 +156,10 @@
             residual_sq += jnp.sum(wide_real * wide_real + wide_imag * wide_imag, keepdims=True)
             stacked.append(jnp.concatenate([real, imag], axis=1))
             stacked.append(jnp.concatenate([imag, -real], axis=1))
+        resids.append(jnp.concatenate(stacked, axis=0))
+    for k in range(2):
         direction = lax.dot_general(
-            op, jnp.concatenate(stacked, axis=0), (((0,), (0,)), ((), ())), preferred_element_type=jnp.float32
+            ops[k], resids[k], (((0,), (0,)), ((), ())), preferred_element_type=jnp.float32
         )
         direction_sq += jnp.sum(direction * direction, keepdims=True)
         for c in range(2):

time: 159 us -> 158 us (level)
  no operation moved by 1% of the time
where the time goes in v7:
time: 158 us
  starting transfers between devices  53.7 us (34%)
  waiting for transfers between devices  53.6 us (34%)
  blocking collectives  25.9 us (16%)
  Pallas kernels  15.3 us (10%)
  local copies, waits for them, and re-layouts  8.42 us (5%)
    all_to_all x3, starting transfers between devices, exchange(): lax.all_to_all(pairs, ALL, split_axis=0, concat_axis=0, tiled=True)  32.7 us
    ppermute x14, waiting for transfers between devices, trade(): lax.ppermute(pieces[place], 'rcv', [(source, source ^ place) for source i...  29.4 us
    all_to_all x1, blocking collectives, exchange(): lax.all_to_all(pairs, ALL, split_axis=0, concat_axis=0, tiled=True)  25.9 us
    all_to_all x3, waiting for transfers between devices, exchange(): lax.all_to_all(pairs, ALL, split_axis=0, concat_axis=0, tiled=True)  24.2 us
    ppermute x14, starting transfers between devices, trade(): lax.ppermute(pieces[place], 'rcv', [(source, source ^ place) for source i...  21 us
    pallas_call x7, Pallas kernels, call(): pl.pallas_call(kernel, out_shape=out_shape, in_specs=[pl.BlockSpec(memory...  15.2 us
    unnamed x49, local copies, waits for them, and re-layouts  8.42 us
  transfers between devices with their start and end apart: 17, of which 10 were waited for; matrix products, arithmetic and copies ran while one was open for 1% of the time, Pallas kernels for 2%

profile of v7, /device:TPU:1, one launch (start us, length us, event | category | flops | bytes accessed | tf_op | source)
XLA Modules:
  0.0 157.8 jit_solution(8706806393935881111)
XLA Ops:
  0.6 3.7 %shard_map.68 = (bf16[960,128]{1,0:T(8,128)(2,1)S(1)}, bf16[960,128]{1,0:T(8,128)(2,1)}, bf16[960,128]{1,0:T(8,128)(2,1)}, bf16[960,128]{1,0:T(8,128)(2,1)}, bf1...) custom-call(s32[1]{0:T(128)} %bitcast.me_ref, ...), custom_call_target="tpu_custom_call" | custom-call | flops 536870912 | bytes 4194304 | tf_op jit(solution)/shard_map/pallas_call | solution.py:50
  4.4 15.6 %all-to-all-start = ((bf16[256,4,2,128]{3,2,1,0:T(2,128)(2,1)}), bf16[256,4,2,128]{3,2,1,0:T(2,128)(2,1)S(1)}, u32[]{:S(2)}, u32[]{:S(2)}) async-start(bf16[256,4,2,128]{3,2,1,0:T(2,128)(2,1)} %bitcast.20), calls=%async_computation | async-start | bytes 1048576 | tf_op jit(solution)/shard_map/all_to_all | solution.py:283
  20.0 2.2 %collective-permute-start = (bf16[960,128]{1,0:T(8,128)(2,1)}, bf16[960,128]{1,0:T(8,128)(2,1)S(1)}, u32[]{:S(2)}, u32[]{:S(2)}) collective-permute-start(bf16[960,128]{1,0:T(8,128)(2,1)} %get-tuple-element.27), channel_id=1, source_target_pairs={{0,1},{1,0},{2,3},{3,2},{4,5},{5,4},{6,7},{7,6},{8,9},{9,8},{10,11... | collective-permute-start | bytes 737288 | tf_op jit(solution)/shard_map/ppermute | solution.py:277
  22.2 0.0 collective-permute-start.1
  22.3 1.7 %collective-permute-start.2 = (bf16[960,128]{1,0:T(8,128)(2,1)}, bf16[960,128]{1,0:T(8,128)(2,1)S(1)}, u32[]{:S(2)}, u32[]{:S(2)}) collective-permute-start(bf16[960,128]{1,0:T(8,128)(2,1)} %get-tuple-element.29), channel_id=1, source_target_pairs={{0,3},{1,2},{2,1},{3,0},{4,7},{5,6},{6,5},{7,4},{8,11},{9,10},{10,... | collective-permute-start | bytes 737288 | tf_op jit(solution)/shard_map/ppermute | solution.py:277
  24.0 1.1 collective-permute-start.3
  25.1 2.1 %collective-permute-start.4 = (bf16[960,128]{1,0:T(8,128)(2,1)}, bf16[960,128]{1,0:T(8,128)(2,1)S(1)}, u32[]{:S(2)}, u32[]{:S(2)}) collective-permute-start(bf16[960,128]{1,0:T(8,128)(2,1)} %get-tuple-element.31), channel_id=1, source_target_pairs={{0,5},{1,4},{2,7},{3,6},{4,1},{5,0},{6,3},{7,2},{8,13},{9,12},{10,... | collective-permute-start | bytes 737288 | tf_op jit(solution)/shard_map/ppermute | solution.py:277
  27.3 0.9 collective-permute-start.5
  28.1 5.0 %collective-permute-done.1.refs_2_ = bf16[960,128]{1,0:T(8,128)(2,1)S(1)} collective-permute-done((bf16[960,128]{1,0:T(8,128)(2,1)}, bf16[960,128]{1,0:T(8,128)(2,1)S(1)}, u32[]{:S(2)}, u32[]{:S(2)}) %collective-permute-start.1) | collective-permute-done | bytes 245792 | tf_op jit(solution)/shard_map/ppermute | solution.py:277
  33.2 2.6 %collective-permute-start.6 = (bf16[960,128]{1,0:T(8,128)(2,1)}, bf16[960,128]{1,0:T(8,128)(2,1)S(1)}, u32[]{:S(2)}, u32[]{:S(2)}) collective-permute-start(bf16[960,128]{1,0:T(8,128)(2,1)} %get-tuple-element.33), channel_id=1, source_target_pairs={{0,7},{1,6},{2,5},{3,4},{4,3},{5,2},{6,1},{7,0},{8,15},{9,14},{10,... | collective-permute-start | bytes 737288 | tf_op jit(solution)/shard_map/ppermute | solution.py:277
  35.7 5.1 %collective-permute-done.2.refs_3_ = bf16[960,128]{1,0:T(8,128)(2,1)S(1)} collective-permute-done((bf16[960,128]{1,0:T(8,128)(2,1)}, bf16[960,128]{1,0:T(8,128)(2,1)S(1)}, u32[]{:S(2)}, u32[]{:S(2)}) %collective-permute-start.2) | collective-permute-done | bytes 245792 | tf_op jit(solution)/shard_map/ppermute | solution.py:277
  40.8 5.4 %collective-permute-done.3.refs_4_ = bf16[960,128]{1,0:T(8,128)(2,1)S(1)} collective-permute-done((bf16[960,128]{1,0:T(8,128)(2,1)}, bf16[960,128]{1,0:T(8,128)(2,1)S(1)}, u32[]{:S(2)}, u32[]{:S(2)}) %collective-permute-start.3) | collective-permute-done | bytes 245792 | tf_op jit(solution)/shard_map/ppermute | solution.py:277
  46.1 5.4 %collective-permute-done.4.refs_5_ = bf16[960,128]{1,0:T(8,128)(2,1)S(1)} collective-permute-done((bf16[960,128]{1,0:T(8,128)(2,1)}, bf16[960,128]{1,0:T(8,128)(2,1)S(1)}, u32[]{:S(2)}, u32[]{:S(2)}) %collective-permute-start.4) | collective-permute-done | bytes 245792 | tf_op jit(solution)/shard_map/ppermute | solution.py:277
  51.5 0.7 copy-done.12
  52.2 0.0 collective-permute-done.5.refs_6_
  52.2 0.7 copy-done.15
  52.9 2.2 %collective-permute-done.6.refs_7_ = bf16[960,128]{1,0:T(8,128)(2,1)S(1)} collective-permute-done((bf16[960,128]{1,0:T(8,128)(2,1)}, bf16[960,128]{1,0:T(8,128)(2,1)S(1)}, u32[]{:S(2)}, u32[]{:S(2)}) %collective-permute-start.6) | collective-permute-done | bytes 245792 | tf_op jit(solution)/shard_map/ppermute | solution.py:277
  55.1 0.7 copy-done.18
  55.8 0.9 copy-done.13
  56.7 0.9 copy-done.16
  57.7 0.9 copy-done.19
  58.6 2.1 %shard_map.69 = bf16[2560,128]{1,0:T(8,128)(2,1)} custom-call(bf16[2048,128]{1,0:T(8,128)(2,1)S(1)} %bitcast.13, bf16[960,128]{1,0:T(8,128)(2,1)S(1)} %get-tuple-element.26.refs_0_, bf16[960,128]{1,0:T(8,128)(2,1)S(1)} %collective-permute-done.refs_1_, bf16[960,128]{1,0:T(8,128)(2,1)S(1)} %collective-permute-done.1.refs_2_, ...), custom_call_target="tpu_custom_call" | custom-call | flops 805306368 | bytes 4194304 | tf_op jit(solution)/shard_map/pallas_call | solution.py:50
  60.8 10.6 %all-to-all-start.1 = ((bf16[256,5,2,128]{3,2,1,0:T(2,128)(2,1)}), bf16[256,5,2,128]{3,2,1,0:T(2,128)(2,1)S(1)}, u32[]{:S(2)}, u32[]{:S(2)}) async-start(bf16[256,5,2,128]{3,2,1,0:T(2,128)(2,1)} %bitcast.4), calls=%async_computation.1 | async-start | bytes 1310720 | tf_op jit(solution)/shard_map/all_to_all | solution.py:283
  71.4 2.4 %shard_map.70 = (bf16[1024,1024]{1,0:T(8,128)(2,1)}, bf16[1024,1024]{1,0:T(8,128)(2,1)}) custom-call(f32[2,512,128]{2,1,0:T(8,128)S(1)} %copy-done.1), custom_call_target="tpu_custom_call" | custom-call | flops 1048576 | bytes 4194304 | tf_op jit(solution)/shard_map/pallas_call | solution.py:50
  73.8 20.5 %all-to-all-done.1 = bf16[256,5,2,128]{3,2,1,0:T(2,128)(2,1)S(1)} async-done(((bf16[256,5,2,128]{3,2,1,0:T(2,128)(2,1)}), bf16[256,5,2,128]{3,2,1,0:T(2,128)(2,1)S(1)}, u32[]{:S(2)}, u32[]{:S(2)}) %all-to-all-start.1) | async-done | bytes 655392 | tf_op jit(solution)/shard_map/all_to_all | solution.py:283
  94.3 1.6 %copy-done.23 = bf16[1024,1024]{1,0:T(8,128)(2,1)S(1)} copy-done((bf16[1024,1024]{1,0:T(8,128)(2,1)S(1)}, bf16[1024,1024]{1,0:T(8,128)(2,1)}, u32[]{:S(2)}) %copy-start.23) | copy-done | bytes 2097176
  95.9 0.0 copy-start.14
  95.9 1.8 %shard_map.71 = (f32[2,1024,128]{2,1,0:T(8,128)S(1)}, bf16[2048,128]{1,0:T(8,128)(2,1)S(1)}) custom-call(bf16[2560,128]{1,0:T(8,128)(2,1)S(1)} %bitcast.15, bf16[1024,1024]{1,0:T(8,128)(2,1)S(1)} %copy-done.23, f32[2,1024,128]{2,1,0:T(8,128)S(1)} %copy-done.3, f32[1,128]{1,0:T(1,128)S(1)} %bitcast.18), custom_call_target="tpu_custom_call" | custom-call | flops 1073741824 | bytes 4194304 | tf_op jit(solution)/shard_map/pallas_call | solution.py:50
  97.7 25.9 %all_to_all.20 = bf16[256,4,2,128]{3,2,1,0:T(2,128)(2,1)S(1)} all-to-all(bf16[256,4,2,128]{3,2,1,0:T(2,128)(2,1)S(1)} %bitcast.17), channel_id=1, replica_groups=mesh['freq'=32,'rcv'=8] {'rcv','freq'}, dimensions={0} | all-to-all | bytes 1048576 | tf_op jit(solution)/shard_map/all_to_all | solution.py:283
  123.7 2.1 %shard_map.72 = (bf16[2560,128]{1,0:T(8,128)(2,1)}, bf16[8,2,2,48,128]{4,3,2,1,0:T(8,128)(2,1)S(1)}) custom-call(bf16[2048,128]{1,0:T(8,128)(2,1)S(1)} %bitcast.16, bf16[960,128]{1,0:T(8,128)(2,1)S(1)} %get-tuple-element.26.refs_0_, bf16[960,128]{1,0:T(8,128)(2,1)S(1)} %copy-done.5, bf16[960,128]{1,0:T(8,128)(2,1)S(1)} %copy-done.7, ...), custom_call_target="tpu_custom_call" | custom-call | flops 805306368 | bytes 4194304 | tf_op jit(solution)/shard_map/pallas_call | solution.py:50
  125.8 6.5 %all-to-all-start.3 = ((bf16[256,5,2,128]{3,2,1,0:T(2,128)(2,1)}), bf16[256,5,2,128]{3,2,1,0:T(2,128)(2,1)S(1)}, u32[]{:S(2)}, u32[]{:S(2)}) async-start(bf16[256,5,2,128]{3,2,1,0:T(2,128)(2,1)} %bitcast.9), calls=%async_computation.3 | async-start | bytes 1310720 | tf_op jit(solution)/shard_map/all_to_all | solution.py:283
  132.3 0.8 shard_map.74
  133.2 2.4 %collective-permute-start.7 = (bf16[2,2,48,128]{3,2,1,0:T(8,128)(2,1)}, bf16[2,2,48,128]{3,2,1,0:T(8,128)(2,1)S(1)}, u32[]{:S(2)}, u32[]{:S(2)}) collective-permute-start(bf16[2,2,48,128]{3,2,1,0:T(8,128)(2,1)} %get-tuple-element.41), channel_id=1, source_target_pairs={{0,1},{1,0},{2,3},{3,2},{4,5},{5,4},{6,7},{7,6},{8,9},{9,8},{10,11... | collective-permute-start | bytes 147464 | tf_op jit(solution)/shard_map/ppermute | solution.py:277
  135.5 0.0 collective-permute-start.8
  135.5 1.7 %collective-permute-start.9 = (bf16[2,2,48,128]{3,2,1,0:T(8,128)(2,1)}, bf16[2,2,48,128]{3,2,1,0:T(8,128)(2,1)S(1)}, u32[]{:S(2)}, u32[]{:S(2)}) collective-permute-start(bf16[2,2,48,128]{3,2,1,0:T(8,128)(2,1)} %get-tuple-element.43), channel_id=1, source_target_pairs={{0,3},{1,2},{2,1},{3,0},{4,7},{5,6},{6,5},{7,4},{8,11},{9,10},{10,... | collective-permute-start | bytes 147464 | tf_op jit(solution)/shard_map/ppermute | solution.py:277
  137.3 1.1 collective-permute-start.10
  138.4 2.1 %collective-permute-start.11 = (bf16[2,2,48,128]{3,2,1,0:T(8,128)(2,1)}, bf16[2,2,48,128]{3,2,1,0:T(8,128)(2,1)S(1)}, u32[]{:S(2)}, u32[]{:S(2)}) collective-permute-start(bf16[2,2,48,128]{3,2,1,0:T(8,128)(2,1)} %get-tuple-element.45), channel_id=1, source_target_pairs={{0,5},{1,4},{2,7},{3,6},{4,1},{5,0},{6,3},{7,2},{8,13},{9,12},{10,... | collective-permute-start | bytes 147464 | tf_op jit(solution)/shard_map/ppermute | solution.py:277
  140.5 0.0 collective-permute-done.7.refs_1_
  140.5 0.9 collective-permute-start.12
  141.4 2.1 %collective-permute-start.13 = (bf16[2,2,48,128]{3,2,1,0:T(8,128)(2,1)}, bf16[2,2,48,128]{3,2,1,0:T(8,128)(2,1)S(1)}, u32[]{:S(2)}, u32[]{:S(2)}) collective-permute-start(bf16[2,2,48,128]{3,2,1,0:T(8,128)(2,1)} %get-tuple-element.47), channel_id=1, source_target_pairs={{0,7},{1,6},{2,5},{3,4},{4,3},{5,2},{6,1},{7,0},{8,15},{9,14},{10,... | collective-permute-start | bytes 147464 | tf_op jit(solution)/shard_map/ppermute | solution.py:277
  143.5 0.0 collective-permute-done.10.refs_4_
  143.5 2.5 %collective-permute-done.11.refs_5_ = bf16[2,2,48,128]{3,2,1,0:T(8,128)(2,1)S(1)} collective-permute-done((bf16[2,2,48,128]{3,2,1,0:T(8,128)(2,1)}, bf16[2,2,48,128]{3,2,1,0:T(8,128)(2,1)S(1)}, u32[]{:S(2)}, u32[]{:S(2)}) %collective-permute-start.11) | collective-permute-done | bytes 49184 | tf_op jit(solution)/shard_map/ppermute | solution.py:277
  146.0 1.9 %collective-permute-done.12.refs_6_ = bf16[2,2,48,128]{3,2,1,0:T(8,128)(2,1)S(1)} collective-permute-done((bf16[2,2,48,128]{3,2,1,0:T(8,128)(2,1)}, bf16[2,2,48,128]{3,2,1,0:T(8,128)(2,1)S(1)}, u32[]{:S(2)}, u32[]{:S(2)}) %collective-permute-start.12) | collective-permute-done | bytes 49184 | tf_op jit(solution)/shard_map/ppermute | solution.py:277
  148.0 1.8 %collective-permute-done.13.refs_7_ = bf16[2,2,48,128]{3,2,1,0:T(8,128)(2,1)S(1)} collective-permute-done((bf16[2,2,48,128]{3,2,1,0:T(8,128)(2,1)}, bf16[2,2,48,128]{3,2,1,0:T(8,128)(2,1)S(1)}, u32[]{:S(2)}, u32[]{:S(2)}) %collective-permute-start.13) | collective-permute-done | bytes 49184 | tf_op jit(solution)/shard_map/ppermute | solution.py:277
  149.8 0.8 copy-done.21
  150.6 1.1 copy.7
  151.7 3.7 %all-to-all-done.3 = bf16[256,5,2,128]{3,2,1,0:T(2,128)(2,1)S(1)} async-done(((bf16[256,5,2,128]{3,2,1,0:T(2,128)(2,1)}), bf16[256,5,2,128]{3,2,1,0:T(2,128)(2,1)S(1)}, u32[]{:S(2)}, u32[]{:S(2)}) %all-to-all-start.3) | async-done | bytes 655392 | tf_op jit(solution)/shard_map/all_to_all | solution.py:283
  155.4 2.3 %shard_map.73 = f32[2,1024,128]{2,1,0:T(8,128)} custom-call(bf16[2560,128]{1,0:T(8,128)(2,1)S(1)} %bitcast.12, bf16[1024,1024]{1,0:T(8,128)(2,1)S(1)} %copy-done, f32[2,1024,128]{2,1,0:T(8,128)} %copy-done.2, f32[1,128]{1,0:T(1,128)S(1)} %bitcast.19), custom_call_target="tpu_custom_call" | custom-call | flops 536870912 | bytes 4194304 | tf_op jit(solution)/shard_map/pallas_call | solution.py:50
  (44 shorter events, 0.1 us)
Async XLA Ops:
  4.4 51.4 %all-to-all-start = ((bf16[256,4,2,128]{3,2,1,0:T(2,128)(2,1)}), bf16[256,4,2,128]{3,2,1,0:T(2,128)(2,1)S(1)}, u32[]{:S(2)}, u32[]{:S(2)}) async-start(bf16[256,4,2,128]{3,2,1,0:T(2,128)(2,1)} %bitcast.20), calls=%async_computation | async-start | bytes 1048576 | tf_op jit(solution)/shard_map/all_to_all | solution.py:283
  20.0 7.2 %collective-permute-start = (bf16[960,128]{1,0:T(8,128)(2,1)}, bf16[960,128]{1,0:T(8,128)(2,1)S(1)}, u32[]{:S(2)}, u32[]{:S(2)}) collective-permute-start(bf16[960,128]{1,0:T(8,128)(2,1)} %get-tuple-element.27), channel_id=1, source_target_pairs={{0,1},{1,0},{2,3},{3,2},{4,5},{5,4},{6,7},{7,6},{8,9},{9,8},{10,11... | collective-permute-start | bytes 737288 | tf_op jit(solution)/shard_map/ppermute | solution.py:277
  22.2 10.9 %collective-permute-start.1 = (bf16[960,128]{1,0:T(8,128)(2,1)}, bf16[960,128]{1,0:T(8,128)(2,1)S(1)}, u32[]{:S(2)}, u32[]{:S(2)}) collective-permute-start(bf16[960,128]{1,0:T(8,128)(2,1)} %get-tuple-element.28), channel_id=1, source_target_pairs={{0,2},{1,3},{2,0},{3,1},{4,6},{5,7},{6,4},{7,5},{8,10},{9,11},{10,... | collective-permute-start | bytes 737288 | tf_op jit(solution)/shard_map/ppermute | solution.py:277
  22.3 18.5 %collective-permute-start.2 = (bf16[960,128]{1,0:T(8,128)(2,1)}, bf16[960,128]{1,0:T(8,128)(2,1)S(1)}, u32[]{:S(2)}, u32[]{:S(2)}) collective-permute-start(bf16[960,128]{1,0:T(8,128)(2,1)} %get-tuple-element.29), channel_id=1, source_target_pairs={{0,3},{1,2},{2,1},{3,0},{4,7},{5,6},{6,5},{7,4},{8,11},{9,10},{10,... | collective-permute-start | bytes 737288 | tf_op jit(solution)/shard_map/ppermute | solution.py:277
  24.0 22.2 %collective-permute-start.3 = (bf16[960,128]{1,0:T(8,128)(2,1)}, bf16[960,128]{1,0:T(8,128)(2,1)S(1)}, u32[]{:S(2)}, u32[]{:S(2)}) collective-permute-start(bf16[960,128]{1,0:T(8,128)(2,1)} %get-tuple-element.30), channel_id=1, source_target_pairs={{0,4},{1,5},{2,6},{3,7},{4,0},{5,1},{6,2},{7,3},{8,12},{9,13},{10,... | collective-permute-start | bytes 737288 | tf_op jit(solution)/shard_map/ppermute | solution.py:277
  25.1 26.4 %collective-permute-start.4 = (bf16[960,128]{1,0:T(8,128)(2,1)}, bf16[960,128]{1,0:T(8,128)(2,1)S(1)}, u32[]{:S(2)}, u32[]{:S(2)}) collective-permute-start(bf16[960,128]{1,0:T(8,128)(2,1)} %get-tuple-element.31), channel_id=1, source_target_pairs={{0,5},{1,4},{2,7},{3,6},{4,1},{5,0},{6,3},{7,2},{8,13},{9,12},{10,... | collective-permute-start | bytes 737288 | tf_op jit(solution)/shard_map/ppermute | solution.py:277
  27.2 33.5 %copy-start.4 = (bf16[960,128]{1,0:T(8,128)(2,1)}, bf16[960,128]{1,0:T(8,128)(2,1)S(1)}, u32[]{:S(2)}) copy-start(bf16[960,128]{1,0:T(8,128)(2,1)S(1)} %collective-permute-done.refs_1_) | copy-start | bytes 737284
  27.3 25.0 %collective-permute-start.5 = (bf16[960,128]{1,0:T(8,128)(2,1)}, bf16[960,128]{1,0:T(8,128)(2,1)S(1)}, u32[]{:S(2)}, u32[]{:S(2)}) collective-permute-start(bf16[960,128]{1,0:T(8,128)(2,1)} %get-tuple-element.32), channel_id=1, source_target_pairs={{0,6},{1,7},{2,4},{3,5},{4,2},{5,3},{6,0},{7,1},{8,14},{9,15},{10,... | collective-permute-start | bytes 737288 | tf_op jit(solution)/shard_map/ppermute | solution.py:277
  33.2 27.6 %copy-start.6 = (bf16[960,128]{1,0:T(8,128)(2,1)}, bf16[960,128]{1,0:T(8,128)(2,1)S(1)}, u32[]{:S(2)}) copy-start(bf16[960,128]{1,0:T(8,128)(2,1)S(1)} %collective-permute-done.1.refs_2_) | copy-start | bytes 737284
  33.2 21.9 %collective-permute-start.6 = (bf16[960,128]{1,0:T(8,128)(2,1)}, bf16[960,128]{1,0:T(8,128)(2,1)S(1)}, u32[]{:S(2)}, u32[]{:S(2)}) collective-permute-start(bf16[960,128]{1,0:T(8,128)(2,1)} %get-tuple-element.33), channel_id=1, source_target_pairs={{0,7},{1,6},{2,5},{3,4},{4,3},{5,2},{6,1},{7,0},{8,15},{9,14},{10,... | collective-permute-start | bytes 737288 | tf_op jit(solution)/shard_map/ppermute | solution.py:277
  40.8 20.0 %copy-start.8 = (bf16[960,128]{1,0:T(8,128)(2,1)}, bf16[960,128]{1,0:T(8,128)(2,1)S(1)}, u32[]{:S(2)}) copy-start(bf16[960,128]{1,0:T(8,128)(2,1)S(1)} %collective-permute-done.2.refs_3_) | copy-start | bytes 737284
  46.1 14.6 %copy-start.10 = (bf16[960,128]{1,0:T(8,128)(2,1)}, bf16[960,128]{1,0:T(8,128)(2,1)S(1)}, u32[]{:S(2)}) copy-start(bf16[960,128]{1,0:T(8,128)(2,1)S(1)} %collective-permute-done.3.refs_4_) | copy-start | bytes 737284
  51.5 0.7 copy-start.12
  52.2 0.7 copy-start.15
  55.1 0.7 copy-start.18
  55.8 0.9 copy-start.13
  56.7 0.9 copy-start.16
  57.7 0.9 copy-start.19
  58.6 12.8 %copy-start.1 = (f32[2,512,128]{2,1,0:T(8,128)S(1)}, f32[2,512,128]{2,1,0:T(8,128)}, u32[]{:S(2)}) copy-start(f32[2,512,128]{2,1,0:T(8,128)} %constant.6.clone.base_ref) | copy-start | bytes 1572868
  58.6 35.7 %copy-start.3 = (f32[2,1024,128]{2,1,0:T(8,128)S(1)}, f32[2,1024,128]{2,1,0:T(8,128)}, u32[]{:S(2)}) copy-start(f32[2,1024,128]{2,1,0:T(8,128)} %primaries_ref.3) | copy-start | bytes 3145732
  58.6 35.7 %copy-start.22 = (f32[128]{0:T(128)S(1)}, f32[128]{0:T(128)}, u32[]{:S(2)}) copy-start(f32[128]{0:T(128)} %param.8) | copy-start | bytes 1540
  60.8 33.5 %all-to-all-start.1 = ((bf16[256,5,2,128]{3,2,1,0:T(2,128)(2,1)}), bf16[256,5,2,128]{3,2,1,0:T(2,128)(2,1)S(1)}, u32[]{:S(2)}, u32[]{:S(2)}) async-start(bf16[256,5,2,128]{3,2,1,0:T(2,128)(2,1)} %bitcast.4), calls=%async_computation.1 | async-start | bytes 1310720 | tf_op jit(solution)/shard_map/all_to_all | solution.py:283
  94.3 1.6 %copy-start.23 = (bf16[1024,1024]{1,0:T(8,128)(2,1)S(1)}, bf16[1024,1024]{1,0:T(8,128)(2,1)}, u32[]{:S(2)}) copy-start(bf16[1024,1024]{1,0:T(8,128)(2,1)} %get-tuple-element.34.table_ref) | copy-start | bytes 6291460
  95.9 27.7 %copy-start.5 = (bf16[960,128]{1,0:T(8,128)(2,1)S(1)}, bf16[960,128]{1,0:T(8,128)(2,1)}, u32[]{:S(2)}) copy-start(bf16[960,128]{1,0:T(8,128)(2,1)} %copy-done.4) | copy-start | bytes 737284
  95.9 27.7 %copy-start.7 = (bf16[960,128]{1,0:T(8,128)(2,1)S(1)}, bf16[960,128]{1,0:T(8,128)(2,1)}, u32[]{:S(2)}) copy-start(bf16[960,128]{1,0:T(8,128)(2,1)} %copy-done.6) | copy-start | bytes 737284
  95.9 27.7 %copy-start.9 = (bf16[960,128]{1,0:T(8,128)(2,1)S(1)}, bf16[960,128]{1,0:T(8,128)(2,1)}, u32[]{:S(2)}) copy-start(bf16[960,128]{1,0:T(8,128)(2,1)} %copy-done.8) | copy-start | bytes 737284
  95.9 27.7 %copy-start.11 = (bf16[960,128]{1,0:T(8,128)(2,1)S(1)}, bf16[960,128]{1,0:T(8,128)(2,1)}, u32[]{:S(2)}) copy-start(bf16[960,128]{1,0:T(8,128)(2,1)} %copy-done.10) | copy-start | bytes 737284
  95.9 27.7 %copy-start.14 = (bf16[960,128]{1,0:T(8,128)(2,1)S(1)}, bf16[960,128]{1,0:T(8,128)(2,1)}, u32[]{:S(2)}) copy-start(bf16[960,128]{1,0:T(8,128)(2,1)} %copy-done.12) | copy-start | bytes 737284
  95.9 27.7 %copy-start.17 = (bf16[960,128]{1,0:T(8,128)(2,1)S(1)}, bf16[960,128]{1,0:T(8,128)(2,1)}, u32[]{:S(2)}) copy-start(bf16[960,128]{1,0:T(8,128)(2,1)} %copy-done.15) | copy-start | bytes 737284
  95.9 27.7 %copy-start.20 = (bf16[960,128]{1,0:T(8,128)(2,1)S(1)}, bf16[960,128]{1,0:T(8,128)(2,1)}, u32[]{:S(2)}) copy-start(bf16[960,128]{1,0:T(8,128)(2,1)} %copy-done.18) | copy-start | bytes 737284
  97.7 25.9 %copy-start.2 = (f32[2,1024,128]{2,1,0:T(8,128)}, f32[2,1024,128]{2,1,0:T(8,128)S(1)}, u32[]{:S(2)}) copy-start(f32[2,1024,128]{2,1,0:T(8,128)S(1)} %get-tuple-element.38.primaries_ref) | copy-start | bytes 3145732
  125.8 29.6 %copy-start = (bf16[1024,1024]{1,0:T(8,128)(2,1)S(1)}, bf16[1024,1024]{1,0:T(8,128)(2,1)}, u32[]{:S(2)}) copy-start(bf16[1024,1024]{1,0:T(8,128)(2,1)} %get-tuple-element.37.table_ref) | copy-start | bytes 6291460
  125.8 29.6 %all-to-all-start.3 = ((bf16[256,5,2,128]{3,2,1,0:T(2,128)(2,1)}), bf16[256,5,2,128]{3,2,1,0:T(2,128)(2,1)S(1)}, u32[]{:S(2)}, u32[]{:S(2)}) async-start(bf16[256,5,2,128]{3,2,1,0:T(2,128)(2,1)} %bitcast.9), calls=%async_computation.3 | async-start | bytes 1310720 | tf_op jit(solution)/shard_map/all_to_all | solution.py:283
  133.2 7.4 %collective-permute-start.7 = (bf16[2,2,48,128]{3,2,1,0:T(8,128)(2,1)}, bf16[2,2,48,128]{3,2,1,0:T(8,128)(2,1)S(1)}, u32[]{:S(2)}, u32[]{:S(2)}) collective-permute-start(bf16[2,2,48,128]{3,2,1,0:T(8,128)(2,1)} %get-tuple-element.41), channel_id=1, source_target_pairs={{0,1},{1,0},{2,3},{3,2},{4,5},{5,4},{6,7},{7,6},{8,9},{9,8},{10,11... | collective-permute-start | bytes 147464 | tf_op jit(solution)/shard_map/ppermute | solution.py:277
  135.5 5.9 %collective-permute-start.8 = (bf16[2,2,48,128]{3,2,1,0:T(8,128)(2,1)}, bf16[2,2,48,128]{3,2,1,0:T(8,128)(2,1)S(1)}, u32[]{:S(2)}, u32[]{:S(2)}) collective-permute-start(bf16[2,2,48,128]{3,2,1,0:T(8,128)(2,1)} %get-tuple-element.42), channel_id=1, source_target_pairs={{0,2},{1,3},{2,0},{3,1},{4,6},{5,7},{6,4},{7,5},{8,10},{9,11},{10,... | collective-permute-start | bytes 147464 | tf_op jit(solution)/shard_map/ppermute | solution.py:277
  135.5 7.9 %collective-permute-start.9 = (bf16[2,2,48,128]{3,2,1,0:T(8,128)(2,1)}, bf16[2,2,48,128]{3,2,1,0:T(8,128)(2,1)S(1)}, u32[]{:S(2)}, u32[]{:S(2)}) collective-permute-start(bf16[2,2,48,128]{3,2,1,0:T(8,128)(2,1)} %get-tuple-element.43), channel_id=1, source_target_pairs={{0,3},{1,2},{2,1},{3,0},{4,7},{5,6},{6,5},{7,4},{8,11},{9,10},{10,... | collective-permute-start | bytes 147464 | tf_op jit(solution)/shard_map/ppermute | solution.py:277
  137.3 6.3 %collective-permute-start.10 = (bf16[2,2,48,128]{3,2,1,0:T(8,128)(2,1)}, bf16[2,2,48,128]{3,2,1,0:T(8,128)(2,1)S(1)}, u32[]{:S(2)}, u32[]{:S(2)}) collective-permute-start(bf16[2,2,48,128]{3,2,1,0:T(8,128)(2,1)} %get-tuple-element.44), channel_id=1, source_target_pairs={{0,4},{1,5},{2,6},{3,7},{4,0},{5,1},{6,2},{7,3},{8,12},{9,13},{10,... | collective-permute-start | bytes 147464 | tf_op jit(solution)/shard_map/ppermute | solution.py:277
  138.4 7.7 %collective-permute-start.11 = (bf16[2,2,48,128]{3,2,1,0:T(8,128)(2,1)}, bf16[2,2,48,128]{3,2,1,0:T(8,128)(2,1)S(1)}, u32[]{:S(2)}, u32[]{:S(2)}) collective-permute-start(bf16[2,2,48,128]{3,2,1,0:T(8,128)(2,1)} %get-tuple-element.45), channel_id=1, source_target_pairs={{0,5},{1,4},{2,7},{3,6},{4,1},{5,0},{6,3},{7,2},{8,13},{9,12},{10,... | collective-permute-start | bytes 147464 | tf_op jit(solution)/shard_map/ppermute | solution.py:277
  140.5 7.4 %collective-permute-start.12 = (bf16[2,2,48,128]{3,2,1,0:T(8,128)(2,1)}, bf16[2,2,48,128]{3,2,1,0:T(8,128)(2,1)S(1)}, u32[]{:S(2)}, u32[]{:S(2)}) collective-permute-start(bf16[2,2,48,128]{3,2,1,0:T(8,128)(2,1)} %get-tuple-element.46), channel_id=1, source_target_pairs={{0,6},{1,7},{2,4},{3,5},{4,2},{5,3},{6,0},{7,1},{8,14},{9,15},{10,... | collective-permute-start | bytes 147464 | tf_op jit(solution)/shard_map/ppermute | solution.py:277
  141.4 8.4 %collective-permute-start.13 = (bf16[2,2,48,128]{3,2,1,0:T(8,128)(2,1)}, bf16[2,2,48,128]{3,2,1,0:T(8,128)(2,1)S(1)}, u32[]{:S(2)}, u32[]{:S(2)}) collective-permute-start(bf16[2,2,48,128]{3,2,1,0:T(8,128)(2,1)} %get-tuple-element.47), channel_id=1, source_target_pairs={{0,7},{1,6},{2,5},{3,4},{4,3},{5,2},{6,1},{7,0},{8,15},{9,14},{10,... | collective-permute-start | bytes 147464 | tf_op jit(solution)/shard_map/ppermute | solution.py:277
  149.8 0.8 copy-start.21
